TPU v7x, 512 devices: a whole 4x8x8 slice. The times are simulated.
512 devices in a mesh: row: 16 (over y, core), col: 32 (over z, x).
Axes of the slice: x: 4, y: 8, z: 8, core: 2. Of those that a mesh axis runs over, the one named last changes fastest.
Arguments:
- scatter_vectors: float32 [2, 2, 3, 512, 16384], P(None, None, None, 'row', 'col'), may hold values from -80 to 80
- ground_ratio: float32 [3], replicated, may hold values from 0.1 to 1
- vertical_wavenumber: float32 [512, 16384], P('row', 'col'), may hold values from 0.45 to 1.1
- initial_phase: float32 [512, 16384], P('row', 'col'), may hold values from 0.1 to 3.6
- initial_extinction: float32 [512, 16384], P('row', 'col'), may hold values from 0.1 to 2.9
Outputs:
- heights: float32 [512, 16384], P('row', 'col')
- extinction_depth: float32 [512, 16384], P('row', 'col')
All inputs are finite; a program needn't handle non-finite values.
Results may differ from a plain program's by a relative error of at most 0.00022.
Values sent between devices are 32-bit elements; how exact they have to be, the bound alone decides.
No kernel may reach another device: no remote copies, remote signals or barrier semaphores. Data moves between devices by JAX's collectives and lax.ppermute only.
A program may use at most 64 MiB of HBM per device.

v0:
```python
import jax
import jax.numpy as jnp
from jax import lax
from jax.sharding import PartitionSpec as P

RADIUS = 9
LAYERS = 16
GAUSS_STEPS = 2
ITERS = 3


EPSILON = 1e-06
DAMPING = 0.002
SMOOTHING = 1.0


def with_halo(block, sides, width, periodic):
    for axis, dim in sides:
        count = lax.axis_size(axis)
        forward = [(i, i + 1) for i in range(count - 1)]
        if periodic:
            forward.append((count - 1, 0))
        backward = [(target, source) for source, target in forward]
        low = lax.ppermute(
            lax.slice_in_dim(block, block.shape[dim] - width, None, axis=dim), axis, forward
        )
        high = lax.ppermute(lax.slice_in_dim(block, 0, width, axis=dim), axis, backward)
        block = jnp.concatenate([low, block, high], axis=dim)
    return block


def product_fields(vectors):
    real_one = vectors[0, 0]
    imag_one = vectors[0, 1]
    real_two = vectors[1, 0]
    imag_two = vectors[1, 1]
    return jnp.stack(
        [
            real_one * real_one + imag_one * imag_one,
            real_two * real_two + imag_two * imag_two,
            real_one * real_two + imag_one * imag_two,
            real_one * imag_two - imag_one * real_two,
        ]
    )


def column_window(padded, radius):
    span_cols = padded.shape[-1] - 2 * radius
    running = padded[..., 0:span_cols]
    for offset in range(1, 2 * radius + 1):
        running = running + padded[..., offset : offset + span_cols]
    return running


def row_window(padded, radius):
    span_rows = padded.shape[-2] - 2 * radius
    running = padded[..., 0:span_rows, :]
    for offset in range(1, 2 * radius + 1):
        running = running + padded[..., offset : offset + span_rows, :]
    return running


def coherence_pair(window_sums):
    norm_scale = lax.rsqrt(window_sums[0] * window_sums[1] + EPSILON)
    return (window_sums[2] * norm_scale, window_sums[3] * norm_scale)


def channel_summary(coherence_re, coherence_im, ground_ratio):
    ground_weight = 1.0 / (1.0 + ground_ratio)
    weighted_re = jnp.sum(coherence_re * ground_weight[:, None, None], axis=0)
    weighted_im = jnp.sum(coherence_im * ground_weight[:, None, None], axis=0)
    weight_total = jnp.sum(ground_weight * ground_weight)
    offset_total = jnp.sum(ground_ratio * ground_weight * ground_weight)
    confidence = jnp.mean(coherence_re * coherence_re + coherence_im * coherence_im, axis=0)
    return (weighted_re, weighted_im, weight_total, offset_total, confidence)


def volume_moments(phase_height, attenuation):
    weight_sum = jnp.zeros_like(phase_height)
    depth_sum = jnp.zeros_like(phase_height)
    cosine_sum = jnp.zeros_like(phase_height)
    sine_sum = jnp.zeros_like(phase_height)
    depth_cosine = jnp.zeros_like(phase_height)
    depth_sine = jnp.zeros_like(phase_height)
    for layer_index in range(LAYERS):
        layer_depth = (layer_index + 0.5) / LAYERS
        weight = jnp.exp(attenuation * layer_depth)
        cosine = weight * jnp.cos(phase_height * layer_depth)
        sine_term = weight * jnp.sin(phase_height * layer_depth)
        weight_sum = weight_sum + weight
        depth_sum = depth_sum + weight * layer_depth
        cosine_sum = cosine_sum + cosine
        sine_sum = sine_sum + sine_term
        depth_cosine = depth_cosine + cosine * layer_depth
        depth_sine = depth_sine + sine_term * layer_depth
    norm_scale = 1.0 / weight_sum
    return (
        depth_sum * norm_scale,
        cosine_sum * norm_scale,
        sine_sum * norm_scale,
        depth_cosine * norm_scale,
        depth_sine * norm_scale,
    )


def gauss_newton(phase_height, attenuation, weighted_re, weighted_im, weight_total, offset_total):
    for gauss_step in range(GAUSS_STEPS):
        mean_depth, real_part, imag_part, depth_cosine, depth_sine = volume_moments(
            phase_height, attenuation
        )
        real_by_atten = depth_cosine - mean_depth * real_part
        real_by_phase = -depth_sine
        imag_by_atten = depth_sine - mean_depth * imag_part
        misfit_re = weighted_re - weight_total * real_part - offset_total
        misfit_im = weighted_im - weight_total * imag_part
        normal_aa = (
            weight_total * (real_by_atten * real_by_atten + imag_by_atten * imag_by_atten) + DAMPING
        )
        normal_ap = weight_total * (real_by_atten * real_by_phase + imag_by_atten * depth_cosine)
        normal_pp = (
            weight_total * (real_by_phase * real_by_phase + depth_cosine * depth_cosine) + DAMPING
        )
        grad_atten = real_by_atten * misfit_re + imag_by_atten * misfit_im
        grad_phase = real_by_phase * misfit_re + depth_cosine * misfit_im
        determinant = normal_aa * normal_pp - normal_ap * normal_ap
        new_atten = attenuation + (normal_pp * grad_atten - normal_ap * grad_phase) / determinant
        phase_height = (
            phase_height + (normal_aa * grad_phase - normal_ap * grad_atten) / determinant
        )
        attenuation = new_atten
    return (phase_height, attenuation)


def apply_operator(grid_field, confidence):
    padded = with_halo(grid_field, (("row", 0), ("col", 1)), 1, False)
    beside = padded[2:, 1:-1] + padded[:-2, 1:-1] + padded[1:-1, 2:] + padded[1:-1, :-2]
    return confidence * grid_field + SMOOTHING * (4.0 * grid_field - beside)


def residual_square(residual):
    return lax.psum(jnp.sum(residual * residual), ("row", "col"))


def smooth_heights(start_height, confidence):
    solution = start_height
    residual = confidence * start_height - apply_operator(start_height, confidence)
    direction = residual
    norm_now = residual_square(residual)
    for iteration in range(ITERS):
        image_field = apply_operator(direction, confidence)
        step_length = norm_now / lax.psum(jnp.sum(direction * image_field), ("row", "col"))
        solution = solution + step_length * direction
        residual = residual - step_length * image_field
        norm_next = residual_square(residual)
        direction = residual + norm_next / norm_now * direction
        norm_now = norm_next
    return solution


def local(scatter_vectors, ground_ratio, vertical_wavenumber, initial_phase, initial_extinction):
    rimmed = with_halo(scatter_vectors, (("row", 3), ("col", 4)), RADIUS, True and False)
    window_sums = row_window(column_window(product_fields(rimmed), RADIUS), RADIUS)
    coherence_re, coherence_im = coherence_pair(window_sums)
    weighted_re, weighted_im, weight_total, offset_total, confidence = channel_summary(
        coherence_re, coherence_im, ground_ratio
    )
    phase_height, extinction_depth = gauss_newton(
        initial_phase, initial_extinction, weighted_re, weighted_im, weight_total, offset_total
    )
    start_height = phase_height / vertical_wavenumber
    heights = smooth_heights(start_height, confidence)
    return (heights, extinction_depth)


def solution(mesh):
    placed = (
        P(None, None, None, "row", "col"),
        P(),
        P("row", "col"),
        P("row", "col"),
        P("row", "col"),
    )
    return jax.shard_map(
        local,
        mesh=mesh,
        in_specs=placed,
        out_specs=(P("row", "col"), P("row", "col")),
        check_vma=False,
    )
```

profile of v0, /device:TPU:1, one launch (start us, length us, event | category | flops | bytes accessed | tf_op | source)
XLA Modules:
  0.0 640.6 jit_solution(5073688693235799006)
XLA Ops:
  0.6 1.3 fusion.27
  1.9 4.6 collective-permute-start
  6.5 5.5 collective-permute-start.1
  12.0 3.6 collective-permute-done.1
  15.8 3.1 collective-permute-start.2
  18.9 1.3 collective-permute-start.3
  21.0 2.3 collective-permute-done.2
  23.2 4.1 collective-permute-done.3
  27.4 0.8 pad_maximum_fusion
  28.5 6.5 %slice_add_fusion = f32[4,3,50,512]{3,2,1,0:T(8,128)S(1)} fusion(f32[4,3,50,530]{3,2,1,0:T(8,128)S(1)} %pad_maximum_fusion.1), kind=kLoop, calls=%fused_computation.2 | loop fusion | flops 5529600 | bytes 24576000 | tf_op jit(solution)/shard_map/add | solution.py:51
  35.1 1.3 slice_add_fusion.18
  36.5 5.8 multiply_add_fusion.9
  42.2 1.5 multiply_add_fusion.8
  43.8 4.4 add_multiply_fusion.3
  48.2 3.6 add_multiply_fusion.4
  51.8 6.5 %divide_add_fusion = (f32[32,512]{1,0:T(8,128)}, f32[32,512]{1,0:T(8,128)S(1)}, f32[32,512]{1,0:T(8,128)S(1)}, f32[32,512]{1,0:T(8,128)S(1)}, f32[32,512]{1,0:T(...) fusion(f32[32,512]{1,0:T(8,128)S(1)} %get-tuple-element.25, ...), kind=kLoop, calls=%fused_computation.109 | loop fusion | flops 2719744 | bytes 1048584 | tf_op jit(solution)/shard_map/add | solution.py:126
  58.2 0.8 add_divide_fusion
  59.0 1.9 collective-permute-start.4
  60.9 5.8 collective-permute-start.5
  66.8 0.7 collective-permute-done.5
  67.6 1.3 collective-permute-start.6
  68.9 4.0 collective-permute-start.7
  72.9 0.9 collective-permute-done.7
  73.9 1.9 collective-permute-start.8
  75.8 5.5 collective-permute-start.9
  81.9 1.3 collective-permute-start.10
  83.2 4.6 collective-permute-start.11
  87.8 0.9 collective-permute-done.11
  88.7 0.8 multiply_reduce_fusion.5
  89.5 116.7 %all-reduce = (f32[]{:T(128)}, f32[]{:T(128)}) all-reduce(f32[]{:T(128)} %get-tuple-element.6, f32[]{:T(128)} %get-tuple-element.5), channel_id=1, replica_groups=mesh['row'=16,'col'=32] {'row','col'}, use_global_device_ids=true, to_apply=%region_6.0 | all-reduce | flops 2 | bytes 16 | tf_op jit(solution)/shard_map/psum | solution.py:141
  207.4 0.7 multiply_reduce_fusion.4
  208.2 96.0 %psum.44 = f32[]{:T(128)} all-reduce(f32[]{:T(128)} %get-tuple-element.21), channel_id=1, replica_groups=mesh['row'=16,'col'=32] {'row','col'}, use_global_device_ids=true, to_apply=%region_10.0 | all-reduce | flops 1 | bytes 8 | tf_op jit(solution)/shard_map/psum | solution.py:141
  305.5 2.6 collective-permute-start.12
  308.0 4.5 collective-permute-start.13
  312.5 0.7 collective-permute-done.13
  313.3 1.3 collective-permute-start.14
  314.6 4.0 collective-permute-start.15
  318.6 0.9 collective-permute-done.15
  319.5 0.8 multiply_reduce_fusion.3
  320.2 102.6 %psum.45 = f32[]{:T(128)} all-reduce(f32[]{:T(128)} %get-tuple-element.19), channel_id=1, replica_groups=mesh['row'=16,'col'=32] {'row','col'}, use_global_device_ids=true, to_apply=%region_12.0 | all-reduce | flops 1 | bytes 8 | tf_op jit(solution)/shard_map/psum | solution.py:151
  424.8 95.0 %psum.46 = f32[]{:T(128)} all-reduce(f32[]{:T(128)} %multiply_reduce_fusion.2), channel_id=1, replica_groups=mesh['row'=16,'col'=32] {'row','col'}, use_global_device_ids=true, to_apply=%region_14.0 | all-reduce | flops 1 | bytes 8 | tf_op jit(solution)/shard_map/psum | solution.py:141
  521.2 2.6 collective-permute-start.16
  523.8 4.2 collective-permute-start.17
  528.8 1.3 collective-permute-start.18
  530.1 4.0 collective-permute-start.19
  534.1 0.9 collective-permute-done.19
  534.9 0.7 fusion.8
  535.7 102.9 %psum.47 = f32[]{:T(128)} all-reduce(f32[]{:T(128)} %fusion.8), channel_id=1, replica_groups=mesh['row'=16,'col'=32] {'row','col'}, use_global_device_ids=true, to_apply=%region_16.0 | all-reduce | flops 1 | bytes 8 | tf_op jit(solution)/shard_map/psum | solution.py:151
  (39 shorter events, 4.4 us)
Async XLA Ops:
  0.6 15.0 %copy-start = (f32[2,2,3,32,512]{4,3,2,1,0:T(8,128)S(1)}, f32[2,2,3,32,512]{4,3,2,1,0:T(8,128)}, u32[]{:S(2)}) copy-start(f32[2,2,3,32,512]{4,3,2,1,0:T(8,128)} %param.5) | copy-start | bytes 2359300
  1.9 18.3 %copy-start.3 = (f32[3]{0:T(128)S(1)}, f32[3]{0:T(128)}, u32[]{:S(2)}) copy-start(f32[3]{0:T(128)} %param.6) | copy-start | bytes 40
  1.9 10.1 %collective-permute-start = (f32[2,2,3,9,512]{4,3,2,1,0:T(8,128)S(1)}, f32[2,2,3,9,512]{4,3,2,1,0:T(8,128)S(1)}, u32[]{:S(2)}, u32[]{:S(2)}) collective-permute-start(f32[2,2,3,9,512]{4,3,2,1,0:T(8,128)S(1)} %get-tuple-element.43), channel_id=1, source_target_pairs={{0,32},{32,64},{64,96},{96,128},{128,160},{160,192},{192,224},{224... | collective-permute-start | bytes 663560 | tf_op jit(solution)/shard_map/ppermute | solution.py:24
  6.5 9.1 %collective-permute-start.1 = (f32[2,2,3,9,512]{4,3,2,1,0:T(8,128)S(1)}, f32[2,2,3,9,512]{4,3,2,1,0:T(8,128)S(1)}, u32[]{:S(2)}, u32[]{:S(2)}) collective-permute-start(f32[2,2,3,9,512]{4,3,2,1,0:T(8,128)S(1)} %get-tuple-element.44), channel_id=1, source_target_pairs={{32,0},{64,32},{96,64},{128,96},{160,128},{192,160},{224,192},{256... | collective-permute-start | bytes 663560 | tf_op jit(solution)/shard_map/ppermute | solution.py:27
  15.8 7.4 %collective-permute-start.2 = (f32[2,2,3,50,9]{4,3,2,1,0:T(8,128)S(1)}, f32[2,2,3,50,9]{4,3,2,1,0:T(8,128)S(1)}, u32[]{:S(2)}, u32[]{:S(2)}) collective-permute-start(f32[2,2,3,50,9]{4,3,2,1,0:T(8,128)S(1)} %get-tuple-element.41), channel_id=1, source_target_pairs={{0,1},{1,2},{2,3},{3,4},{4,5},{5,6},{6,7},{7,8},{8,9},{9,10},{10,1... | collective-permute-start | bytes 64808 | tf_op jit(solution)/shard_map/ppermute | solution.py:24
  18.9 8.4 %collective-permute-start.3 = (f32[2,2,3,50,9]{4,3,2,1,0:T(8,128)S(1)}, f32[2,2,3,50,9]{4,3,2,1,0:T(8,128)S(1)}, u32[]{:S(2)}, u32[]{:S(2)}) collective-permute-start(f32[2,2,3,50,9]{4,3,2,1,0:T(8,128)S(1)} %get-tuple-element.42), channel_id=1, source_target_pairs={{1,0},{2,1},{3,2},{4,3},{5,4},{6,5},{7,6},{8,7},{9,8},{10,9},{11,1... | collective-permute-start | bytes 64808 | tf_op jit(solution)/shard_map/ppermute | solution.py:27
  35.0 1.4 copy-start.2
  35.0 1.4 copy-start.4
  48.1 10.1 %copy-start.1 = (f32[32,512]{1,0:T(8,128)S(1)}, f32[32,512]{1,0:T(8,128)}, u32[]{:S(2)}) copy-start(f32[32,512]{1,0:T(8,128)} %param.7) | copy-start | bytes 196612
  59.0 7.8 %collective-permute-start.4 = (f32[1,512]{1,0:T(1,128)S(1)}, f32[1,512]{1,0:T(1,128)S(1)}, u32[]{:S(2)}, u32[]{:S(2)}) collective-permute-start(f32[1,512]{1,0:T(1,128)S(1)} %get-tuple-element.62), channel_id=1, source_target_pairs={{32,0},{64,32},{96,64},{128,96},{160,128},{192,160},{224,192},{256... | collective-permute-start | bytes 6152 | tf_op jit(solution)/shard_map/ppermute | solution.py:27
  60.9 6.6 %collective-permute-start.5 = (f32[1,512]{1,0:T(1,128)S(1)}, f32[1,512]{1,0:T(1,128)S(1)}, u32[]{:S(2)}, u32[]{:S(2)}) collective-permute-start(f32[1,512]{1,0:T(1,128)S(1)} %get-tuple-element.61), channel_id=1, source_target_pairs={{0,32},{32,64},{64,96},{96,128},{128,160},{160,192},{192,224},{224... | collective-permute-start | bytes 6152 | tf_op jit(solution)/shard_map/ppermute | solution.py:24
  67.6 5.3 collective-permute-start.6
  68.9 4.9 collective-permute-start.7
  73.9 7.4 %collective-permute-start.8 = (f32[1,512]{1,0:T(1,128)S(1)}, f32[1,512]{1,0:T(1,128)S(1)}, u32[]{:S(2)}, u32[]{:S(2)}) collective-permute-start(f32[1,512]{1,0:T(1,128)S(1)} %get-tuple-element.60), channel_id=1, source_target_pairs={{32,0},{64,32},{96,64},{128,96},{160,128},{192,160},{224,192},{256... | collective-permute-start | bytes 6152 | tf_op jit(solution)/shard_map/ppermute | solution.py:27
  75.8 6.0 collective-permute-start.9
  81.9 5.9 collective-permute-start.10
  83.2 5.5 collective-permute-start.11
  305.5 7.0 %collective-permute-start.12 = (f32[1,512]{1,0:T(1,128)S(1)}, f32[1,512]{1,0:T(1,128)S(1)}, u32[]{:S(2)}, u32[]{:S(2)}) collective-permute-start(f32[1,512]{1,0:T(1,128)S(1)} %get-tuple-element.58), channel_id=1, source_target_pairs={{32,0},{64,32},{96,64},{128,96},{160,128},{192,160},{224,192},{256... | collective-permute-start | bytes 6152 | tf_op jit(solution)/shard_map/ppermute | solution.py:27
  308.0 5.2 collective-permute-start.13
  313.3 5.3 collective-permute-start.14
  314.6 4.9 collective-permute-start.15
  521.2 6.7 %collective-permute-start.16 = (f32[1,512]{1,0:T(1,128)S(1)}, f32[1,512]{1,0:T(1,128)S(1)}, u32[]{:S(2)}, u32[]{:S(2)}) collective-permute-start(f32[1,512]{1,0:T(1,128)S(1)} %get-tuple-element.56), channel_id=1, source_target_pairs={{32,0},{64,32},{96,64},{128,96},{160,128},{192,160},{224,192},{256... | collective-permute-start | bytes 6152 | tf_op jit(solution)/shard_map/ppermute | solution.py:27
  523.8 4.9 collective-permute-start.17
  528.8 5.3 collective-permute-start.18
  530.1 4.9 collective-permute-start.19
where the time goes:
time: 642 us; the launch traced here: 641 us
  blocking collectives  513 us (80%)
  starting transfers between devices  65.1 us (10%)
  other arithmetic  37.2 us (6%)
  waiting for transfers between devices  16.2 us (3%)
  between operations  7.58 us (1%)
    psum x3, blocking collectives, residual_square(): return lax.psum(jnp.sum(residual * residual), ('row', 'col'))  308 us
    psum x2, blocking collectives, smooth_heights(): lax.psum(jnp.sum(direction * image_field), ('row', 'col'))  206 us
    ppermute x10, starting transfers between devices, with_halo(): lax.ppermute(lax.slice_in_dim(block, block.shape[dim] - width, None, axis...  44.2 us
    ppermute x10, starting transfers between devices, with_halo(): lax.ppermute(lax.slice_in_dim(block, 0, width, axis=dim), axis, backward)  20.9 us
  transfers between devices with their start and end apart: 20, of which 11 were waited for; matrix products, arithmetic and copies ran while one was open for 0% of the time, Pallas kernels for 0%

commit v1 on v0

v1 whole, which is shorter than its diff:
```python
import jax
import jax.numpy as jnp
from jax import lax
from jax.experimental import pallas as pl
from jax.experimental.pallas import tpu as pltpu
from jax.sharding import PartitionSpec as P

RADIUS = 9
LAYERS = 16
GAUSS_STEPS = 2
EPSILON = 1e-06
DAMPING = 0.002
SCALE = 4.5

H = 32
W = 512
EH = 40
EW = 640
FIELDS = 12
SEND_ROWS = FIELDS * 16 + 3 * 8
STRIPS = (FIELDS + 3) * (EH // 8)
PACK = -(-STRIPS // 8) * 8
VM = pl.BlockSpec(memory_space=pltpu.VMEM)
SM = pl.BlockSpec(memory_space=pltpu.SMEM)
ANY = pl.BlockSpec(memory_space=pl.ANY)
INTERPRET = False


def f32(*shape):
    return jax.ShapeDtypeStruct(shape, jnp.float32)


def call(kernel, outs, ins, scratch=(), name=None):
    return pl.pallas_call(
        kernel,
        out_shape=outs,
        in_specs=ins,
        out_specs=jax.tree.map(lambda _: VM, outs),
        scratch_shapes=scratch,
        name=name,
        interpret=INTERPRET,
    )


def edges_kernel(sv, vw, ip, ie, up, down, sems):
    copies = []
    for f in range(FIELDS):
        copies.append((sv.at[f, pl.ds(0, 16)], up.at[pl.ds(16 * f, 16)]))
        copies.append((sv.at[f, pl.ds(16, 16)], down.at[pl.ds(16 * f, 16)]))
    for j, ref in enumerate((vw, ip, ie)):
        at = FIELDS * 16 + 8 * j
        copies.append((ref.at[pl.ds(0, 8)], up.at[pl.ds(at, 8)]))
        copies.append((ref.at[pl.ds(24, 8)], down.at[pl.ds(at, 8)]))
    started = []
    for n, (src, dst) in enumerate(copies):
        copy = pltpu.make_async_copy(src, dst, sems.at[n])
        copy.start()
        started.append(copy)
    for copy in started:
        copy.wait()


def strip_source(rows, ext, strip):
    field, tile = divmod(strip, EH // 8)
    if field < FIELDS:
        return rows, field * EH + 8 * tile
    return ext, (field - FIELDS) * EH + 8 * tile


def rows_kernel(sv, vw, ip, ie, above, below, rows, ext, left, right, px, s4):
    sub = lax.broadcasted_iota(jnp.int32, (8, 128), 0)
    lane = lax.broadcasted_iota(jnp.int32, (8, 128), 1)

    def one(n, carry):
        k = n // 4
        b = n % 4
        cols = pl.ds(pl.multiple_of(b * 128, 128), 128)

        def parts(q):
            f = q * 3 + k
            return (
                above[pl.ds(pl.multiple_of(16 * f, 16), 16), cols],
                sv[f, :, cols],
                below[pl.ds(pl.multiple_of(16 * f, 16), 16), cols],
            )

        quads = [parts(q) for q in range(4)]
        for p, (at, size) in enumerate(((8, 16), (24, H), (24 + H, 16))):
            re1, im1, re2, im2 = (quad[p] for quad in quads)
            px[0, at : at + size] = re1 * re1 + im1 * im1
            px[1, at : at + size] = re2 * re2 + im2 * im2
            px[2, at : at + size] = re1 * re2 + im1 * im2
            px[3, at : at + size] = re1 * im2 - im1 * re2
        for j in range(4):
            two = px[j, 7:79] + px[j, 8:80]
            four = two[0:64] + (px[j, 9:73] + px[j, 10:74])
            s4[j, 0:64] = four
            eight = four[0:56] + s4[j, 4:60]
            sixteen = eight[0:48] + eight[8:56]
            total = sixteen + two[16:64] + px[j, 25:73]
            at = pl.multiple_of((j * 3 + k) * EH, 8)
            rows[pl.ds(at, H), cols] = total[8:40]
            rows[pl.ds(at + H, 8), cols] = jnp.where(sub < 4, total[40:48], total[0:8])
        return carry

    lax.fori_loop(0, 12, one, 0)
    for j, ref in enumerate((vw, ip, ie)):
        at = FIELDS * 16 + 8 * j
        ext[j * EH : j * EH + H] = ref[...]
        for b in range(4):
            cols = slice(128 * b, 128 * b + 128)
            ext[j * EH + H : j * EH + EH, cols] = jnp.where(
                sub < 4, below[at : at + 8, cols], above[at : at + 8, cols]
            )
    for v in range(PACK // 8):
        low = jnp.zeros((8, 128), jnp.float32)
        high = jnp.zeros((8, 128), jnp.float32)
        for g in range(8):
            strip = 8 * v + g
            if strip >= STRIPS:
                break
            ref, at = strip_source(rows, ext, strip)
            here = (lane >= 16 * g) & (lane < 16 * g + 16)
            first = ref[at : at + 8, 0:128]
            last = ref[at : at + 8, W - 128 : W]
            if g:
                first = pltpu.roll(first, 16 * g, 1)
            if g != 7:
                last = pltpu.roll(last, (16 * g + 16) % 128, 1)
            low = jnp.where(here, first, low)
            high = jnp.where(here, last, high)
        left[8 * v : 8 * v + 8] = low
        right[8 * v : 8 * v + 8] = high


def sincos(x):
    turns = jnp.floor(x * 0.3183098861837907 + 0.5)
    y = x - turns * 3.140625
    y = y - turns * 9.67502593994140625e-4
    y = y - turns * 1.509957990978376432e-7
    odd = turns - 2.0 * jnp.floor(turns * 0.5)
    sign = 1.0 - 2.0 * odd
    z = y * y
    s = -2.3889859e-08
    s = s * z + 2.7525562e-06
    s = s * z - 1.9840874e-04
    s = s * z + 8.3333310e-03
    s = s * z - 1.6666667e-01
    s = y + y * z * s
    c = 2.0875723e-09
    c = c * z - 2.7557319e-07
    c = c * z + 2.4801587e-05
    c = c * z - 1.3888889e-03
    c = c * z + 4.1666667e-02
    c = 1.0 + z * (c * z - 0.5)
    return sign * s, sign * c


def cmul(ar, ai, br, bi):
    return ar * br - ai * bi, ar * bi + ai * br


def moments(phase, atten):
    half_s, half_c = sincos(phase * (0.5 / LAYERS))
    r = jnp.exp(atten * (1.0 / LAYERS))
    zr = r * (half_c * half_c - half_s * half_s)
    zi = r * (2.0 * half_c * half_s)
    n_sum, n_dep = 1.0 + r, r
    sr, si = 1.0 + zr, zi
    dr, di = zr, zi
    count = 2.0
    while count < LAYERS:
        r = r * r
        zr, zi = zr * zr - zi * zi, 2.0 * zr * zi
        n_dep = n_dep + r * (n_dep + count * n_sum)
        n_sum = n_sum + r * n_sum
        tr, ti = cmul(zr, zi, dr + count * sr, di + count * si)
        dr, di = dr + tr, di + ti
        tr, ti = cmul(zr, zi, sr, si)
        sr, si = sr + tr, si + ti
        count = 2.0 * count
    norm = 1.0 / n_sum
    half_c = half_c * norm
    half_s = half_s * norm
    real, imag = cmul(sr, si, half_c, half_s)
    dr, di = cmul(dr, di, half_c, half_s)
    step = 1.0 / LAYERS
    return (
        (n_dep * norm + 0.5) * step,
        real,
        imag,
        (dr + 0.5 * real) * step,
        (di + 0.5 * imag) * step,
    )


def gauss_step(phase, atten, mom, wre, wim, weight, offset):
    mean_depth, real_part, imag_part, depth_cos, depth_sin = mom
    ra = depth_cos - mean_depth * real_part
    rt = -depth_sin
    ia = depth_sin - mean_depth * imag_part
    it = depth_cos
    er = wre - weight * real_part - offset
    ei = wim - weight * imag_part
    maa = weight * (ra * ra + ia * ia) + DAMPING
    map_ = weight * (ra * rt + ia * it)
    mpp = weight * (rt * rt + it * it) + DAMPING
    ga = ra * er + ia * ei
    gp = rt * er + it * ei
    inverse = 1.0 / (maa * mpp - map_ * map_)
    return (
        phase + (maa * gp - map_ * ga) * inverse,
        atten + (mpp * ga - map_ * gp) * inverse,
    )


def around(field):
    return (
        pltpu.roll(field, 1, 0)
        + pltpu.roll(field, EH - 1, 0)
        + pltpu.roll(field, 1, 1)
        + pltpu.roll(field, EW - 1, 1)
    )


def make_fit_kernel(row_count, col_count, group):
    def kernel(
        place, ground, rows, ext, from_left, from_right,
        depth, base, v0, v1, v2, sums,
        hi, mid, lo, win, wide, conf,
    ):
        lane = lax.broadcasted_iota(jnp.int32, (8, 128), 1)

        def halo_tile(strip):
            v, g = divmod(strip, 8)
            lo_part = from_right[8 * v : 8 * v + 8]
            hi_part = from_left[8 * v : 8 * v + 8]
            if g:
                lo_part = pltpu.roll(lo_part, 128 - 16 * g, 1)
            if g != 7:
                hi_part = pltpu.roll(hi_part, 112 - 16 * g, 1)
            return jnp.where(lane < 16, lo_part, jnp.where(lane >= 112, hi_part, 0.0))

        def split(value, at, cols):
            first = value.astype(jnp.bfloat16)
            rest = value - first.astype(jnp.float32)
            second = rest.astype(jnp.bfloat16)
            third = (rest - second.astype(jnp.float32)).astype(jnp.bfloat16)
            for c in cols:
                end = c + value.shape[1]
                hi[at : at + value.shape[0], c:end] = first
                mid[at : at + value.shape[0], c:end] = second
                lo[at : at + value.shape[0], c:end] = third

        for f in range(FIELDS):
            at = f * EH
            halo = jnp.concatenate([halo_tile(f * 5 + i) for i in range(5)], axis=0)
            wide[0, 0:EH, 0:128] = halo
            split(wide[0, 0:EH, 0:128], at, (0, 640))
            split(rows[at : at + EH, 0:128], at, (128, 768))
            for b in range(1, 4):
                split(rows[at : at + EH, 128 * b : 128 * b + 128], at, (128 + 128 * b,))
        for j in range(3):
            wide[j, :, 0:W] = ext[j * EH : j * EH + EH]
            for i in range(5):
                wide[j, 8 * i : 8 * i + 8, W:EW] = halo_tile((FIELDS + j) * 5 + i)

        up = lax.broadcasted_iota(jnp.int32, (384, 128), 0) - 128
        across = lax.broadcasted_iota(jnp.int32, (384, 128), 1)
        band = (jnp.abs(up - across) <= RADIUS).astype(jnp.float32).astype(jnp.bfloat16)

        def dot(a):
            return jnp.dot(a, band, preferred_element_type=jnp.float32)

        for b in range(5):
            cols = slice(128 * b, 128 * b + 384)
            win[:, 128 * b : 128 * b + 128] = dot(hi[:, cols]) + (dot(mid[:, cols]) + dot(lo[:, cols]))

        ratios = [jnp.full((8, 128), ground[k], jnp.float32) for k in range(3)]
        weights = [1.0 / (1.0 + g) for g in ratios]
        weight = weights[0] * weights[0] + weights[1] * weights[1] + weights[2] * weights[2]
        offset = (
            ratios[0] * weights[0] * weights[0]
            + ratios[1] * weights[1] * weights[1]
            + ratios[2] * weights[2] * weights[2]
        )

        def fit(i, carry):
            def tile(f, b):
                return win[pl.ds(pl.multiple_of(f * EH + 8 * i, 8), 8), 128 * b : 128 * b + 128]

            here = pl.ds(pl.multiple_of(8 * i, 8), 8)
            for b in range(5):
                cols = slice(128 * b, 128 * b + 128)
                wre = wim = power = None
                for k in range(3):
                    scale = lax.rsqrt(tile(k, b) * tile(3 + k, b) + EPSILON)
                    cre = tile(6 + k, b) * scale
                    cim = tile(9 + k, b) * scale
                    square = cre * cre + cim * cim
                    if k:
                        wre = wre + cre * weights[k]
                        wim = wim + cim * weights[k]
                        power = power + square
                    else:
                        wre = cre * weights[k]
                        wim = cim * weights[k]
                        power = square
                conf[here, cols] = power * (1.0 / 3.0)
                phase = wide[1, here, cols]
                atten = wide[2, here, cols]
                for _ in range(GAUSS_STEPS):
                    phase, atten = gauss_step(
                        phase, atten, moments(phase, atten), wre, wim, weight, offset
                    )
                wide[2, here, cols] = atten
                wide[0, here, cols] = phase / wide[0, here, cols]
            return carry

        lax.fori_loop(0, 5, fit, 0)

        r = lax.broadcasted_iota(jnp.int32, (EH, EW), 0)
        c = lax.broadcasted_iota(jnp.int32, (EH, EW), 1)
        row_low = jnp.where(place[0] == 0, EH - 4, EH)
        row_high = jnp.where(place[0] == row_count - 1, H, EH - 4)
        col_low = jnp.where(place[1] == 0, EW, EW - 4)
        col_high = jnp.where(place[1] == col_count - 1, W, W + 4)
        row_bad = ((r >= row_high) & (r < EH - 4)) | (r >= row_low)
        col_bad = (c >= col_high) & (c < col_low)
        inside = jnp.logical_not(row_bad | col_bad)

        start = jnp.where(inside, wide[0], 0.0)
        confidence = conf[...] - 0.5
        depth[...] = wide[2, 0:H, 0:W]
        base[...] = start[0:H, 0:W]
        first = jnp.where(inside, around(start) - 4.0 * start, 0.0)
        v0[...] = first[0:H, 0:W]

        def advance(field):
            return jnp.where(inside, (confidence * field - around(field)) * (1.0 / SCALE), 0.0)

        second = advance(first)
        v1[...] = second[0:H, 0:W]
        third = advance(second)
        v2[...] = third[0:H, 0:W]
        fourth = advance(third)
        a0, a1, a2, a3 = (x[0:H, 0:W] for x in (first, second, third, fourth))
        spots = lax.broadcasted_iota(jnp.int32, (1, 128), 1)
        line = jnp.zeros((1, 128), jnp.float32)
        for n, (p, q) in enumerate(((a0, a0), (a0, a1), (a1, a1), (a1, a2), (a2, a2), (a2, a3))):
            product = p * q
            total = jnp.sum(jnp.sum(product, axis=0, keepdims=True), axis=1, keepdims=True)
            line = jnp.where(spots == n, total, line)
        sums[...] = jnp.broadcast_to(line, (group, 128))

    return kernel


def make_relay_kernel(out_group):
    def kernel(parts, out):
        out[...] = jnp.broadcast_to(jnp.sum(parts[...], axis=0, keepdims=True), (out_group, 128))

    return kernel


def form(p, q, b):
    total = None
    for i, x in enumerate(p):
        for j, y in enumerate(q):
            term = x * y * b[i + j]
            total = term if total is None else total + term
    return total


def final_kernel(parts, base, v0, v1, v2, heights):
    line = jnp.sum(parts[...], axis=0, keepdims=True)
    spots = lax.broadcasted_iota(jnp.int32, (1, 128), 1)
    b = [
        jnp.sum(jnp.where(spots == n, line, 0.0), axis=1, keepdims=True) for n in range(6)
    ]

    def times_a(p):
        out = [SCALE * p[0]]
        for low, high in zip(p[:-1], p[1:]):
            out.append(SCALE * (low + high))
        return out + [SCALE * p[-1]]

    one = jnp.ones((1, 1), jnp.float32)
    zero = jnp.zeros((1, 1), jnp.float32)
    residual = [one]
    direction = [one]
    answer = [zero, zero, zero]
    now = b[0]
    for iteration in range(3):
        image = times_a(direction)
        alpha = now / form(direction, image, b)
        for n, x in enumerate(direction):
            answer[n] = answer[n] + alpha * x
        if iteration == 2:
            break
        residual = [
            (residual[n] if n < len(residual) else 0.0) - alpha * x for n, x in enumerate(image)
        ]
        after = form(residual, residual, b)
        beta = after / now
        direction = [
            x + (beta * direction[n] if n < len(direction) else 0.0)
            for n, x in enumerate(residual)
        ]
        now = after
    heights[...] = base[...] + (answer[0] * v0[...] + (answer[1] * v1[...] + answer[2] * v2[...]))


def solution(mesh):
    row_count = mesh.shape["row"]
    col_count = mesh.shape["col"]
    near = 2 * col_count
    far = row_count // 2

    def index(r, c):
        return r * col_count + c

    near_groups = [
        [index(2 * y + core, c) for core in range(2) for c in range(col_count)] for y in range(far)
    ]
    far_groups = [
        [index(2 * y + core, c) for y in range(far)] for core in range(2) for c in range(col_count)
    ]
    both = ("row", "col")

    def chain(count, step):
        return [(i, i + step) for i in range(count) if 0 <= i + step < count]

    def local(scatter_vectors, ground_ratio, wavenumber, phase, extinction):
        sv = scatter_vectors.reshape(FIELDS, H, W)
        copies = 2 * (FIELDS + 3)
        up, down = call(
            edges_kernel,
            (f32(SEND_ROWS, W), f32(SEND_ROWS, W)),
            [ANY] * 4,
            [pltpu.SemaphoreType.DMA((copies,))],
            name="edges",
        )(sv, wavenumber, phase, extinction)
        below = lax.ppermute(up, "row", chain(row_count, -1))
        above = lax.ppermute(down, "row", chain(row_count, 1))
        rows, ext, left, right = call(
            rows_kernel,
            (f32(FIELDS * EH, W), f32(3 * EH, W), f32(PACK, 128), f32(PACK, 128)),
            [VM] * 6,
            [pltpu.VMEM((4, 88, 128), jnp.float32), pltpu.VMEM((4, 64, 128), jnp.float32)],
            name="rowsums",
        )(sv, wavenumber, phase, extinction, above, below)
        from_right = lax.ppermute(left, "col", chain(col_count, -1))
        from_left = lax.ppermute(right, "col", chain(col_count, 1))
        place = jnp.stack([lax.axis_index("row"), lax.axis_index("col")]).astype(jnp.int32)
        depth, base, v0, v1, v2, sums = call(
            make_fit_kernel(row_count, col_count, near),
            tuple(f32(H, W) for _ in range(5)) + (f32(near, 128),),
            [SM, SM] + [VM] * 4,
            [pltpu.VMEM((FIELDS * EH, 896), jnp.bfloat16)] * 3
            + [
                pltpu.VMEM((FIELDS * EH, EW), jnp.float32),
                pltpu.VMEM((3, EH, EW), jnp.float32),
                pltpu.VMEM((EH, EW), jnp.float32),
            ],
            name="fit",
        )(place, ground_ratio, rows, ext, from_left, from_right)
        parts = lax.all_to_all(
            sums.reshape(near, 1, 128), both, 0, 0, axis_index_groups=near_groups
        ).reshape(near, 128)
        parts = call(make_relay_kernel(far), f32(far, 128), [VM], name="relay")(parts)
        parts = lax.all_to_all(
            parts.reshape(far, 1, 128), both, 0, 0, axis_index_groups=far_groups
        ).reshape(far, 128)
        heights = call(final_kernel, f32(H, W), [VM] * 5, name="final")(parts, base, v0, v1, v2)
        return heights, depth

    placed = (P(None, None, None, "row", "col"), P(), P("row", "col"), P("row", "col"), P("row", "col"))
    return jax.shard_map(
        local,
        mesh=mesh,
        in_specs=placed,
        out_specs=(P("row", "col"), P("row", "col")),
        check_vma=False,
    )
```

time: 642 us -> 79.5 us (0.12)
  blocking collectives: 513 us -> 39.6 us
  starting transfers between devices: 65.1 us -> 14.5 us
  other arithmetic: 37.2 us -> 0.65 us
  Pallas kernels: 0 us -> 14.9 us
  waiting for transfers between devices: 16.2 us -> 7.34 us
  between operations: 7.58 us -> 0.68 us
    psum x5 -> x0, blocking collectives: 513 us -> none  [the longest x3 308 us: residual_square(): return lax.psum(jnp.sum(residual * residual), ('row', 'col'))]
    ppermute x20 -> x4, starting transfers between devices: 65.1 us -> 14.5 us  [the longest x1 5.48 us: local(): below = lax.ppermute(up, 'row', chain(row_count, -1))]
    all_to_all x0 -> x2, blocking collectives: none -> 39.6 us  [the longest x1 24.9 us: local(): lax.all_to_all(sums.reshape(near, 1, 128), both, 0, 0, axis_index_groups=...]
    add x9 -> x0, other arithmetic: 22.4 us -> none  [the longest x1 6.54 us: column_window(): running = running + padded[..., offset:offset + span_cols]]
    pallas_call x0 -> x5, Pallas kernels: none -> 14.9 us  [the longest x1 6.12 us: local(): call(make_fit_kernel(row_count, col_count, near), tuple((f32(H, W) for _...]
    ppermute x20 -> x4, waiting for transfers between devices: 16.2 us -> 7.34 us  [the longest x1 4.29 us: local(): below = lax.ppermute(up, 'row', chain(row_count, -1))]
    mul x2 -> x0, other arithmetic: 7.97 us -> none  [the longest x1 4.37 us: volume_moments(): cosine_sum * norm_scale]
  transfers between devices with their start and end apart: 20 -> 4, of which waited for: 11 -> 2; matrix products, arithmetic and copies ran while one was open for 0% -> 1% of each run, Pallas kernels for 0% -> 0%
where the time goes in v1:
time: 79.5 us; the launch traced here: 78.9 us
  blocking collectives  39.6 us (50%)
  Pallas kernels  14.9 us (19%)
  starting transfers between devices  14.5 us (18%)
  waiting for transfers between devices  7.34 us (9%)
  local copies, waits for them, and re-layouts  1.39 us (2%)
    all_to_all x1, blocking collectives, local(): lax.all_to_all(sums.reshape(near, 1, 128), both, 0, 0, axis_index_groups=...  24.9 us
    all_to_all x1, blocking collectives, local(): lax.all_to_all(parts.reshape(far, 1, 128), both, 0, 0, axis_index_groups=...  14.7 us
    pallas_call x1, Pallas kernels, local(): call(make_fit_kernel(row_count, col_count, near), tuple((f32(H, W) for _...  6.12 us
    ppermute x1, starting transfers between devices, local(): below = lax.ppermute(up, 'row', chain(row_count, -1))  5.48 us
    ppermute x1, starting transfers between devices, local(): above = lax.ppermute(down, 'row', chain(row_count, 1))  4.58 us
    ppermute x1, waiting for transfers between devices, local(): below = lax.ppermute(up, 'row', chain(row_count, -1))  4.29 us
    pallas_call x1, Pallas kernels, local(): call(rows_kernel, (f32(FIELDS * EH, W), f32(3 * EH, W), f32(PACK, 128), f...  3.34 us
    ppermute x1, starting transfers between devices, local(): from_left = lax.ppermute(right, 'col', chain(col_count, 1))  3.11 us
  transfers between devices with their start and end apart: 4, of which 2 were waited for; matrix products, arithmetic and copies ran while one was open for 1% of the time, Pallas kernels for 0%

profile of v1, /device:TPU:1, one launch (start us, length us, event | category | flops | bytes accessed | tf_op | source)
XLA Modules:
  0.0 78.9 jit_solution(63122328382638278)
XLA Ops:
  0.6 2.3 %edges.1 = (f32[216,512]{1,0:T(8,128)}, f32[216,512]{1,0:T(8,128)}) custom-call(f32[12,32,512]{2,1,0:T(8,128)} %bitcast.11, f32[32,512]{1,0:T(8,128)} %vw.3, f32[32,512]{1,0:T(8,128)} %ip.3, f32[32,512]{1,0:T(8,128)} %ie.3), custom_call_target="tpu_custom_call" | custom-call | tf_op jit(solution)/shard_map/edges/pallas_call | solution.py:437
  2.9 4.6 %collective-permute-start = (f32[216,512]{1,0:T(8,128)}, f32[216,512]{1,0:T(8,128)S(1)}, u32[]{:S(2)}, u32[]{:S(2)}) collective-permute-start(f32[216,512]{1,0:T(8,128)} %get-tuple-element.14), channel_id=1, source_target_pairs={{0,32},{32,64},{64,96},{96,128},{128,160},{160,192},{192,224},{224... | collective-permute-start | bytes 1327112 | tf_op jit(solution)/shard_map/ppermute | solution.py:445
  7.5 5.5 %collective-permute-start.1 = (f32[216,512]{1,0:T(8,128)}, f32[216,512]{1,0:T(8,128)S(1)}, u32[]{:S(2)}, u32[]{:S(2)}) collective-permute-start(f32[216,512]{1,0:T(8,128)} %get-tuple-element.15), channel_id=1, source_target_pairs={{32,0},{64,32},{96,64},{128,96},{160,128},{192,160},{224,192},{256... | collective-permute-start | bytes 1327112 | tf_op jit(solution)/shard_map/ppermute | solution.py:444
  13.0 0.0 collective-permute-done.above
  13.1 0.0 copy-start
  13.1 4.3 %collective-permute-done.1.below = f32[216,512]{1,0:T(8,128)S(1)} collective-permute-done((f32[216,512]{1,0:T(8,128)}, f32[216,512]{1,0:T(8,128)S(1)}, u32[]{:S(2)}, u32[]{:S(2)}) %collective-permute-start.1) | collective-permute-done | bytes 442400 | tf_op jit(solution)/shard_map/ppermute | solution.py:444
  17.4 0.0 copy-done
  17.4 0.0 copy-start.1
  17.4 0.8 copy-done.1
  18.1 3.3 %rowsums.1 = (f32[480,512]{1,0:T(8,128)}, f32[120,512]{1,0:T(8,128)}, f32[80,128]{1,0:T(8,128)}, f32[80,128]{1,0:T(8,128)}) custom-call(f32[12,32,512]{2,1,0:T(8,128)} %bitcast.12, f32[32,512]{1,0:T(8,128)} %vw.3, f32[32,512]{1,0:T(8,128)} %ip.3, f32[32,512]{1,0:T(8,128)} %ie.3, f32[216,512]{1,0:T(8,128)} %copy-done, f32[216,512]{1,0:T(8,128)} %copy-done.1), custom_call_target="tpu_custom_call" | custom-call | tf_op jit(solution)/shard_map/rowsums/pallas_call | solution.py:446
  21.5 3.1 %collective-permute-start.2 = (f32[80,128]{1,0:T(8,128)}, f32[80,128]{1,0:T(8,128)S(1)}, u32[]{:S(2)}, u32[]{:S(2)}) collective-permute-start(f32[80,128]{1,0:T(8,128)} %get-tuple-element.18), channel_id=1, source_target_pairs={{0,1},{1,2},{2,3},{3,4},{4,5},{5,6},{6,7},{7,8},{8,9},{9,10},{10,1... | collective-permute-start | bytes 122888 | tf_op jit(solution)/shard_map/ppermute | solution.py:454
  24.6 1.3 %collective-permute-start.3 = (f32[80,128]{1,0:T(8,128)}, f32[80,128]{1,0:T(8,128)S(1)}, u32[]{:S(2)}, u32[]{:S(2)}) collective-permute-start(f32[80,128]{1,0:T(8,128)} %get-tuple-element.19), channel_id=1, source_target_pairs={{1,0},{2,1},{3,2},{4,3},{5,4},{6,5},{7,6},{8,7},{9,8},{10,9},{11,1... | collective-permute-start | bytes 122888 | tf_op jit(solution)/shard_map/ppermute | solution.py:453
  25.9 0.7 pad_add_fusion.place
  26.5 0.0 collective-permute-done.2.from_left
  26.5 0.0 copy-start.2
  26.5 3.0 %collective-permute-done.3.from_right = f32[80,128]{1,0:T(8,128)S(1)} collective-permute-done((f32[80,128]{1,0:T(8,128)}, f32[80,128]{1,0:T(8,128)S(1)}, u32[]{:S(2)}, u32[]{:S(2)}) %collective-permute-start.3) | collective-permute-done | bytes 40992 | tf_op jit(solution)/shard_map/ppermute | solution.py:453
  29.5 0.0 copy-start.3
  29.5 0.0 copy-done.2
  29.5 0.6 copy-done.3
  30.2 6.1 %fit.1 = (f32[32,512]{1,0:T(8,128)}, f32[32,512]{1,0:T(8,128)}, f32[32,512]{1,0:T(8,128)}, f32[32,512]{1,0:T(8,128)}, f32[32,512]{1,0:T(8,128)}, /*index=5*/f32[64,128]{1,0:T(8,128)}) custom-call(s32[2]{0:T(128)} %pad_add_fusion.place, f32[3]{0:T(128)} %ground.1, f32[480,512]{1,0:T(8,128)} %get-tuple-element.16.rows, f32[120,512]{1,0:T(8,128)} %get-tuple-element.17.ext, ...), custom_call_target="tpu_custom_call" | custom-call | tf_op jit(solution)/shard_map/fit/pallas_call | solution.py:456
  36.3 24.9 %all_to_all.10 = f32[64,1,128]{2,1,0:T(1,128)} all-to-all(f32[64,1,128]{2,1,0:T(1,128)} %bitcast.14), channel_id=1, replica_groups={{0,1,2,3,4,5,6,7,8,9,10,11,12,13,14,15,16,17,18,19,20,21,22,23,24,25,26..., dimensions={0} | all-to-all | bytes 65536 | tf_op jit(solution)/shard_map/all_to_all | solution.py:468
  61.1 1.4 %relay.1 = f32[8,128]{1,0:T(8,128)} custom-call(f32[64,128]{1,0:T(8,128)} %bitcast.13), custom_call_target="tpu_custom_call" | custom-call | tf_op jit(solution)/shard_map/relay/pallas_call | solution.py:471
  62.5 14.7 %all_to_all.11 = f32[8,1,128]{2,1,0:T(1,128)} all-to-all(f32[8,1,128]{2,1,0:T(1,128)} %bitcast.15), channel_id=1, replica_groups={{0,64,128,192,256,320,384,448},{1,65,129,193,257,321,385,449},{2,66,130..., dimensions={0} | all-to-all | bytes 8192 | tf_op jit(solution)/shard_map/all_to_all | solution.py:472
  77.2 1.7 %final.1 = f32[32,512]{1,0:T(8,128)} custom-call(f32[8,128]{1,0:T(8,128)} %bitcast.16, f32[32,512]{1,0:T(8,128)} %get-tuple-element.21.base, f32[32,512]{1,0:T(8,128)} %get-tuple-element.22.v0, f32[32,512]{1,0:T(8,128)} %get-tuple-element.23.v1, f32[32,512]{1,0:T(8,128)} %get-tuple-element.24.v2), custom_call_target="tpu_custom_call" | custom-call | tf_op jit(solution)/shard_map/final/pallas_call | solution.py:475
Async XLA Ops:
  2.9 10.1 %collective-permute-start = (f32[216,512]{1,0:T(8,128)}, f32[216,512]{1,0:T(8,128)S(1)}, u32[]{:S(2)}, u32[]{:S(2)}) collective-permute-start(f32[216,512]{1,0:T(8,128)} %get-tuple-element.14), channel_id=1, source_target_pairs={{0,32},{32,64},{64,96},{96,128},{128,160},{160,192},{192,224},{224... | collective-permute-start | bytes 1327112 | tf_op jit(solution)/shard_map/ppermute | solution.py:445
  7.5 9.8 %collective-permute-start.1 = (f32[216,512]{1,0:T(8,128)}, f32[216,512]{1,0:T(8,128)S(1)}, u32[]{:S(2)}, u32[]{:S(2)}) collective-permute-start(f32[216,512]{1,0:T(8,128)} %get-tuple-element.15), channel_id=1, source_target_pairs={{32,0},{64,32},{96,64},{128,96},{160,128},{192,160},{224,192},{256... | collective-permute-start | bytes 1327112 | tf_op jit(solution)/shard_map/ppermute | solution.py:444
  13.1 4.3 %copy-start = (f32[216,512]{1,0:T(8,128)}, f32[216,512]{1,0:T(8,128)S(1)}, u32[]{:S(2)}) copy-start(f32[216,512]{1,0:T(8,128)S(1)} %collective-permute-done.above) | copy-start | bytes 1327108
  17.4 0.8 copy-start.1
  21.5 5.1 %collective-permute-start.2 = (f32[80,128]{1,0:T(8,128)}, f32[80,128]{1,0:T(8,128)S(1)}, u32[]{:S(2)}, u32[]{:S(2)}) collective-permute-start(f32[80,128]{1,0:T(8,128)} %get-tuple-element.18), channel_id=1, source_target_pairs={{0,1},{1,2},{2,3},{3,4},{4,5},{5,6},{6,7},{7,8},{8,9},{9,10},{10,1... | collective-permute-start | bytes 122888 | tf_op jit(solution)/shard_map/ppermute | solution.py:454
  24.6 5.0 %collective-permute-start.3 = (f32[80,128]{1,0:T(8,128)}, f32[80,128]{1,0:T(8,128)S(1)}, u32[]{:S(2)}, u32[]{:S(2)}) collective-permute-start(f32[80,128]{1,0:T(8,128)} %get-tuple-element.19), channel_id=1, source_target_pairs={{1,0},{2,1},{3,2},{4,3},{5,4},{6,5},{7,6},{8,7},{9,8},{10,9},{11,1... | collective-permute-start | bytes 122888 | tf_op jit(solution)/shard_map/ppermute | solution.py:453
  26.5 3.0 %copy-start.2 = (f32[80,128]{1,0:T(8,128)}, f32[80,128]{1,0:T(8,128)S(1)}, u32[]{:S(2)}) copy-start(f32[80,128]{1,0:T(8,128)S(1)} %collective-permute-done.2.from_left) | copy-start | bytes 122884
  29.5 0.6 copy-start.3

commit v2 on v1

--- a/solution.py
+++ b/solution.py
@@ -30,16 +30,37 @@
     return jax.ShapeDtypeStruct(shape, jnp.float32)
 
 
-def call(kernel, outs, ins, scratch=(), name=None):
-    return pl.pallas_call(
+def call(kernel, outs, ins, scratch=(), name=None, kept=(), far=(), leaves=(), plain=()):
+    single = not isinstance(outs, tuple)
+    shapes = (outs,) if single else outs
+    specs = tuple(ANY if n in leaves else VM for n in range(len(shapes)))
+    if not INTERPRET:
+        shapes = tuple(
+            x if n in leaves or n in plain else pltpu.VMEM(x.shape, x.dtype)
+            for n, x in enumerate(shapes)
+        )
+    run = pl.pallas_call(
         kernel,
-        out_shape=outs,
+        out_shape=shapes[0] if single else shapes,
         in_specs=ins,
-        out_specs=jax.tree.map(lambda _: VM, outs),
+        out_specs=specs[0] if single else specs,
         scratch_shapes=scratch,
         name=name,
         interpret=INTERPRET,
+        compiler_params=pltpu.CompilerParams(vmem_limit_bytes=16 << 20),
     )
+
+    def apply(*args):
+        if not INTERPRET:
+            args = tuple(
+                pltpu.with_memory_space_constraint(x, pltpu.VMEM if n in kept else pltpu.HBM)
+                if n in kept or n in far
+                else x
+                for n, x in enumerate(args)
+            )
+        return run(*args)
+
+    return apply
 
 
 def edges_kernel(sv, vw, ip, ie, up, down, sems):
@@ -227,7 +248,7 @@
     def kernel(
         place, ground, rows, ext, from_left, from_right,
         depth, base, v0, v1, v2, sums,
-        hi, mid, lo, win, wide, conf,
+        hi, mid, lo, win, wide, conf, sem,
     ):
         lane = lax.broadcasted_iota(jnp.int32, (8, 128), 1)
 
@@ -318,6 +339,8 @@
             return carry
 
         lax.fori_loop(0, 5, fit, 0)
+        written = pltpu.make_async_copy(wide.at[2, pl.ds(0, H), pl.ds(0, W)], depth, sem)
+        written.start()
 
         r = lax.broadcasted_iota(jnp.int32, (EH, EW), 0)
         c = lax.broadcasted_iota(jnp.int32, (EH, EW), 1)
@@ -331,7 +354,6 @@
 
         start = jnp.where(inside, wide[0], 0.0)
         confidence = conf[...] - 0.5
-        depth[...] = wide[2, 0:H, 0:W]
         base[...] = start[0:H, 0:W]
         first = jnp.where(inside, around(start) - 4.0 * start, 0.0)
         v0[...] = first[0:H, 0:W]
@@ -352,6 +374,7 @@
             total = jnp.sum(jnp.sum(product, axis=0, keepdims=True), axis=1, keepdims=True)
             line = jnp.where(spots == n, total, line)
         sums[...] = jnp.broadcast_to(line, (group, 128))
+        written.wait()
 
     return kernel
 
@@ -440,6 +463,7 @@
             [ANY] * 4,
             [pltpu.SemaphoreType.DMA((copies,))],
             name="edges",
+            far=range(4),
         )(sv, wavenumber, phase, extinction)
         below = lax.ppermute(up, "row", chain(row_count, -1))
         above = lax.ppermute(down, "row", chain(row_count, 1))
@@ -449,6 +473,7 @@
             [VM] * 6,
             [pltpu.VMEM((4, 88, 128), jnp.float32), pltpu.VMEM((4, 64, 128), jnp.float32)],
             name="rowsums",
+            kept=range(6),
         )(sv, wavenumber, phase, extinction, above, below)
         from_right = lax.ppermute(left, "col", chain(col_count, -1))
         from_left = lax.ppermute(right, "col", chain(col_count, 1))
@@ -462,17 +487,20 @@
                 pltpu.VMEM((FIELDS * EH, EW), jnp.float32),
                 pltpu.VMEM((3, EH, EW), jnp.float32),
                 pltpu.VMEM((EH, EW), jnp.float32),
+                pltpu.SemaphoreType.DMA,
             ],
             name="fit",
+            kept=(2, 3, 4, 5),
+            leaves=(0,),
         )(place, ground_ratio, rows, ext, from_left, from_right)
         parts = lax.all_to_all(
             sums.reshape(near, 1, 128), both, 0, 0, axis_index_groups=near_groups
         ).reshape(near, 128)
-        parts = call(make_relay_kernel(far), f32(far, 128), [VM], name="relay")(parts)
+        parts = call(make_relay_kernel(far), f32(far, 128), [VM], name="relay", kept=(0,))(parts)
         parts = lax.all_to_all(
             parts.reshape(far, 1, 128), both, 0, 0, axis_index_groups=far_groups
         ).reshape(far, 128)
-        heights = call(final_kernel, f32(H, W), [VM] * 5, name="final")(parts, base, v0, v1, v2)
+        heights = call(final_kernel, f32(H, W), [VM] * 5, name="final", kept=range(5), plain=(0,))(parts, base, v0, v1, v2)
         return heights, depth
 
     placed = (P(None, None, None, "row", "col"), P(), P("row", "col"), P("row", "col"), P("row", "col"))

time: 79.5 us -> 71.2 us (0.90)
  Pallas kernels: 14.9 us -> 8.54 us
  blocking collectives: 39.6 us -> 38.8 us
    pallas_call x5, Pallas kernels: 14.9 us -> 8.54 us  [apply(): return run(*args)]
  transfers between devices with their start and end apart: 4 -> 4, of which waited for: 2 -> 2; matrix products, arithmetic and copies ran while one was open for 1% -> 0% of each run, Pallas kernels for 0% -> 0%
where the time goes in v2:
time: 71.2 us; the launch traced here: 70.8 us
  blocking collectives  38.8 us (54%)
  starting transfers between devices  14.5 us (20%)
  Pallas kernels  8.54 us (12%)
  waiting for transfers between devices  7.54 us (11%)
  between operations  0.75 us (1%)
    all_to_all x1, blocking collectives, local(): lax.all_to_all(sums.reshape(near, 1, 128), both, 0, 0, axis_index_groups=...  24.4 us
    all_to_all x1, blocking collectives, local(): lax.all_to_all(parts.reshape(far, 1, 128), both, 0, 0, axis_index_groups=...  14.3 us
    pallas_call x5, Pallas kernels, apply(): return run(*args)  8.54 us
    ppermute x1, starting transfers between devices, local(): below = lax.ppermute(up, 'row', chain(row_count, -1))  5.48 us
    ppermute x1, starting transfers between devices, local(): above = lax.ppermute(down, 'row', chain(row_count, 1))  4.58 us
    ppermute x1, waiting for transfers between devices, local(): below = lax.ppermute(up, 'row', chain(row_count, -1))  4.12 us
    ppermute x1, waiting for transfers between devices, local(): from_right = lax.ppermute(left, 'col', chain(col_count, -1))  3.42 us
    ppermute x1, starting transfers between devices, local(): from_left = lax.ppermute(right, 'col', chain(col_count, 1))  3.12 us
  transfers between devices with their start and end apart: 4, of which 2 were waited for; matrix products, arithmetic and copies ran while one was open for 0% of the time, Pallas kernels for 0%

profile of v2, /device:TPU:1, one launch (start us, length us, event | category | flops | bytes accessed | tf_op | source)
XLA Modules:
  0.0 70.8 jit_solution(9591129081920598743)
XLA Ops:
  0.6 0.0 copy-start
  0.6 0.0 copy-start.1
  0.7 0.0 copy-start.2
  0.7 0.0 copy-start.3
  0.7 1.4 %edges.1 = (f32[216,512]{1,0:T(8,128)S(1)}, f32[216,512]{1,0:T(8,128)S(1)}) custom-call(f32[12,32,512]{2,1,0:T(8,128)} %bitcast.11, f32[32,512]{1,0:T(8,128)} %vw.3, f32[32,512]{1,0:T(8,128)} %ip.3, f32[32,512]{1,0:T(8,128)} %ie.3), custom_call_target="tpu_custom_call" | custom-call | tf_op jit(solution)/shard_map/edges/pallas_call | solution.py:61
  2.1 4.6 %collective-permute-start = (f32[216,512]{1,0:T(8,128)S(1)}, f32[216,512]{1,0:T(8,128)S(1)}, u32[]{:S(2)}, u32[]{:S(2)}) collective-permute-start(f32[216,512]{1,0:T(8,128)S(1)} %get-tuple-element.14), channel_id=1, source_target_pairs={{0,32},{32,64},{64,96},{96,128},{128,160},{160,192},{192,224},{224... | collective-permute-start | bytes 1327112 | tf_op jit(solution)/shard_map/ppermute | solution.py:469
  6.7 5.5 %collective-permute-start.1 = (f32[216,512]{1,0:T(8,128)S(1)}, f32[216,512]{1,0:T(8,128)S(1)}, u32[]{:S(2)}, u32[]{:S(2)}) collective-permute-start(f32[216,512]{1,0:T(8,128)S(1)} %get-tuple-element.15), channel_id=1, source_target_pairs={{32,0},{64,32},{96,64},{128,96},{160,128},{192,160},{224,192},{256... | collective-permute-start | bytes 1327112 | tf_op jit(solution)/shard_map/ppermute | solution.py:468
  12.2 0.0 collective-permute-done.above
  12.2 4.1 %collective-permute-done.1.below = f32[216,512]{1,0:T(8,128)S(1)} collective-permute-done((f32[216,512]{1,0:T(8,128)S(1)}, f32[216,512]{1,0:T(8,128)S(1)}, u32[]{:S(2)}, u32[]{:S(2)}) %collective-permute-start.1) | collective-permute-done | bytes 442400 | tf_op jit(solution)/shard_map/ppermute | solution.py:468
  16.3 0.0 copy-done
  16.3 0.0 copy-done.1
  16.3 0.0 copy-done.2
  16.3 0.0 copy-done.3
  16.3 1.1 %rowsums.1 = (f32[480,512]{1,0:T(8,128)S(1)}, f32[120,512]{1,0:T(8,128)S(1)}, f32[80,128]{1,0:T(8,128)S(1)}, f32[80,128]{1,0:T(8,128)S(1)}) custom-call(f32[12,32,512]{2,1,0:T(8,128)S(1)} %bitcast.12, f32[32,512]{1,0:T(8,128)S(1)} %copy-done.1, f32[32,512]{1,0:T(8,128)S(1)} %copy-done.2, f32[32,512]{1,0:T(8,128)S(1)} %copy-done.3, ...), custom_call_target="tpu_custom_call" | custom-call | tf_op jit(solution)/shard_map/rowsums/pallas_call | solution.py:61
  17.4 3.1 %collective-permute-start.2 = (f32[80,128]{1,0:T(8,128)S(1)}, f32[80,128]{1,0:T(8,128)S(1)}, u32[]{:S(2)}, u32[]{:S(2)}) collective-permute-start(f32[80,128]{1,0:T(8,128)S(1)} %get-tuple-element.18), channel_id=1, source_target_pairs={{0,1},{1,2},{2,3},{3,4},{4,5},{5,6},{6,7},{7,8},{8,9},{9,10},{10,1... | collective-permute-start | bytes 122888 | tf_op jit(solution)/shard_map/ppermute | solution.py:479
  20.5 1.3 %collective-permute-start.3 = (f32[80,128]{1,0:T(8,128)S(1)}, f32[80,128]{1,0:T(8,128)S(1)}, u32[]{:S(2)}, u32[]{:S(2)}) collective-permute-start(f32[80,128]{1,0:T(8,128)S(1)} %get-tuple-element.19), channel_id=1, source_target_pairs={{1,0},{2,1},{3,2},{4,3},{5,4},{6,5},{7,6},{8,7},{9,8},{10,9},{11,1... | collective-permute-start | bytes 122888 | tf_op jit(solution)/shard_map/ppermute | solution.py:478
  21.8 0.1 pad_add_fusion.place
  21.9 0.0 collective-permute-done.2.from_left
  21.9 3.4 %collective-permute-done.3.from_right = f32[80,128]{1,0:T(8,128)S(1)} collective-permute-done((f32[80,128]{1,0:T(8,128)S(1)}, f32[80,128]{1,0:T(8,128)S(1)}, u32[]{:S(2)}, u32[]{:S(2)}) %collective-permute-start.3) | collective-permute-done | bytes 40992 | tf_op jit(solution)/shard_map/ppermute | solution.py:478
  25.3 0.0 copy-start.4
  25.3 0.7 copy-done.4
  26.0 5.2 %fit.1 = (f32[32,512]{1,0:T(8,128)}, f32[32,512]{1,0:T(8,128)S(1)}, f32[32,512]{1,0:T(8,128)S(1)}, f32[32,512]{1,0:T(8,128)S(1)}, f32[32,512]{1,0:T(8,128)S(1)}, /*index=5*/f32[64,128]{1,0:T(8,128)S(1)}) custom-call(s32[2]{0:T(128)S(1)} %pad_add_fusion.place, f32[3]{0:T(128)S(1)} %copy-done.4, f32[480,512]{1,0:T(8,128)S(1)} %get-tuple-element.16.rows, ...), custom_call_target="tpu_custom_call" | custom-call | tf_op jit(solution)/shard_map/fit/pallas_call | solution.py:61
  31.2 24.4 %all_to_all.10 = f32[64,1,128]{2,1,0:T(1,128)S(1)} all-to-all(f32[64,1,128]{2,1,0:T(1,128)S(1)} %bitcast.14), channel_id=1, replica_groups={{0,1,2,3,4,5,6,7,8,9,10,11,12,13,14,15,16,17,18,19,20,21,22,23,24,25,26..., dimensions={0} | all-to-all | bytes 65536 | tf_op jit(solution)/shard_map/all_to_all | solution.py:496
  55.7 14.3 %all_to_all.11 = f32[8,1,128]{2,1,0:T(1,128)S(1)} all-to-all(f32[8,1,128]{2,1,0:T(1,128)S(1)} %bitcast.15), channel_id=1, replica_groups={{0,64,128,192,256,320,384,448},{1,65,129,193,257,321,385,449},{2,66,130..., dimensions={0} | all-to-all | bytes 8192 | tf_op jit(solution)/shard_map/all_to_all | solution.py:500
  70.0 0.8 %final.1 = f32[32,512]{1,0:T(8,128)} custom-call(f32[8,128]{1,0:T(8,128)S(1)} %bitcast.16, f32[32,512]{1,0:T(8,128)S(1)} %get-tuple-element.21.base, f32[32,512]{1,0:T(8,128)S(1)} %get-tuple-element.22.v0, f32[32,512]{1,0:T(8,128)S(1)} %get-tuple-element.23.v1, f32[32,512]{1,0:T(8,128)S(1)} %get-tuple-element.24.v2), custom_call_target="tpu_custom_call" | custom-call | tf_op jit(solution)/shard_map/final/pallas_call | solution.py:61
  (1 shorter events, 0.0 us)
Async XLA Ops:
  0.6 15.7 %copy-start = (f32[2,2,3,32,512]{4,3,2,1,0:T(8,128)S(1)}, f32[2,2,3,32,512]{4,3,2,1,0:T(8,128)}, u32[]{:S(2)}) copy-start(f32[2,2,3,32,512]{4,3,2,1,0:T(8,128)} %param.5) | copy-start | bytes 2359300
  0.6 15.7 %copy-start.1 = (f32[32,512]{1,0:T(8,128)S(1)}, f32[32,512]{1,0:T(8,128)}, u32[]{:S(2)}) copy-start(f32[32,512]{1,0:T(8,128)} %vw.3) | copy-start | bytes 196612
  0.7 15.7 %copy-start.2 = (f32[32,512]{1,0:T(8,128)S(1)}, f32[32,512]{1,0:T(8,128)}, u32[]{:S(2)}) copy-start(f32[32,512]{1,0:T(8,128)} %ip.3) | copy-start | bytes 196612
  0.7 15.7 %copy-start.3 = (f32[32,512]{1,0:T(8,128)S(1)}, f32[32,512]{1,0:T(8,128)}, u32[]{:S(2)}) copy-start(f32[32,512]{1,0:T(8,128)} %ie.3) | copy-start | bytes 196612
  2.1 10.1 %collective-permute-start = (f32[216,512]{1,0:T(8,128)S(1)}, f32[216,512]{1,0:T(8,128)S(1)}, u32[]{:S(2)}, u32[]{:S(2)}) collective-permute-start(f32[216,512]{1,0:T(8,128)S(1)} %get-tuple-element.14), channel_id=1, source_target_pairs={{0,32},{32,64},{64,96},{96,128},{128,160},{160,192},{192,224},{224... | collective-permute-start | bytes 1327112 | tf_op jit(solution)/shard_map/ppermute | solution.py:469
  6.7 9.6 %collective-permute-start.1 = (f32[216,512]{1,0:T(8,128)S(1)}, f32[216,512]{1,0:T(8,128)S(1)}, u32[]{:S(2)}, u32[]{:S(2)}) collective-permute-start(f32[216,512]{1,0:T(8,128)S(1)} %get-tuple-element.15), channel_id=1, source_target_pairs={{32,0},{64,32},{96,64},{128,96},{160,128},{192,160},{224,192},{256... | collective-permute-start | bytes 1327112 | tf_op jit(solution)/shard_map/ppermute | solution.py:468
  17.4 4.5 %collective-permute-start.2 = (f32[80,128]{1,0:T(8,128)S(1)}, f32[80,128]{1,0:T(8,128)S(1)}, u32[]{:S(2)}, u32[]{:S(2)}) collective-permute-start(f32[80,128]{1,0:T(8,128)S(1)} %get-tuple-element.18), channel_id=1, source_target_pairs={{0,1},{1,2},{2,3},{3,4},{4,5},{5,6},{6,7},{7,8},{8,9},{9,10},{10,1... | collective-permute-start | bytes 122888 | tf_op jit(solution)/shard_map/ppermute | solution.py:479
  20.5 4.8 %collective-permute-start.3 = (f32[80,128]{1,0:T(8,128)S(1)}, f32[80,128]{1,0:T(8,128)S(1)}, u32[]{:S(2)}, u32[]{:S(2)}) collective-permute-start(f32[80,128]{1,0:T(8,128)S(1)} %get-tuple-element.19), channel_id=1, source_target_pairs={{1,0},{2,1},{3,2},{4,3},{5,4},{6,5},{7,6},{8,7},{9,8},{10,9},{11,1... | collective-permute-start | bytes 122888 | tf_op jit(solution)/shard_map/ppermute | solution.py:478
  25.3 0.7 copy-start.4

commit v3 on v2

--- a/solution.py
+++ b/solution.py
@@ -30,7 +30,7 @@
     return jax.ShapeDtypeStruct(shape, jnp.float32)
 
 
-def call(kernel, outs, ins, scratch=(), name=None, kept=(), far=(), leaves=(), plain=()):
+def call(kernel, outs, ins, scratch=(), name=None, kept=(), far=(), leaves=(), plain=(), aliases=None, cost=None):
     single = not isinstance(outs, tuple)
     shapes = (outs,) if single else outs
     specs = tuple(ANY if n in leaves else VM for n in range(len(shapes)))
@@ -47,6 +47,8 @@
         scratch_shapes=scratch,
         name=name,
         interpret=INTERPRET,
+        input_output_aliases=aliases or {},
+        cost_estimate=cost,
         compiler_params=pltpu.CompilerParams(vmem_limit_bytes=16 << 20),
     )
 
@@ -63,22 +65,25 @@
     return apply
 
 
-def edges_kernel(sv, vw, ip, ie, up, down, sems):
-    copies = []
-    for f in range(FIELDS):
-        copies.append((sv.at[f, pl.ds(0, 16)], up.at[pl.ds(16 * f, 16)]))
-        copies.append((sv.at[f, pl.ds(16, 16)], down.at[pl.ds(16 * f, 16)]))
-    for j, ref in enumerate((vw, ip, ie)):
-        at = FIELDS * 16 + 8 * j
-        copies.append((ref.at[pl.ds(0, 8)], up.at[pl.ds(at, 8)]))
-        copies.append((ref.at[pl.ds(24, 8)], down.at[pl.ds(at, 8)]))
-    started = []
-    for n, (src, dst) in enumerate(copies):
-        copy = pltpu.make_async_copy(src, dst, sems.at[n])
-        copy.start()
-        started.append(copy)
-    for copy in started:
-        copy.wait()
+def edges_kernel(lifts):
+    def kernel(sv, vw, ip, ie, out, sems):
+        low = lax.rem(lax.axis_index("row") + lifts, 2)
+        copies = []
+        for f in range(FIELDS):
+            at = pl.ds(pl.multiple_of(16 * low, 16), 16)
+            copies.append((sv.at[f, at], out.at[pl.ds(16 * f, 16)]))
+        for j, ref in enumerate((vw, ip, ie)):
+            at = pl.ds(pl.multiple_of(24 * low, 8), 8)
+            copies.append((ref.at[at], out.at[pl.ds(FIELDS * 16 + 8 * j, 8)]))
+        started = []
+        for n, (src, dst) in enumerate(copies):
+            copy = pltpu.make_async_copy(src, dst, sems.at[n])
+            copy.start()
+            started.append(copy)
+        for copy in started:
+            copy.wait()
+
+    return kernel
 
 
 def strip_source(rows, ext, strip):
@@ -88,9 +93,16 @@
     return ext, (field - FIELDS) * EH + 8 * tile
 
 
-def rows_kernel(sv, vw, ip, ie, above, below, rows, ext, left, right, px, s4):
+def rows_kernel(sv, vw, ip, ie, far, near, rows, ext, far_pack, near_pack, px, s4):
     sub = lax.broadcasted_iota(jnp.int32, (8, 128), 0)
     lane = lax.broadcasted_iota(jnp.int32, (8, 128), 1)
+    odd_row = lax.rem(lax.axis_index("row"), 2) == 1
+    odd_col = lax.rem(lax.axis_index("col"), 2) == 1
+
+    def sides(at, size, cols):
+        one = far[pl.ds(at, size), cols]
+        two = near[pl.ds(at, size), cols]
+        return jnp.where(odd_row, two, one), jnp.where(odd_row, one, two)
 
     def one(n, carry):
         k = n // 4
@@ -99,11 +111,8 @@
 
         def parts(q):
             f = q * 3 + k
-            return (
-                above[pl.ds(pl.multiple_of(16 * f, 16), 16), cols],
-                sv[f, :, cols],
-                below[pl.ds(pl.multiple_of(16 * f, 16), 16), cols],
-            )
+            above, below = sides(pl.multiple_of(16 * f, 16), 16, cols)
+            return above, sv[f, :, cols], below
 
         quads = [parts(q) for q in range(4)]
         for p, (at, size) in enumerate(((8, 16), (24, H), (24 + H, 16))):
@@ -126,13 +135,11 @@
 
     lax.fori_loop(0, 12, one, 0)
     for j, ref in enumerate((vw, ip, ie)):
-        at = FIELDS * 16 + 8 * j
         ext[j * EH : j * EH + H] = ref[...]
         for b in range(4):
             cols = slice(128 * b, 128 * b + 128)
-            ext[j * EH + H : j * EH + EH, cols] = jnp.where(
-                sub < 4, below[at : at + 8, cols], above[at : at + 8, cols]
-            )
+            above, below = sides(FIELDS * 16 + 8 * j, 8, cols)
+            ext[j * EH + H : j * EH + EH, cols] = jnp.where(sub < 4, below, above)
     for v in range(PACK // 8):
         low = jnp.zeros((8, 128), jnp.float32)
         high = jnp.zeros((8, 128), jnp.float32)
@@ -150,8 +157,8 @@
                 last = pltpu.roll(last, (16 * g + 16) % 128, 1)
             low = jnp.where(here, first, low)
             high = jnp.where(here, last, high)
-        left[8 * v : 8 * v + 8] = low
-        right[8 * v : 8 * v + 8] = high
+        far_pack[8 * v : 8 * v + 8] = jnp.where(odd_col, high, low)
+        near_pack[8 * v : 8 * v + 8] = jnp.where(odd_col, low, high)
 
 
 def sincos(x):
@@ -235,6 +242,68 @@
     )
 
 
+def early_kernel(ground, ip, ie, mom, shares):
+    ratios = [jnp.full((8, 128), ground[k], jnp.float32) for k in range(3)]
+    weights = [1.0 / (1.0 + g) for g in ratios]
+    weight = weights[0] * weights[0] + weights[1] * weights[1] + weights[2] * weights[2]
+    offset = (
+        ratios[0] * weights[0] * weights[0]
+        + ratios[1] * weights[1] * weights[1]
+        + ratios[2] * weights[2] * weights[2]
+    )
+    for n, value in enumerate((*weights, weight, offset)):
+        shares[8 * n : 8 * n + 8] = value
+
+    def tiles(i, carry):
+        here = pl.ds(pl.multiple_of(8 * i, 8), 8)
+        for b in range(4):
+            cols = slice(128 * b, 128 * b + 128)
+            for n, value in enumerate(moments(ip[here, cols], ie[here, cols])):
+                mom[n, here, cols] = value
+        return carry
+
+    lax.fori_loop(0, H // 8, tiles, 0)
+
+
+def split(value):
+    first = value.astype(jnp.bfloat16)
+    return first, (value - first.astype(jnp.float32)).astype(jnp.bfloat16)
+
+
+def band(height, width, shift):
+    up = lax.broadcasted_iota(jnp.int32, (height, width), 0) - shift
+    across = lax.broadcasted_iota(jnp.int32, (height, width), 1)
+    return (jnp.abs(up - across) <= RADIUS).astype(jnp.float32).astype(jnp.bfloat16)
+
+
+def dot(a, b):
+    return jnp.dot(a, b, preferred_element_type=jnp.float32)
+
+
+def columns_kernel(rows, ext, held, win, mom, hi, lo):
+    if INTERPRET:
+        mom[:, 0:H] = held[:, 0:H]
+    for n in range(6):
+        here = slice(80 * n, 80 * n + 80)
+        for b in range(4):
+            cols = slice(128 * b, 128 * b + 128)
+            hi[here, cols], lo[here, cols] = split(rows[here, cols])
+    left = band(384, 256, 0)
+    right = band(384, 256, 128)
+    win[:, 0:256] = dot(hi[:, 0:384], left) + dot(lo[:, 0:384], left)
+    win[:, 256:512] = dot(hi[:, 128:512], right) + dot(lo[:, 128:512], right)
+    before = band(128, 128, 128)
+    after = band(128, 128, -128)
+    win[:, 512:640] = (dot(hi[:, 384:512], before) + dot(lo[:, 384:512], before)) + (
+        dot(hi[:, 0:128], after) + dot(lo[:, 0:128], after)
+    )
+    for b in range(4):
+        cols = slice(128 * b, 128 * b + 128)
+        values = moments(ext[EH + H : EH + EH, cols], ext[2 * EH + H : 2 * EH + EH, cols])
+        for n, value in enumerate(values):
+            mom[n, H:EH, cols] = value
+
+
 def around(field):
     return (
         pltpu.roll(field, 1, 0)
@@ -246,71 +315,53 @@
 
 def make_fit_kernel(row_count, col_count, group):
     def kernel(
-        place, ground, rows, ext, from_left, from_right,
+        win, ext, mom, shares, far, near,
         depth, base, v0, v1, v2, sums,
-        hi, mid, lo, win, wide, conf, sem,
+        hi, lo, rim, wide, conf, sem,
     ):
         lane = lax.broadcasted_iota(jnp.int32, (8, 128), 1)
+        row = lax.axis_index("row")
+        col = lax.axis_index("col")
+        odd_col = lax.rem(col, 2) == 1
+        packs = {}
 
         def halo_tile(strip):
             v, g = divmod(strip, 8)
-            lo_part = from_right[8 * v : 8 * v + 8]
-            hi_part = from_left[8 * v : 8 * v + 8]
+            if v not in packs:
+                one = far[8 * v : 8 * v + 8]
+                two = near[8 * v : 8 * v + 8]
+                packs[v] = (jnp.where(odd_col, one, two), jnp.where(odd_col, two, one))
+            lo_part, hi_part = packs[v]
             if g:
                 lo_part = pltpu.roll(lo_part, 128 - 16 * g, 1)
             if g != 7:
                 hi_part = pltpu.roll(hi_part, 112 - 16 * g, 1)
             return jnp.where(lane < 16, lo_part, jnp.where(lane >= 112, hi_part, 0.0))
 
-        def split(value, at, cols):
-            first = value.astype(jnp.bfloat16)
-            rest = value - first.astype(jnp.float32)
-            second = rest.astype(jnp.bfloat16)
-            third = (rest - second.astype(jnp.float32)).astype(jnp.bfloat16)
-            for c in cols:
-                end = c + value.shape[1]
-                hi[at : at + value.shape[0], c:end] = first
-                mid[at : at + value.shape[0], c:end] = second
-                lo[at : at + value.shape[0], c:end] = third
-
-        for f in range(FIELDS):
-            at = f * EH
-            halo = jnp.concatenate([halo_tile(f * 5 + i) for i in range(5)], axis=0)
-            wide[0, 0:EH, 0:128] = halo
-            split(wide[0, 0:EH, 0:128], at, (0, 640))
-            split(rows[at : at + EH, 0:128], at, (128, 768))
-            for b in range(1, 4):
-                split(rows[at : at + EH, 128 * b : 128 * b + 128], at, (128 + 128 * b,))
+        for n in range(6):
+            halo = jnp.concatenate([halo_tile(10 * n + i) for i in range(10)], axis=0)
+            hi[80 * n : 80 * n + 80], lo[80 * n : 80 * n + 80] = split(halo)
         for j in range(3):
-            wide[j, :, 0:W] = ext[j * EH : j * EH + EH]
             for i in range(5):
                 wide[j, 8 * i : 8 * i + 8, W:EW] = halo_tile((FIELDS + j) * 5 + i)
-
-        up = lax.broadcasted_iota(jnp.int32, (384, 128), 0) - 128
-        across = lax.broadcasted_iota(jnp.int32, (384, 128), 1)
-        band = (jnp.abs(up - across) <= RADIUS).astype(jnp.float32).astype(jnp.bfloat16)
-
-        def dot(a):
-            return jnp.dot(a, band, preferred_element_type=jnp.float32)
-
-        for b in range(5):
-            cols = slice(128 * b, 128 * b + 384)
-            win[:, 128 * b : 128 * b + 128] = dot(hi[:, cols]) + (dot(mid[:, cols]) + dot(lo[:, cols]))
-
-        ratios = [jnp.full((8, 128), ground[k], jnp.float32) for k in range(3)]
-        weights = [1.0 / (1.0 + g) for g in ratios]
-        weight = weights[0] * weights[0] + weights[1] * weights[1] + weights[2] * weights[2]
-        offset = (
-            ratios[0] * weights[0] * weights[0]
-            + ratios[1] * weights[1] * weights[1]
-            + ratios[2] * weights[2] * weights[2]
-        )
+        for n, shift in enumerate((128, 0, -128)):
+            part = band(128, 128, shift)
+            rim[:, 128 * n : 128 * n + 128] = dot(hi[...], part) + dot(lo[...], part)
+        rim_of = {0: 0, 4: 1, 3: 2}
+        weights = [shares[8 * n : 8 * n + 8] for n in range(3)]
+        weight = shares[24:32]
+        offset = shares[32:40]
 
         def fit(i, carry):
+            here = pl.ds(pl.multiple_of(8 * i, 8), 8)
+
             def tile(f, b):
-                return win[pl.ds(pl.multiple_of(f * EH + 8 * i, 8), 8), 128 * b : 128 * b + 128]
-
-            here = pl.ds(pl.multiple_of(8 * i, 8), 8)
+                at = pl.ds(pl.multiple_of(f * EH + 8 * i, 8), 8)
+                value = win[at, 128 * b : 128 * b + 128]
+                if b in rim_of:
+                    value = value + rim[at, 128 * rim_of[b] : 128 * rim_of[b] + 128]
+                return value
+
             for b in range(5):
                 cols = slice(128 * b, 128 * b + 128)
                 wre = wim = power = None
@@ -328,14 +379,20 @@
                         wim = cim * weights[k]
                         power = square
                 conf[here, cols] = power * (1.0 / 3.0)
-                phase = wide[1, here, cols]
-                atten = wide[2, here, cols]
-                for _ in range(GAUSS_STEPS):
-                    phase, atten = gauss_step(
-                        phase, atten, moments(phase, atten), wre, wim, weight, offset
+                if b < 4:
+                    kz, phase, atten = (
+                        ext[pl.ds(pl.multiple_of(j * EH + 8 * i, 8), 8), cols] for j in range(3)
                     )
+                else:
+                    kz, phase, atten = (wide[j, here, cols] for j in range(3))
+                for step in range(GAUSS_STEPS):
+                    if step or b == 4:
+                        now = moments(phase, atten)
+                    else:
+                        now = tuple(mom[n, here, cols] for n in range(5))
+                    phase, atten = gauss_step(phase, atten, now, wre, wim, weight, offset)
                 wide[2, here, cols] = atten
-                wide[0, here, cols] = phase / wide[0, here, cols]
+                wide[0, here, cols] = phase / kz
             return carry
 
         lax.fori_loop(0, 5, fit, 0)
@@ -344,10 +401,10 @@
 
         r = lax.broadcasted_iota(jnp.int32, (EH, EW), 0)
         c = lax.broadcasted_iota(jnp.int32, (EH, EW), 1)
-        row_low = jnp.where(place[0] == 0, EH - 4, EH)
-        row_high = jnp.where(place[0] == row_count - 1, H, EH - 4)
-        col_low = jnp.where(place[1] == 0, EW, EW - 4)
-        col_high = jnp.where(place[1] == col_count - 1, W, W + 4)
+        row_low = jnp.where(row == 0, EH - 4, EH)
+        row_high = jnp.where(row == row_count - 1, H, EH - 4)
+        col_low = jnp.where(col == 0, EW, EW - 4)
+        col_high = jnp.where(col == col_count - 1, W, W + 4)
         row_bad = ((r >= row_high) & (r < EH - 4)) | (r >= row_low)
         col_bad = (c >= col_high) & (c < col_low)
         inside = jnp.logical_not(row_bad | col_bad)
@@ -437,36 +494,50 @@
 def solution(mesh):
     row_count = mesh.shape["row"]
     col_count = mesh.shape["col"]
-    near = 2 * col_count
-    far = row_count // 2
+    near_count = 2 * col_count
+    far_count = row_count // 2
 
     def index(r, c):
         return r * col_count + c
 
     near_groups = [
-        [index(2 * y + core, c) for core in range(2) for c in range(col_count)] for y in range(far)
+        [index(2 * y + core, c) for core in range(2) for c in range(col_count)] for y in range(far_count)
     ]
     far_groups = [
-        [index(2 * y + core, c) for y in range(far)] for core in range(2) for c in range(col_count)
+        [index(2 * y + core, c) for y in range(far_count)] for core in range(2) for c in range(col_count)
     ]
     both = ("row", "col")
 
-    def chain(count, step):
-        return [(i, i + step) for i in range(count) if 0 <= i + step < count]
+    def swap(count, start):
+        pairs = [(i, i + 1) for i in range(start, count - 1, 2)]
+        return pairs + [(j, i) for i, j in pairs]
 
     def local(scatter_vectors, ground_ratio, wavenumber, phase, extinction):
         sv = scatter_vectors.reshape(FIELDS, H, W)
-        copies = 2 * (FIELDS + 3)
-        up, down = call(
-            edges_kernel,
-            (f32(SEND_ROWS, W), f32(SEND_ROWS, W)),
-            [ANY] * 4,
-            [pltpu.SemaphoreType.DMA((copies,))],
-            name="edges",
-            far=range(4),
-        )(sv, wavenumber, phase, extinction)
-        below = lax.ppermute(up, "row", chain(row_count, -1))
-        above = lax.ppermute(down, "row", chain(row_count, 1))
+        inputs = (sv, wavenumber, phase, extinction)
+
+        def edges(lifts, name):
+            return call(
+                edges_kernel(lifts),
+                f32(SEND_ROWS, W),
+                [ANY] * 4,
+                [pltpu.SemaphoreType.DMA((FIELDS + 3,))],
+                name=name,
+                far=range(4),
+            )(*inputs)
+
+        busy = pl.CostEstimate(flops=6000000, transcendentals=0, bytes_accessed=0)
+        far = lax.ppermute(edges(0, "faredges"), "row", swap(row_count, 1))
+        near = lax.ppermute(edges(1, "nearedges"), "row", swap(row_count, 0))
+        mom, shares = call(
+            early_kernel,
+            (f32(5, EH, W), f32(40, 128)),
+            [SM, VM, VM],
+            name="early",
+            kept=(1, 2),
+            cost=busy,
+        )(ground_ratio, phase, extinction)
+        far, near, mom, shares = lax.optimization_barrier((far, near, mom, shares))
         rows, ext, left, right = call(
             rows_kernel,
             (f32(FIELDS * EH, W), f32(3 * EH, W), f32(PACK, 128), f32(PACK, 128)),
@@ -474,32 +545,41 @@
             [pltpu.VMEM((4, 88, 128), jnp.float32), pltpu.VMEM((4, 64, 128), jnp.float32)],
             name="rowsums",
             kept=range(6),
-        )(sv, wavenumber, phase, extinction, above, below)
-        from_right = lax.ppermute(left, "col", chain(col_count, -1))
-        from_left = lax.ppermute(right, "col", chain(col_count, 1))
-        place = jnp.stack([lax.axis_index("row"), lax.axis_index("col")]).astype(jnp.int32)
+        )(*inputs, far, near)
+        far = lax.ppermute(left, "col", swap(col_count, 1))
+        near = lax.ppermute(right, "col", swap(col_count, 0))
+        win, mom = call(
+            columns_kernel,
+            (f32(FIELDS * EH, EW), f32(5, EH, W)),
+            [VM] * 3,
+            [pltpu.VMEM((FIELDS * EH, W), jnp.bfloat16)] * 2,
+            name="colsums",
+            kept=range(3),
+            aliases={2: 1},
+            cost=busy,
+        )(rows, ext, mom)
         depth, base, v0, v1, v2, sums = call(
-            make_fit_kernel(row_count, col_count, near),
-            tuple(f32(H, W) for _ in range(5)) + (f32(near, 128),),
-            [SM, SM] + [VM] * 4,
-            [pltpu.VMEM((FIELDS * EH, 896), jnp.bfloat16)] * 3
+            make_fit_kernel(row_count, col_count, near_count),
+            tuple(f32(H, W) for _ in range(5)) + (f32(near_count, 128),),
+            [VM] * 6,
+            [pltpu.VMEM((FIELDS * EH, 128), jnp.bfloat16)] * 2
             + [
-                pltpu.VMEM((FIELDS * EH, EW), jnp.float32),
+                pltpu.VMEM((FIELDS * EH, 384), jnp.float32),
                 pltpu.VMEM((3, EH, EW), jnp.float32),
                 pltpu.VMEM((EH, EW), jnp.float32),
                 pltpu.SemaphoreType.DMA,
             ],
             name="fit",
-            kept=(2, 3, 4, 5),
+            kept=range(6),
             leaves=(0,),
-        )(place, ground_ratio, rows, ext, from_left, from_right)
+        )(win, ext, mom, shares, far, near)
         parts = lax.all_to_all(
-            sums.reshape(near, 1, 128), both, 0, 0, axis_index_groups=near_groups
-        ).reshape(near, 128)
-        parts = call(make_relay_kernel(far), f32(far, 128), [VM], name="relay", kept=(0,))(parts)
+            sums.reshape(near_count, 1, 128), both, 0, 0, axis_index_groups=near_groups
+        ).reshape(near_count, 128)
+        parts = call(make_relay_kernel(far_count), f32(far_count, 128), [VM], name="relay", kept=(0,))(parts)
         parts = lax.all_to_all(
-            parts.reshape(far, 1, 128), both, 0, 0, axis_index_groups=far_groups
-        ).reshape(far, 128)
+            parts.reshape(far_count, 1, 128), both, 0, 0, axis_index_groups=far_groups
+        ).reshape(far_count, 128)
         heights = call(final_kernel, f32(H, W), [VM] * 5, name="final", kept=range(5), plain=(0,))(parts, base, v0, v1, v2)
         return heights, depth
 

time: 71.2 us -> 64 us (0.90)
  waiting for transfers between devices: 7.54 us -> 1.59 us
  blocking collectives: 38.8 us -> 37.9 us
    ppermute x4, waiting for transfers between devices: 7.54 us -> 1.59 us  [the longest x1 1.21 us: local(): near = lax.ppermute(right, 'col', swap(col_count, 0))]
    all_to_all x2, blocking collectives: 38.8 us -> 37.9 us  [the longest x1 22 us: local(): lax.all_to_all(sums.reshape(near_count, 1, 128), both, 0, 0, axis_index_g...]
    pallas_call x5 -> x8, Pallas kernels: 8.54 us -> 8.98 us  [apply(): return run(*args)]
  transfers between devices with their start and end apart: 4 -> 4, of which waited for: 2 -> 2; matrix products, arithmetic and copies ran while one was open for 0% -> 0% of each run, Pallas kernels for 0% -> 5%
where the time goes in v3:
time: 64 us; the launch traced here: 63.6 us
  blocking collectives  37.9 us (59%)
  starting transfers between devices  14.3 us (22%)
  Pallas kernels  8.98 us (14%)
  waiting for transfers between devices  1.59 us (2%)
  between operations  0.79 us (1%)
    all_to_all x1, blocking collectives, local(): lax.all_to_all(sums.reshape(near_count, 1, 128), both, 0, 0, axis_index_g...  22 us
    all_to_all x1, blocking collectives, local(): lax.all_to_all(parts.reshape(far_count, 1, 128), both, 0, 0, axis_index_g...  15.9 us
    pallas_call x8, Pallas kernels, apply(): return run(*args)  8.98 us
    ppermute x1, starting transfers between devices, local(): near = lax.ppermute(edges(1, 'nearedges'), 'row', swap(row_count, 0))  4.85 us
    ppermute x1, starting transfers between devices, local(): far = lax.ppermute(edges(0, 'faredges'), 'row', swap(row_count, 1))  4.58 us
    ppermute x1, starting transfers between devices, local(): near = lax.ppermute(right, 'col', swap(col_count, 0))  4.22 us
  transfers between devices with their start and end apart: 4, of which 2 were waited for; matrix products, arithmetic and copies ran while one was open for 0% of the time, Pallas kernels for 5%

profile of v3, /device:TPU:1, one launch (start us, length us, event | category | flops | bytes accessed | tf_op | source)
XLA Modules:
  0.0 63.6 jit_solution(3407509320302234039)
XLA Ops:
  0.6 0.0 copy-start.1
  0.6 0.0 copy-start.2
  0.7 0.0 copy-start.4
  0.7 0.0 copy-start
  0.7 0.0 copy-start.3
  0.7 1.2 %faredges.1 = f32[216,512]{1,0:T(8,128)S(1)} custom-call(f32[12,32,512]{2,1,0:T(8,128)} %bitcast.9, f32[32,512]{1,0:T(8,128)} %vw.5, f32[32,512]{1,0:T(8,128)} %ip.7, f32[32,512]{1,0:T(8,128)} %ie.7), custom_call_target="tpu_custom_call" | custom-call | tf_op jit(solution)/shard_map/faredges/pallas_call | solution.py:63
  1.9 4.6 %collective-permute-start = (f32[216,512]{1,0:T(8,128)S(1)}, f32[216,512]{1,0:T(8,128)S(1)}, u32[]{:S(2)}, u32[]{:S(2)}) collective-permute-start(f32[216,512]{1,0:T(8,128)S(1)} %faredges.1), channel_id=1, source_target_pairs={{32,64},{96,128},{160,192},{224,256},{288,320},{352,384},{416,448}... | collective-permute-start | bytes 1327112 | tf_op jit(solution)/shard_map/ppermute | solution.py:530
  6.4 1.1 %nearedges.1 = f32[216,512]{1,0:T(8,128)S(1)} custom-call(f32[12,32,512]{2,1,0:T(8,128)} %bitcast.10, f32[32,512]{1,0:T(8,128)} %vw.5, f32[32,512]{1,0:T(8,128)} %ip.7, f32[32,512]{1,0:T(8,128)} %ie.7), custom_call_target="tpu_custom_call" | custom-call | tf_op jit(solution)/shard_map/nearedges/pallas_call | solution.py:63
  7.5 4.9 %collective-permute-start.1 = (f32[216,512]{1,0:T(8,128)S(1)}, f32[216,512]{1,0:T(8,128)S(1)}, u32[]{:S(2)}, u32[]{:S(2)}) collective-permute-start(f32[216,512]{1,0:T(8,128)S(1)} %nearedges.1), channel_id=1, source_target_pairs={{0,32},{64,96},{128,160},{192,224},{256,288},{320,352},{384,416},{... | collective-permute-start | bytes 1327112 | tf_op jit(solution)/shard_map/ppermute | solution.py:531
  12.4 0.0 copy-done.1
  12.4 0.0 copy-done.2
  12.4 0.0 copy-done.4
  12.4 1.0 %early.1 = (f32[5,40,512]{2,1,0:T(8,128)S(1)}, f32[40,128]{1,0:T(8,128)S(1)}) custom-call(f32[3]{0:T(128)S(1)} %copy-done.4, f32[32,512]{1,0:T(8,128)S(1)} %copy-done.1, f32[32,512]{1,0:T(8,128)S(1)} %copy-done.2), custom_call_target="tpu_custom_call" | custom-call | flops 6000000 | tf_op jit(solution)/shard_map/early/pallas_call | solution.py:63
  13.4 0.0 collective-permute-done.far
  13.4 0.4 collective-permute-done.1.near
  13.8 0.0 copy-done
  13.8 0.0 copy-done.3
  13.8 1.1 %rowsums.1 = (f32[480,512]{1,0:T(8,128)S(1)}, f32[120,512]{1,0:T(8,128)S(1)}, f32[80,128]{1,0:T(8,128)S(1)}, f32[80,128]{1,0:T(8,128)S(1)}) custom-call(f32[12,32,512]{2,1,0:T(8,128)S(1)} %bitcast.11, f32[32,512]{1,0:T(8,128)S(1)} %copy-done.3, f32[32,512]{1,0:T(8,128)S(1)} %copy-done.1, f32[32,512]{1,0:T(8,128)S(1)} %copy-done.2, ...), custom_call_target="tpu_custom_call" | custom-call | tf_op jit(solution)/shard_map/rowsums/pallas_call | solution.py:63
  14.9 0.7 %collective-permute-start.2 = (f32[80,128]{1,0:T(8,128)S(1)}, f32[80,128]{1,0:T(8,128)S(1)}, u32[]{:S(2)}, u32[]{:S(2)}) collective-permute-start(f32[80,128]{1,0:T(8,128)S(1)} %get-tuple-element.30), channel_id=1, source_target_pairs={{1,2},{3,4},{5,6},{7,8},{9,10},{11,12},{13,14},{15,16},{17,18},{19... | collective-permute-start | bytes 122888 | tf_op jit(solution)/shard_map/ppermute | solution.py:549
  15.6 4.2 %collective-permute-start.3 = (f32[80,128]{1,0:T(8,128)S(1)}, f32[80,128]{1,0:T(8,128)S(1)}, u32[]{:S(2)}, u32[]{:S(2)}) collective-permute-start(f32[80,128]{1,0:T(8,128)S(1)} %get-tuple-element.31), channel_id=1, source_target_pairs={{0,1},{2,3},{4,5},{6,7},{8,9},{10,11},{12,13},{14,15},{16,17},{18,... | collective-permute-start | bytes 122888 | tf_op jit(solution)/shard_map/ppermute | solution.py:550
  19.8 0.8 %colsums.1 = (f32[480,640]{1,0:T(8,128)S(1)}, f32[5,40,512]{2,1,0:T(8,128)S(1)}) custom-call(f32[480,512]{1,0:T(8,128)S(1)} %get-tuple-element.24.rows, f32[120,512]{1,0:T(8,128)S(1)} %get-tuple-element.25.ext, f32[5,40,512]{2,1,0:T(8,128)S(1)} %get-tuple-element.26.held), custom_call_target="tpu_custom_call", output_to_operand_aliasing={{1}: (2, {})} | custom-call | flops 6000000 | tf_op jit(solution)/shard_map/colsums/pallas_call | solution.py:63
  20.7 0.0 collective-permute-done.2.far
  20.7 1.2 %collective-permute-done.3.near = f32[80,128]{1,0:T(8,128)S(1)} collective-permute-done((f32[80,128]{1,0:T(8,128)S(1)}, f32[80,128]{1,0:T(8,128)S(1)}, u32[]{:S(2)}, u32[]{:S(2)}) %collective-permute-start.3) | collective-permute-done | bytes 40992 | tf_op jit(solution)/shard_map/ppermute | solution.py:550
  21.9 3.0 %fit.1 = (f32[32,512]{1,0:T(8,128)}, f32[32,512]{1,0:T(8,128)S(1)}, f32[32,512]{1,0:T(8,128)S(1)}, f32[32,512]{1,0:T(8,128)S(1)}, f32[32,512]{1,0:T(8,128)S(1)}, /*index=5*/f32[64,128]{1,0:T(8,128)S(1)}) custom-call(f32[480,640]{1,0:T(8,128)S(1)} %get-tuple-element.27.win, f32[120,512]{1,0:T(8,128)S(1)} %get-tuple-element.25.ext, ...), custom_call_target="tpu_custom_call" | custom-call | tf_op jit(solution)/shard_map/fit/pallas_call | solution.py:63
  24.9 22.0 %all_to_all.10 = f32[64,1,128]{2,1,0:T(1,128)S(1)} all-to-all(f32[64,1,128]{2,1,0:T(1,128)S(1)} %bitcast.13), channel_id=1, replica_groups={{0,1,2,3,4,5,6,7,8,9,10,11,12,13,14,15,16,17,18,19,20,21,22,23,24,25,26..., dimensions={0} | all-to-all | bytes 65536 | tf_op jit(solution)/shard_map/all_to_all | solution.py:576
  46.9 15.9 %all_to_all.11 = f32[8,1,128]{2,1,0:T(1,128)S(1)} all-to-all(f32[8,1,128]{2,1,0:T(1,128)S(1)} %bitcast.14), channel_id=1, replica_groups={{0,64,128,192,256,320,384,448},{1,65,129,193,257,321,385,449},{2,66,130..., dimensions={0} | all-to-all | bytes 8192 | tf_op jit(solution)/shard_map/all_to_all | solution.py:580
  62.8 0.8 %final.1 = f32[32,512]{1,0:T(8,128)} custom-call(f32[8,128]{1,0:T(8,128)S(1)} %bitcast.15, f32[32,512]{1,0:T(8,128)S(1)} %get-tuple-element.33.base, f32[32,512]{1,0:T(8,128)S(1)} %get-tuple-element.34.v0, f32[32,512]{1,0:T(8,128)S(1)} %get-tuple-element.35.v1, f32[32,512]{1,0:T(8,128)S(1)} %get-tuple-element.36.v2), custom_call_target="tpu_custom_call" | custom-call | tf_op jit(solution)/shard_map/final/pallas_call | solution.py:63
  (1 shorter events, 0.0 us)
Async XLA Ops:
  0.6 11.8 %copy-start.1 = (f32[32,512]{1,0:T(8,128)S(1)}, f32[32,512]{1,0:T(8,128)}, u32[]{:S(2)}) copy-start(f32[32,512]{1,0:T(8,128)} %ip.7) | copy-start | bytes 196612
  0.6 11.8 %copy-start.2 = (f32[32,512]{1,0:T(8,128)S(1)}, f32[32,512]{1,0:T(8,128)}, u32[]{:S(2)}) copy-start(f32[32,512]{1,0:T(8,128)} %ie.7) | copy-start | bytes 196612
  0.7 11.8 %copy-start.4 = (f32[3]{0:T(128)S(1)}, f32[3]{0:T(128)}, u32[]{:S(2)}) copy-start(f32[3]{0:T(128)} %ground.1) | copy-start | bytes 40
  0.7 13.1 %copy-start = (f32[2,2,3,32,512]{4,3,2,1,0:T(8,128)S(1)}, f32[2,2,3,32,512]{4,3,2,1,0:T(8,128)}, u32[]{:S(2)}) copy-start(f32[2,2,3,32,512]{4,3,2,1,0:T(8,128)} %param.5) | copy-start | bytes 2359300
  0.7 13.1 %copy-start.3 = (f32[32,512]{1,0:T(8,128)S(1)}, f32[32,512]{1,0:T(8,128)}, u32[]{:S(2)}) copy-start(f32[32,512]{1,0:T(8,128)} %vw.5) | copy-start | bytes 196612
  1.9 11.6 %collective-permute-start = (f32[216,512]{1,0:T(8,128)S(1)}, f32[216,512]{1,0:T(8,128)S(1)}, u32[]{:S(2)}, u32[]{:S(2)}) collective-permute-start(f32[216,512]{1,0:T(8,128)S(1)} %faredges.1), channel_id=1, source_target_pairs={{32,64},{96,128},{160,192},{224,256},{288,320},{352,384},{416,448}... | collective-permute-start | bytes 1327112 | tf_op jit(solution)/shard_map/ppermute | solution.py:530
  7.5 6.3 %collective-permute-start.1 = (f32[216,512]{1,0:T(8,128)S(1)}, f32[216,512]{1,0:T(8,128)S(1)}, u32[]{:S(2)}, u32[]{:S(2)}) collective-permute-start(f32[216,512]{1,0:T(8,128)S(1)} %nearedges.1), channel_id=1, source_target_pairs={{0,32},{64,96},{128,160},{192,224},{256,288},{320,352},{384,416},{... | collective-permute-start | bytes 1327112 | tf_op jit(solution)/shard_map/ppermute | solution.py:531
  14.9 5.7 %collective-permute-start.2 = (f32[80,128]{1,0:T(8,128)S(1)}, f32[80,128]{1,0:T(8,128)S(1)}, u32[]{:S(2)}, u32[]{:S(2)}) collective-permute-start(f32[80,128]{1,0:T(8,128)S(1)} %get-tuple-element.30), channel_id=1, source_target_pairs={{1,2},{3,4},{5,6},{7,8},{9,10},{11,12},{13,14},{15,16},{17,18},{19... | collective-permute-start | bytes 122888 | tf_op jit(solution)/shard_map/ppermute | solution.py:549
  15.6 6.3 %collective-permute-start.3 = (f32[80,128]{1,0:T(8,128)S(1)}, f32[80,128]{1,0:T(8,128)S(1)}, u32[]{:S(2)}, u32[]{:S(2)}) collective-permute-start(f32[80,128]{1,0:T(8,128)S(1)} %get-tuple-element.31), channel_id=1, source_target_pairs={{0,1},{2,3},{4,5},{6,7},{8,9},{10,11},{12,13},{14,15},{16,17},{18,... | collective-permute-start | bytes 122888 | tf_op jit(solution)/shard_map/ppermute | solution.py:550

commit v4 on v3

--- a/solution.py
+++ b/solution.py
@@ -17,9 +17,13 @@
 EH = 40
 EW = 640
 FIELDS = 12
-SEND_ROWS = FIELDS * 16 + 3 * 8
-STRIPS = (FIELDS + 3) * (EH // 8)
-PACK = -(-STRIPS // 8) * 8
+SIDE = RADIUS + 4
+REST = SIDE - 8
+REST_AT = FIELDS * 8
+EXTRA_AT = REST_AT + FIELDS * REST
+SEND_ROWS = EXTRA_AT + 3 * 4
+GROUPS = 128 // SIDE
+PACK = 8 * (-(-FIELDS * 5 // GROUPS) + 1)
 VM = pl.BlockSpec(memory_space=pltpu.VMEM)
 SM = pl.BlockSpec(memory_space=pltpu.SMEM)
 ANY = pl.BlockSpec(memory_space=pl.ANY)
@@ -66,31 +70,39 @@
 
 
 def edges_kernel(lifts):
-    def kernel(sv, vw, ip, ie, out, sems):
+    def kernel(sv, vw, ip, ie, out, tiles, rest, extra, sems):
         low = lax.rem(lax.axis_index("row") + lifts, 2)
-        copies = []
-        for f in range(FIELDS):
-            at = pl.ds(pl.multiple_of(16 * low, 16), 16)
-            copies.append((sv.at[f, at], out.at[pl.ds(16 * f, 16)]))
+        edge = pl.ds(pl.multiple_of(24 * low, 8), 8)
+        inner = pl.ds(pl.multiple_of(8 + 8 * low, 8), 8)
+        started = [
+            pltpu.make_async_copy(sv.at[:, inner], rest, sems.at[0]),
+            pltpu.make_async_copy(sv.at[:, edge], tiles, sems.at[1]),
+        ]
         for j, ref in enumerate((vw, ip, ie)):
-            at = pl.ds(pl.multiple_of(24 * low, 8), 8)
-            copies.append((ref.at[at], out.at[pl.ds(FIELDS * 16 + 8 * j, 8)]))
-        started = []
-        for n, (src, dst) in enumerate(copies):
-            copy = pltpu.make_async_copy(src, dst, sems.at[n])
+            started.append(pltpu.make_async_copy(ref.at[edge], extra.at[j], sems.at[2 + j]))
+        for copy in started:
             copy.start()
-            started.append(copy)
         for copy in started:
             copy.wait()
+        bottom = low == 1
+        for f in range(FIELDS):
+            out[8 * f : 8 * f + 8] = tiles[f]
+            at = REST_AT + REST * f
+            out[at : at + REST] = jnp.where(bottom, rest[f, 8 - REST : 8], rest[f, 0:REST])
+        for j in range(3):
+            at = EXTRA_AT + 4 * j
+            out[at : at + 4] = jnp.where(bottom, extra[j, 4:8], extra[j, 0:4])
 
     return kernel
 
 
-def strip_source(rows, ext, strip):
-    field, tile = divmod(strip, EH // 8)
-    if field < FIELDS:
-        return rows, field * EH + 8 * tile
-    return ext, (field - FIELDS) * EH + 8 * tile
+def strips():
+    out = []
+    for n in range(FIELDS * 5):
+        out.append((n // GROUPS, SIDE * (n % GROUPS), SIDE))
+    for n in range(3 * 5):
+        out.append((PACK // 8 - 1, 4 * n, 4))
+    return out
 
 
 def rows_kernel(sv, vw, ip, ie, far, near, rows, ext, far_pack, near_pack, px, s4):
@@ -100,65 +112,64 @@
     odd_col = lax.rem(lax.axis_index("col"), 2) == 1
 
     def sides(at, size, cols):
-        one = far[pl.ds(at, size), cols]
-        two = near[pl.ds(at, size), cols]
+        one = far[at : at + size, cols]
+        two = near[at : at + size, cols]
         return jnp.where(odd_row, two, one), jnp.where(odd_row, one, two)
 
-    def one(n, carry):
-        k = n // 4
-        b = n % 4
-        cols = pl.ds(pl.multiple_of(b * 128, 128), 128)
-
-        def parts(q):
-            f = q * 3 + k
-            above, below = sides(pl.multiple_of(16 * f, 16), 16, cols)
-            return above, sv[f, :, cols], below
-
-        quads = [parts(q) for q in range(4)]
-        for p, (at, size) in enumerate(((8, 16), (24, H), (24 + H, 16))):
-            re1, im1, re2, im2 = (quad[p] for quad in quads)
-            px[0, at : at + size] = re1 * re1 + im1 * im1
-            px[1, at : at + size] = re2 * re2 + im2 * im2
-            px[2, at : at + size] = re1 * re2 + im1 * im2
-            px[3, at : at + size] = re1 * im2 - im1 * re2
-        for j in range(4):
-            two = px[j, 7:79] + px[j, 8:80]
-            four = two[0:64] + (px[j, 9:73] + px[j, 10:74])
-            s4[j, 0:64] = four
-            eight = four[0:56] + s4[j, 4:60]
-            sixteen = eight[0:48] + eight[8:56]
-            total = sixteen + two[16:64] + px[j, 25:73]
-            at = pl.multiple_of((j * 3 + k) * EH, 8)
-            rows[pl.ds(at, H), cols] = total[8:40]
-            rows[pl.ds(at + H, 8), cols] = jnp.where(sub < 4, total[40:48], total[0:8])
-        return carry
-
-    lax.fori_loop(0, 12, one, 0)
+    for k in range(3):
+
+        def block(b, carry, k=k):
+            cols = pl.ds(pl.multiple_of(b * 128, 128), 128)
+
+            def parts(q):
+                f = q * 3 + k
+                above, below = sides(8 * f, 8, cols)
+                above_rest, below_rest = sides(REST_AT + REST * f, REST, cols)
+                return above_rest, above, sv[f, :, cols], below, below_rest
+
+            quads = [parts(q) for q in range(4)]
+            at = 24 - SIDE
+            for p, size in enumerate((REST, 8, H, 8, REST)):
+                re1, im1, re2, im2 = (quad[p] for quad in quads)
+                px[0, at : at + size] = re1 * re1 + im1 * im1
+                px[1, at : at + size] = re2 * re2 + im2 * im2
+                px[2, at : at + size] = re1 * re2 + im1 * im2
+                px[3, at : at + size] = re1 * im2 - im1 * re2
+                at += size
+            for j in range(4):
+                two = px[j, 7:79] + px[j, 8:80]
+                four = two[0:64] + (px[j, 9:73] + px[j, 10:74])
+                s4[j, 0:64] = four
+                eight = four[0:56] + s4[j, 4:60]
+                sixteen = eight[0:48] + eight[8:56]
+                total = sixteen + two[16:64] + px[j, 25:73]
+                at = (j * 3 + k) * EH
+                rows[at : at + H, cols] = total[8:40]
+                rows[at + H : at + EH, cols] = jnp.where(sub < 4, total[40:48], total[0:8])
+            return carry
+
+        lax.fori_loop(0, 4, block, 0)
     for j, ref in enumerate((vw, ip, ie)):
         ext[j * EH : j * EH + H] = ref[...]
-        for b in range(4):
-            cols = slice(128 * b, 128 * b + 128)
-            above, below = sides(FIELDS * 16 + 8 * j, 8, cols)
-            ext[j * EH + H : j * EH + EH, cols] = jnp.where(sub < 4, below, above)
+        above, below = sides(EXTRA_AT + 4 * j, 4, slice(0, W))
+        ext[j * EH + H : j * EH + H + 4] = below
+        ext[j * EH + H + 4 : j * EH + EH] = above
+    low = [jnp.zeros((8, 128), jnp.float32)] * (PACK // 8)
+    high = list(low)
+    for n, (v, at, width) in enumerate(strips()):
+        here = (lane >= at) & (lane < at + width)
+        ref = rows if n < FIELDS * 5 else ext
+        top = 8 * n if n < FIELDS * 5 else 8 * n - FIELDS * EH
+        first = ref[top : top + 8, 0:128]
+        last = ref[top : top + 8, W - 128 : W]
+        if at:
+            first = pltpu.roll(first, at, 1)
+        last = pltpu.roll(last, at + width, 1)
+        low[v] = jnp.where(here, first, low[v])
+        high[v] = jnp.where(here, last, high[v])
     for v in range(PACK // 8):
-        low = jnp.zeros((8, 128), jnp.float32)
-        high = jnp.zeros((8, 128), jnp.float32)
-        for g in range(8):
-            strip = 8 * v + g
-            if strip >= STRIPS:
-                break
-            ref, at = strip_source(rows, ext, strip)
-            here = (lane >= 16 * g) & (lane < 16 * g + 16)
-            first = ref[at : at + 8, 0:128]
-            last = ref[at : at + 8, W - 128 : W]
-            if g:
-                first = pltpu.roll(first, 16 * g, 1)
-            if g != 7:
-                last = pltpu.roll(last, (16 * g + 16) % 128, 1)
-            low = jnp.where(here, first, low)
-            high = jnp.where(here, last, high)
-        far_pack[8 * v : 8 * v + 8] = jnp.where(odd_col, high, low)
-        near_pack[8 * v : 8 * v + 8] = jnp.where(odd_col, low, high)
+        far_pack[8 * v : 8 * v + 8] = jnp.where(odd_col, high[v], low[v])
+        near_pack[8 * v : 8 * v + 8] = jnp.where(odd_col, low[v], high[v])
 
 
 def sincos(x):
@@ -242,6 +253,27 @@
     )
 
 
+def fit_tile(sums, weights, weight, offset, phase, atten, first):
+    wre = wim = power = None
+    for k in range(3):
+        scale = lax.rsqrt(sums(k) * sums(3 + k) + EPSILON)
+        cre = sums(6 + k) * scale
+        cim = sums(9 + k) * scale
+        square = cre * cre + cim * cim
+        if k:
+            wre = wre + cre * weights[k]
+            wim = wim + cim * weights[k]
+            power = power + square
+        else:
+            wre = cre * weights[k]
+            wim = cim * weights[k]
+            power = square
+    for step in range(GAUSS_STEPS):
+        now = moments(phase, atten) if step or first is None else first
+        phase, atten = gauss_step(phase, atten, now, wre, wim, weight, offset)
+    return phase, atten, power * (1.0 / 3.0)
+
+
 def early_kernel(ground, ip, ie, mom, shares):
     ratios = [jnp.full((8, 128), ground[k], jnp.float32) for k in range(3)]
     weights = [1.0 / (1.0 + g) for g in ratios]
@@ -280,7 +312,7 @@
     return jnp.dot(a, b, preferred_element_type=jnp.float32)
 
 
-def columns_kernel(rows, ext, held, win, mom, hi, lo):
+def columns_kernel(rows, ext, shares, held, win, mom, mid, hi, lo):
     if INTERPRET:
         mom[:, 0:H] = held[:, 0:H]
     for n in range(6):
@@ -302,6 +334,30 @@
         values = moments(ext[EH + H : EH + EH, cols], ext[2 * EH + H : 2 * EH + EH, cols])
         for n, value in enumerate(values):
             mom[n, H:EH, cols] = value
+    weights = [shares[8 * n : 8 * n + 8] for n in range(3)]
+    weight = shares[24:32]
+    offset = shares[32:40]
+
+    def fit(i, carry):
+        here = pl.ds(pl.multiple_of(8 * i, 8), 8)
+        for b in (1, 2):
+            cols = slice(128 * b, 128 * b + 128)
+
+            def sums(f):
+                return win[pl.ds(pl.multiple_of(f * EH + 8 * i, 8), 8), cols]
+
+            kz, phase, atten = (
+                ext[pl.ds(pl.multiple_of(j * EH + 8 * i, 8), 8), cols] for j in range(3)
+            )
+            first = tuple(mom[n, here, cols] for n in range(5))
+            phase, atten, power = fit_tile(sums, weights, weight, offset, phase, atten, first)
+            spot = slice(128 * b - 128, 128 * b)
+            mid[0, here, spot] = phase / kz
+            mid[1, here, spot] = atten
+            mid[2, here, spot] = power
+        return carry
+
+    lax.fori_loop(0, 5, fit, 0)
 
 
 def around(field):
@@ -315,35 +371,32 @@
 
 def make_fit_kernel(row_count, col_count, group):
     def kernel(
-        win, ext, mom, shares, far, near,
+        win, ext, mom, shares, mid, far, near,
         depth, base, v0, v1, v2, sums,
-        hi, lo, rim, wide, conf, sem,
+        hi, lo, rim, wide, sem,
     ):
         lane = lax.broadcasted_iota(jnp.int32, (8, 128), 1)
         row = lax.axis_index("row")
         col = lax.axis_index("col")
         odd_col = lax.rem(col, 2) == 1
-        packs = {}
+        places = strips()
+        packs = []
+        for v in range(PACK // 8):
+            one = far[8 * v : 8 * v + 8]
+            two = near[8 * v : 8 * v + 8]
+            packs.append((jnp.where(odd_col, one, two), jnp.where(odd_col, two, one)))
 
         def halo_tile(strip):
-            v, g = divmod(strip, 8)
-            if v not in packs:
-                one = far[8 * v : 8 * v + 8]
-                two = near[8 * v : 8 * v + 8]
-                packs[v] = (jnp.where(odd_col, one, two), jnp.where(odd_col, two, one))
-            lo_part, hi_part = packs[v]
-            if g:
-                lo_part = pltpu.roll(lo_part, 128 - 16 * g, 1)
-            if g != 7:
-                hi_part = pltpu.roll(hi_part, 112 - 16 * g, 1)
-            return jnp.where(lane < 16, lo_part, jnp.where(lane >= 112, hi_part, 0.0))
+            v, at, width = places[strip]
+            low, high = packs[v]
+            if at:
+                low = pltpu.roll(low, 128 - at, 1)
+            high = pltpu.roll(high, 128 - at - width, 1)
+            return jnp.where(lane < width, low, jnp.where(lane >= 128 - width, high, 0.0))
 
         for n in range(6):
             halo = jnp.concatenate([halo_tile(10 * n + i) for i in range(10)], axis=0)
             hi[80 * n : 80 * n + 80], lo[80 * n : 80 * n + 80] = split(halo)
-        for j in range(3):
-            for i in range(5):
-                wide[j, 8 * i : 8 * i + 8, W:EW] = halo_tile((FIELDS + j) * 5 + i)
         for n, shift in enumerate((128, 0, -128)):
             part = band(128, 128, shift)
             rim[:, 128 * n : 128 * n + 128] = dot(hi[...], part) + dot(lo[...], part)
@@ -352,51 +405,47 @@
         weight = shares[24:32]
         offset = shares[32:40]
 
-        def fit(i, carry):
-            here = pl.ds(pl.multiple_of(8 * i, 8), 8)
-
-            def tile(f, b):
-                at = pl.ds(pl.multiple_of(f * EH + 8 * i, 8), 8)
-                value = win[at, 128 * b : 128 * b + 128]
-                if b in rim_of:
-                    value = value + rim[at, 128 * rim_of[b] : 128 * rim_of[b] + 128]
-                return value
-
-            for b in range(5):
+        def tile(f, i, b):
+            at = f * EH + 8 * i
+            value = win[at : at + 8, 128 * b : 128 * b + 128]
+            return value + rim[at : at + 8, 128 * rim_of[b] : 128 * rim_of[b] + 128]
+
+        def gathered(parts):
+            out = jnp.zeros((8, 128), jnp.float32)
+            for i, part in enumerate(parts):
+                here = (lane >= 8 * i) & (lane < 8 * i + 8)
+                out = jnp.where(here, pltpu.roll(part, 8 * i + 4, 1), out)
+            return out
+
+        def rim_sums(f):
+            return gathered([tile(f, i, 4) for i in range(5)])
+
+        kz, phase, atten = (
+            gathered([halo_tile((FIELDS + j) * 5 + i) for i in range(5)]) for j in range(3)
+        )
+        phase, _, power = fit_tile(rim_sums, weights, weight, offset, phase, atten, None)
+        phase = phase / kz
+        for i in range(5):
+            here = slice(8 * i, 8 * i + 8)
+            wide[0, here, W:EW] = pltpu.roll(phase, 124 - 8 * i, 1)
+            wide[2, here, W:EW] = pltpu.roll(power, 124 - 8 * i, 1)
+        for i in range(5):
+            here = slice(8 * i, 8 * i + 8)
+            for b in (0, 3):
                 cols = slice(128 * b, 128 * b + 128)
-                wre = wim = power = None
-                for k in range(3):
-                    scale = lax.rsqrt(tile(k, b) * tile(3 + k, b) + EPSILON)
-                    cre = tile(6 + k, b) * scale
-                    cim = tile(9 + k, b) * scale
-                    square = cre * cre + cim * cim
-                    if k:
-                        wre = wre + cre * weights[k]
-                        wim = wim + cim * weights[k]
-                        power = power + square
-                    else:
-                        wre = cre * weights[k]
-                        wim = cim * weights[k]
-                        power = square
-                conf[here, cols] = power * (1.0 / 3.0)
-                if b < 4:
-                    kz, phase, atten = (
-                        ext[pl.ds(pl.multiple_of(j * EH + 8 * i, 8), 8), cols] for j in range(3)
-                    )
-                else:
-                    kz, phase, atten = (wide[j, here, cols] for j in range(3))
-                for step in range(GAUSS_STEPS):
-                    if step or b == 4:
-                        now = moments(phase, atten)
-                    else:
-                        now = tuple(mom[n, here, cols] for n in range(5))
-                    phase, atten = gauss_step(phase, atten, now, wre, wim, weight, offset)
-                wide[2, here, cols] = atten
+                kz, phase, atten = (
+                    ext[j * EH + 8 * i : j * EH + 8 * i + 8, cols] for j in range(3)
+                )
+                first = tuple(mom[n, here, cols] for n in range(5))
+                phase, atten, power = fit_tile(
+                    lambda f: tile(f, i, b), weights, weight, offset, phase, atten, first
+                )
                 wide[0, here, cols] = phase / kz
-            return carry
-
-        lax.fori_loop(0, 5, fit, 0)
-        written = pltpu.make_async_copy(wide.at[2, pl.ds(0, H), pl.ds(0, W)], depth, sem)
+                wide[1, here, cols] = atten
+                wide[2, here, cols] = power
+        for n in range(3):
+            wide[n, :, 128:384] = mid[n]
+        written = pltpu.make_async_copy(wide.at[1, pl.ds(0, H), pl.ds(0, W)], depth, sem)
         written.start()
 
         r = lax.broadcasted_iota(jnp.int32, (EH, EW), 0)
@@ -410,7 +459,7 @@
         inside = jnp.logical_not(row_bad | col_bad)
 
         start = jnp.where(inside, wide[0], 0.0)
-        confidence = conf[...] - 0.5
+        confidence = wide[2] - 0.5
         base[...] = start[0:H, 0:W]
         first = jnp.where(inside, around(start) - 4.0 * start, 0.0)
         v0[...] = first[0:H, 0:W]
@@ -521,7 +570,12 @@
                 edges_kernel(lifts),
                 f32(SEND_ROWS, W),
                 [ANY] * 4,
-                [pltpu.SemaphoreType.DMA((FIELDS + 3,))],
+                [
+                    pltpu.VMEM((FIELDS, 8, W), jnp.float32),
+                    pltpu.VMEM((FIELDS, 8, W), jnp.float32),
+                    pltpu.VMEM((3, 8, W), jnp.float32),
+                    pltpu.SemaphoreType.DMA((5,)),
+                ],
                 name=name,
                 far=range(4),
             )(*inputs)
@@ -548,31 +602,30 @@
         )(*inputs, far, near)
         far = lax.ppermute(left, "col", swap(col_count, 1))
         near = lax.ppermute(right, "col", swap(col_count, 0))
-        win, mom = call(
+        win, mom, mid = call(
             columns_kernel,
-            (f32(FIELDS * EH, EW), f32(5, EH, W)),
-            [VM] * 3,
+            (f32(FIELDS * EH, EW), f32(5, EH, W), f32(3, EH, 256)),
+            [VM] * 4,
             [pltpu.VMEM((FIELDS * EH, W), jnp.bfloat16)] * 2,
             name="colsums",
-            kept=range(3),
-            aliases={2: 1},
+            kept=range(4),
+            aliases={3: 1},
             cost=busy,
-        )(rows, ext, mom)
+        )(rows, ext, shares, mom)
         depth, base, v0, v1, v2, sums = call(
             make_fit_kernel(row_count, col_count, near_count),
             tuple(f32(H, W) for _ in range(5)) + (f32(near_count, 128),),
-            [VM] * 6,
+            [VM] * 7,
             [pltpu.VMEM((FIELDS * EH, 128), jnp.bfloat16)] * 2
             + [
                 pltpu.VMEM((FIELDS * EH, 384), jnp.float32),
                 pltpu.VMEM((3, EH, EW), jnp.float32),
-                pltpu.VMEM((EH, EW), jnp.float32),
                 pltpu.SemaphoreType.DMA,
             ],
             name="fit",
-            kept=range(6),
+            kept=range(7),
             leaves=(0,),
-        )(win, ext, mom, shares, far, near)
+        )(win, ext, mom, shares, mid, far, near)
         parts = lax.all_to_all(
             sums.reshape(near_count, 1, 128), both, 0, 0, axis_index_groups=near_groups
         ).reshape(near_count, 128)

time: 64 us -> 62 us (0.969)
  waiting for transfers between devices: 1.59 us -> 0.25 us
  starting transfers between devices: 14.3 us -> 13.3 us
    all_to_all x1, blocking collectives: 22 us -> 23.4 us  [local(): lax.all_to_all(sums.reshape(near_count, 1, 128), both, 0, 0, axis_index_g...]
    ppermute x1, waiting for transfers between devices: 1.21 us -> 0.01 us  [local(): near = lax.ppermute(right, 'col', swap(col_count, 0))]
    ppermute x1, starting transfers between devices: 4.22 us -> 3.25 us  [local(): near = lax.ppermute(right, 'col', swap(col_count, 0))]
    all_to_all x1, blocking collectives: 15.9 us -> 15 us  [local(): lax.all_to_all(parts.reshape(far_count, 1, 128), both, 0, 0, axis_index_g...]
  transfers between devices with their start and end apart: 4 -> 4, of which waited for: 2 -> 1; matrix products, arithmetic and copies ran while one was open for 0% -> 0% of each run, Pallas kernels for 5% -> 6%
where the time goes in v4:
time: 62 us; the launch traced here: 61.6 us
  blocking collectives  38.5 us (62%)
  starting transfers between devices  13.3 us (21%)
  Pallas kernels  8.71 us (14%)
  between operations  0.79 us (1%)
    all_to_all x1, blocking collectives, local(): lax.all_to_all(sums.reshape(near_count, 1, 128), both, 0, 0, axis_index_g...  23.4 us
    all_to_all x1, blocking collectives, local(): lax.all_to_all(parts.reshape(far_count, 1, 128), both, 0, 0, axis_index_g...  15 us
    pallas_call x8, Pallas kernels, apply(): return run(*args)  8.71 us
    ppermute x1, starting transfers between devices, local(): near = lax.ppermute(edges(1, 'nearedges'), 'row', swap(row_count, 0))  4.85 us
    ppermute x1, starting transfers between devices, local(): far = lax.ppermute(edges(0, 'faredges'), 'row', swap(row_count, 1))  4.58 us
    ppermute x1, starting transfers between devices, local(): near = lax.ppermute(right, 'col', swap(col_count, 0))  3.25 us
  transfers between devices with their start and end apart: 4, of which 1 were waited for; matrix products, arithmetic and copies ran while one was open for 0% of the time, Pallas kernels for 6%

profile of v4, /device:TPU:1, one launch (start us, length us, event | category | flops | bytes accessed | tf_op | source)
XLA Modules:
  0.0 61.6 jit_solution(4689796969511412530)
XLA Ops:
  0.6 0.0 copy-start.1
  0.6 0.0 copy-start.2
  0.7 0.0 copy-start.4
  0.7 0.0 copy-start
  0.7 0.0 copy-start.3
  0.7 1.2 %faredges.1 = f32[168,512]{1,0:T(8,128)S(1)} custom-call(f32[12,32,512]{2,1,0:T(8,128)} %bitcast.9, f32[32,512]{1,0:T(8,128)} %vw.5, f32[32,512]{1,0:T(8,128)} %ip.7, f32[32,512]{1,0:T(8,128)} %ie.7), custom_call_target="tpu_custom_call" | custom-call | tf_op jit(solution)/shard_map/faredges/pallas_call | solution.py:67
  1.9 4.6 %collective-permute-start = (f32[168,512]{1,0:T(8,128)S(1)}, f32[168,512]{1,0:T(8,128)S(1)}, u32[]{:S(2)}, u32[]{:S(2)}) collective-permute-start(f32[168,512]{1,0:T(8,128)S(1)} %faredges.1), channel_id=1, source_target_pairs={{32,64},{96,128},{160,192},{224,256},{288,320},{352,384},{416,448}... | collective-permute-start | bytes 1032200 | tf_op jit(solution)/shard_map/ppermute | solution.py:584
  6.5 1.1 %nearedges.1 = f32[168,512]{1,0:T(8,128)S(1)} custom-call(f32[12,32,512]{2,1,0:T(8,128)} %bitcast.10, f32[32,512]{1,0:T(8,128)} %vw.5, f32[32,512]{1,0:T(8,128)} %ip.7, f32[32,512]{1,0:T(8,128)} %ie.7), custom_call_target="tpu_custom_call" | custom-call | tf_op jit(solution)/shard_map/nearedges/pallas_call | solution.py:67
  7.7 4.8 %collective-permute-start.1 = (f32[168,512]{1,0:T(8,128)S(1)}, f32[168,512]{1,0:T(8,128)S(1)}, u32[]{:S(2)}, u32[]{:S(2)}) collective-permute-start(f32[168,512]{1,0:T(8,128)S(1)} %nearedges.1), channel_id=1, source_target_pairs={{0,32},{64,96},{128,160},{192,224},{256,288},{320,352},{384,416},{... | collective-permute-start | bytes 1032200 | tf_op jit(solution)/shard_map/ppermute | solution.py:585
  12.5 0.0 copy-done.1
  12.5 0.0 copy-done.2
  12.5 0.0 copy-done.4
  12.5 1.0 %early.1 = (f32[5,40,512]{2,1,0:T(8,128)S(1)}, f32[40,128]{1,0:T(8,128)S(1)}) custom-call(f32[3]{0:T(128)S(1)} %copy-done.4, f32[32,512]{1,0:T(8,128)S(1)} %copy-done.1, f32[32,512]{1,0:T(8,128)S(1)} %copy-done.2), custom_call_target="tpu_custom_call" | custom-call | flops 6000000 | tf_op jit(solution)/shard_map/early/pallas_call | solution.py:67
  13.5 0.0 collective-permute-done.far
  13.5 0.2 collective-permute-done.1.near
  13.8 0.0 copy-done
  13.8 0.0 copy-done.3
  13.8 1.1 %rowsums.1 = (f32[480,512]{1,0:T(8,128)S(1)}, f32[120,512]{1,0:T(8,128)S(1)}, f32[64,128]{1,0:T(8,128)S(1)}, f32[64,128]{1,0:T(8,128)S(1)}) custom-call(f32[12,32,512]{2,1,0:T(8,128)S(1)} %bitcast.11, f32[32,512]{1,0:T(8,128)S(1)} %copy-done.3, f32[32,512]{1,0:T(8,128)S(1)} %copy-done.1, f32[32,512]{1,0:T(8,128)S(1)} %copy-done.2, ...), custom_call_target="tpu_custom_call" | custom-call | tf_op jit(solution)/shard_map/rowsums/pallas_call | solution.py:67
  14.9 0.7 %collective-permute-start.2 = (f32[64,128]{1,0:T(8,128)S(1)}, f32[64,128]{1,0:T(8,128)S(1)}, u32[]{:S(2)}, u32[]{:S(2)}) collective-permute-start(f32[64,128]{1,0:T(8,128)S(1)} %get-tuple-element.32), channel_id=1, source_target_pairs={{1,2},{3,4},{5,6},{7,8},{9,10},{11,12},{13,14},{15,16},{17,18},{19... | collective-permute-start | bytes 98312 | tf_op jit(solution)/shard_map/ppermute | solution.py:603
  15.6 3.3 %collective-permute-start.3 = (f32[64,128]{1,0:T(8,128)S(1)}, f32[64,128]{1,0:T(8,128)S(1)}, u32[]{:S(2)}, u32[]{:S(2)}) collective-permute-start(f32[64,128]{1,0:T(8,128)S(1)} %get-tuple-element.33), channel_id=1, source_target_pairs={{0,1},{2,3},{4,5},{6,7},{8,9},{10,11},{12,13},{14,15},{16,17},{18,... | collective-permute-start | bytes 98312 | tf_op jit(solution)/shard_map/ppermute | solution.py:604
  18.8 1.4 %colsums.1 = (f32[480,640]{1,0:T(8,128)S(1)}, f32[5,40,512]{2,1,0:T(8,128)S(1)}, f32[3,40,256]{2,1,0:T(8,128)S(1)}) custom-call(f32[480,512]{1,0:T(8,128)S(1)} %get-tuple-element.25.rows, f32[120,512]{1,0:T(8,128)S(1)} %get-tuple-element.26.ext, f32[40,128]{1,0:T(8,128)S(1)} %get-tuple-element.27.shares, ...), custom_call_target="tpu_custom_call", output_to_operand_aliasing={{1}: (3, {})} | custom-call | flops 6000000 | tf_op jit(solution)/shard_map/colsums/pallas_call | solution.py:67
  20.2 0.0 collective-permute-done.2.far
  20.2 0.0 collective-permute-done.3.near
  20.2 2.1 %fit.1 = (f32[32,512]{1,0:T(8,128)}, f32[32,512]{1,0:T(8,128)S(1)}, f32[32,512]{1,0:T(8,128)S(1)}, f32[32,512]{1,0:T(8,128)S(1)}, f32[32,512]{1,0:T(8,128)S(1)}, /*index=5*/f32[64,128]{1,0:T(8,128)S(1)}) custom-call(f32[480,640]{1,0:T(8,128)S(1)} %get-tuple-element.29.win, f32[120,512]{1,0:T(8,128)S(1)} %get-tuple-element.26.ext, ...), custom_call_target="tpu_custom_call" | custom-call | tf_op jit(solution)/shard_map/fit/pallas_call | solution.py:67
  22.3 23.4 %all_to_all.10 = f32[64,1,128]{2,1,0:T(1,128)S(1)} all-to-all(f32[64,1,128]{2,1,0:T(1,128)S(1)} %bitcast.13), channel_id=1, replica_groups={{0,1,2,3,4,5,6,7,8,9,10,11,12,13,14,15,16,17,18,19,20,21,22,23,24,25,26..., dimensions={0} | all-to-all | bytes 65536 | tf_op jit(solution)/shard_map/all_to_all | solution.py:629
  45.8 15.0 %all_to_all.11 = f32[8,1,128]{2,1,0:T(1,128)S(1)} all-to-all(f32[8,1,128]{2,1,0:T(1,128)S(1)} %bitcast.14), channel_id=1, replica_groups={{0,64,128,192,256,320,384,448},{1,65,129,193,257,321,385,449},{2,66,130..., dimensions={0} | all-to-all | bytes 8192 | tf_op jit(solution)/shard_map/all_to_all | solution.py:633
  60.8 0.8 %final.1 = f32[32,512]{1,0:T(8,128)} custom-call(f32[8,128]{1,0:T(8,128)S(1)} %bitcast.15, f32[32,512]{1,0:T(8,128)S(1)} %get-tuple-element.35.base, f32[32,512]{1,0:T(8,128)S(1)} %get-tuple-element.36.v0, f32[32,512]{1,0:T(8,128)S(1)} %get-tuple-element.37.v1, f32[32,512]{1,0:T(8,128)S(1)} %get-tuple-element.38.v2), custom_call_target="tpu_custom_call" | custom-call | tf_op jit(solution)/shard_map/final/pallas_call | solution.py:67
  (1 shorter events, 0.0 us)
Async XLA Ops:
  0.6 11.9 %copy-start.1 = (f32[32,512]{1,0:T(8,128)S(1)}, f32[32,512]{1,0:T(8,128)}, u32[]{:S(2)}) copy-start(f32[32,512]{1,0:T(8,128)} %ip.7) | copy-start | bytes 196612
  0.6 11.9 %copy-start.2 = (f32[32,512]{1,0:T(8,128)S(1)}, f32[32,512]{1,0:T(8,128)}, u32[]{:S(2)}) copy-start(f32[32,512]{1,0:T(8,128)} %ie.7) | copy-start | bytes 196612
  0.7 11.9 %copy-start.4 = (f32[3]{0:T(128)S(1)}, f32[3]{0:T(128)}, u32[]{:S(2)}) copy-start(f32[3]{0:T(128)} %ground.1) | copy-start | bytes 40
  0.7 13.1 %copy-start = (f32[2,2,3,32,512]{4,3,2,1,0:T(8,128)S(1)}, f32[2,2,3,32,512]{4,3,2,1,0:T(8,128)}, u32[]{:S(2)}) copy-start(f32[2,2,3,32,512]{4,3,2,1,0:T(8,128)} %param.5) | copy-start | bytes 2359300
  0.7 13.1 %copy-start.3 = (f32[32,512]{1,0:T(8,128)S(1)}, f32[32,512]{1,0:T(8,128)}, u32[]{:S(2)}) copy-start(f32[32,512]{1,0:T(8,128)} %vw.5) | copy-start | bytes 196612
  1.9 11.6 %collective-permute-start = (f32[168,512]{1,0:T(8,128)S(1)}, f32[168,512]{1,0:T(8,128)S(1)}, u32[]{:S(2)}, u32[]{:S(2)}) collective-permute-start(f32[168,512]{1,0:T(8,128)S(1)} %faredges.1), channel_id=1, source_target_pairs={{32,64},{96,128},{160,192},{224,256},{288,320},{352,384},{416,448}... | collective-permute-start | bytes 1032200 | tf_op jit(solution)/shard_map/ppermute | solution.py:584
  7.7 6.1 %collective-permute-start.1 = (f32[168,512]{1,0:T(8,128)S(1)}, f32[168,512]{1,0:T(8,128)S(1)}, u32[]{:S(2)}, u32[]{:S(2)}) collective-permute-start(f32[168,512]{1,0:T(8,128)S(1)} %nearedges.1), channel_id=1, source_target_pairs={{0,32},{64,96},{128,160},{192,224},{256,288},{320,352},{384,416},{... | collective-permute-start | bytes 1032200 | tf_op jit(solution)/shard_map/ppermute | solution.py:585
  14.9 5.3 %collective-permute-start.2 = (f32[64,128]{1,0:T(8,128)S(1)}, f32[64,128]{1,0:T(8,128)S(1)}, u32[]{:S(2)}, u32[]{:S(2)}) collective-permute-start(f32[64,128]{1,0:T(8,128)S(1)} %get-tuple-element.32), channel_id=1, source_target_pairs={{1,2},{3,4},{5,6},{7,8},{9,10},{11,12},{13,14},{15,16},{17,18},{19... | collective-permute-start | bytes 98312 | tf_op jit(solution)/shard_map/ppermute | solution.py:603
  15.6 4.7 %collective-permute-start.3 = (f32[64,128]{1,0:T(8,128)S(1)}, f32[64,128]{1,0:T(8,128)S(1)}, u32[]{:S(2)}, u32[]{:S(2)}) collective-permute-start(f32[64,128]{1,0:T(8,128)S(1)} %get-tuple-element.33), channel_id=1, source_target_pairs={{0,1},{2,3},{4,5},{6,7},{8,9},{10,11},{12,13},{14,15},{16,17},{18,... | collective-permute-start | bytes 98312 | tf_op jit(solution)/shard_map/ppermute | solution.py:604

commit v5 on v4

--- a/solution.py
+++ b/solution.py
@@ -69,31 +69,42 @@
     return apply
 
 
-def edges_kernel(lifts):
-    def kernel(sv, vw, ip, ie, out, tiles, rest, extra, sems):
-        low = lax.rem(lax.axis_index("row") + lifts, 2)
-        edge = pl.ds(pl.multiple_of(24 * low, 8), 8)
-        inner = pl.ds(pl.multiple_of(8 + 8 * low, 8), 8)
-        started = [
-            pltpu.make_async_copy(sv.at[:, inner], rest, sems.at[0]),
-            pltpu.make_async_copy(sv.at[:, edge], tiles, sems.at[1]),
-        ]
-        for j, ref in enumerate((vw, ip, ie)):
-            started.append(pltpu.make_async_copy(ref.at[edge], extra.at[j], sems.at[2 + j]))
-        for copy in started:
-            copy.start()
-        for copy in started:
-            copy.wait()
-        bottom = low == 1
-        for f in range(FIELDS):
-            out[8 * f : 8 * f + 8] = tiles[f]
-            at = REST_AT + REST * f
-            out[at : at + REST] = jnp.where(bottom, rest[f, 8 - REST : 8], rest[f, 0:REST])
-        for j in range(3):
-            at = EXTRA_AT + 4 * j
-            out[at : at + 4] = jnp.where(bottom, extra[j, 4:8], extra[j, 0:4])
-
-    return kernel
+def pack_edges(low, out, tiles, rest, extra):
+    bottom = low == 1
+    for f in range(FIELDS):
+        out[8 * f : 8 * f + 8] = tiles(f)
+        at = REST_AT + REST * f
+        value = rest(f)
+        out[at : at + REST] = jnp.where(bottom, value[8 - REST : 8], value[0:REST])
+    for j in range(3):
+        at = EXTRA_AT + 4 * j
+        value = extra(j)
+        out[at : at + 4] = jnp.where(bottom, value[4:8], value[0:4])
+
+
+def far_edges_kernel(sv, vw, ip, ie, out, tiles, rest, extra, sems):
+    low = lax.rem(lax.axis_index("row"), 2)
+    edge = pl.ds(pl.multiple_of(24 * low, 8), 8)
+    inner = pl.ds(pl.multiple_of(8 + 8 * low, 8), 8)
+    started = [
+        pltpu.make_async_copy(sv.at[:, inner], rest, sems.at[0]),
+        pltpu.make_async_copy(sv.at[:, edge], tiles, sems.at[1]),
+    ]
+    for j, ref in enumerate((vw, ip, ie)):
+        started.append(pltpu.make_async_copy(ref.at[edge], extra.at[j], sems.at[2 + j]))
+    for copy in started:
+        copy.start()
+    for copy in started:
+        copy.wait()
+    pack_edges(low, out, lambda f: tiles[f], lambda f: rest[f], lambda j: extra[j])
+
+
+def near_edges_kernel(sv, vw, ip, ie, out):
+    low = 1 - lax.rem(lax.axis_index("row"), 2)
+    edge = pl.ds(pl.multiple_of(24 * low, 8), 8)
+    inner = pl.ds(pl.multiple_of(8 + 8 * low, 8), 8)
+    fields = (vw, ip, ie)
+    pack_edges(low, out, lambda f: sv[f, edge], lambda f: sv[f, inner], lambda j: fields[j][edge])
 
 
 def strips():
@@ -105,37 +116,26 @@
     return out
 
 
-def rows_kernel(sv, vw, ip, ie, far, near, rows, ext, far_pack, near_pack, px, s4):
+def products(re1, im1, re2, im2):
+    return (
+        re1 * re1 + im1 * im1,
+        re2 * re2 + im2 * im2,
+        re1 * re2 + im1 * im2,
+        re1 * im2 - im1 * re2,
+    )
+
+
+def own_rows_kernel(sv, rows, px, s4):
     sub = lax.broadcasted_iota(jnp.int32, (8, 128), 0)
-    lane = lax.broadcasted_iota(jnp.int32, (8, 128), 1)
-    odd_row = lax.rem(lax.axis_index("row"), 2) == 1
-    odd_col = lax.rem(lax.axis_index("col"), 2) == 1
-
-    def sides(at, size, cols):
-        one = far[at : at + size, cols]
-        two = near[at : at + size, cols]
-        return jnp.where(odd_row, two, one), jnp.where(odd_row, one, two)
-
+    for j in range(4):
+        px[j, 0:24] = jnp.zeros((24, 128), jnp.float32)
+        px[j, 24 + H : 88] = jnp.zeros((64 - H, 128), jnp.float32)
     for k in range(3):
 
         def block(b, carry, k=k):
             cols = pl.ds(pl.multiple_of(b * 128, 128), 128)
-
-            def parts(q):
-                f = q * 3 + k
-                above, below = sides(8 * f, 8, cols)
-                above_rest, below_rest = sides(REST_AT + REST * f, REST, cols)
-                return above_rest, above, sv[f, :, cols], below, below_rest
-
-            quads = [parts(q) for q in range(4)]
-            at = 24 - SIDE
-            for p, size in enumerate((REST, 8, H, 8, REST)):
-                re1, im1, re2, im2 = (quad[p] for quad in quads)
-                px[0, at : at + size] = re1 * re1 + im1 * im1
-                px[1, at : at + size] = re2 * re2 + im2 * im2
-                px[2, at : at + size] = re1 * re2 + im1 * im2
-                px[3, at : at + size] = re1 * im2 - im1 * re2
-                at += size
+            for j, value in enumerate(products(*(sv[q * 3 + k, :, cols] for q in range(4)))):
+                px[j, 24 : 24 + H] = value
             for j in range(4):
                 two = px[j, 7:79] + px[j, 8:80]
                 four = two[0:64] + (px[j, 9:73] + px[j, 10:74])
@@ -149,19 +149,97 @@
             return carry
 
         lax.fori_loop(0, 4, block, 0)
+
+
+HALO_SCRATCH = [pltpu.VMEM((4, 32, 128), jnp.float32)] * 4 + [pltpu.VMEM((4, 56, 128), jnp.float32)]
+
+
+def halo_rows(far, near, blocks, scratch, put):
+    odd_row = lax.rem(lax.axis_index("row"), 2) == 1
+    sub = lax.broadcasted_iota(jnp.int32, (8, 128), 0)
+    xa, xb, ta, tb, out = scratch
+    zeros = jnp.zeros((16, 128), jnp.float32)
+    for j in range(4):
+        xa[j, 8:24] = zeros
+        xa[j, 16:32] = zeros
+        xb[j, 0:16] = zeros
+        xb[j, 16:32] = zeros
+        ta[j, 16:32] = zeros
+        tb[j, 0:16] = zeros
+        out[j, 0:16] = zeros
+        out[j, 16:32] = zeros
+        out[j, 24:40] = zeros
+
+    def sides(at, size, cols):
+        one = far[at : at + size, cols]
+        two = near[at : at + size, cols]
+        return jnp.where(odd_row, two, one), jnp.where(odd_row, one, two)
+
+    for b in blocks:
+        cols = slice(128 * b, 128 * b + 128)
+        for k in range(3):
+            tiles = [sides(8 * (q * 3 + k), 8, cols) for q in range(4)]
+            rests = [sides(REST_AT + REST * (q * 3 + k), REST, cols) for q in range(4)]
+            for j, value in enumerate(products(*(x[0] for x in rests))):
+                xa[j, 0:REST] = value
+            for j, value in enumerate(products(*(x[0] for x in tiles))):
+                xa[j, REST:SIDE] = value
+            for j, value in enumerate(products(*(x[1] for x in tiles))):
+                xb[j, 16:24] = value
+            for j, value in enumerate(products(*(x[1] for x in rests))):
+                xb[j, 24 : 24 + REST] = value
+            for j in range(4):
+                four = (xa[j, 0:16] + xa[j, 1:17]) + (xa[j, 2:18] + xa[j, 3:19])
+                ta[j, 0:16] = four
+                total = (four + ta[j, 4:20]) + (ta[j, 8:24] + ta[j, 12:28])
+                out[j, 8:24] = total
+                four = (xb[j, 16:32] + xb[j, 15:31]) + (xb[j, 14:30] + xb[j, 13:29])
+                tb[j, 16:32] = four
+                total = (four + tb[j, 12:28]) + (tb[j, 8:24] + tb[j, 4:20])
+                out[j, 39:55] = total
+                put(
+                    j * 3 + k,
+                    b,
+                    (
+                        out[j, 12:20],
+                        out[j, 20:28],
+                        out[j, 32:40],
+                        out[j, 40:48],
+                        jnp.where(sub < 4, out[j, 48:56], out[j, 4:12]),
+                    ),
+                )
+
+
+def sides_kernel(sums, vw, ip, ie, far, near, outer, ext, far_pack, near_pack, *scratch):
+    lane = lax.broadcasted_iota(jnp.int32, (8, 128), 1)
+    odd_row = lax.rem(lax.axis_index("row"), 2) == 1
+    odd_col = lax.rem(lax.axis_index("col"), 2) == 1
+
+    def put(f, b, parts):
+        for i, part in enumerate(parts):
+            at = f * EH + 8 * i
+            spot = slice(0, 128) if b == 0 else slice(128, 256)
+            outer[at : at + 8, spot] = sums[at : at + 8, 128 * b : 128 * b + 128] + part
+
+    halo_rows(far, near, (0, 3), scratch, put)
     for j, ref in enumerate((vw, ip, ie)):
+        at = EXTRA_AT + 4 * j
+        one = far[at : at + 4]
+        two = near[at : at + 4]
         ext[j * EH : j * EH + H] = ref[...]
-        above, below = sides(EXTRA_AT + 4 * j, 4, slice(0, W))
-        ext[j * EH + H : j * EH + H + 4] = below
-        ext[j * EH + H + 4 : j * EH + EH] = above
+        ext[j * EH + H : j * EH + H + 4] = jnp.where(odd_row, one, two)
+        ext[j * EH + H + 4 : j * EH + EH] = jnp.where(odd_row, two, one)
     low = [jnp.zeros((8, 128), jnp.float32)] * (PACK // 8)
     high = list(low)
     for n, (v, at, width) in enumerate(strips()):
         here = (lane >= at) & (lane < at + width)
-        ref = rows if n < FIELDS * 5 else ext
-        top = 8 * n if n < FIELDS * 5 else 8 * n - FIELDS * EH
-        first = ref[top : top + 8, 0:128]
-        last = ref[top : top + 8, W - 128 : W]
+        if n < FIELDS * 5:
+            first = outer[8 * n : 8 * n + 8, 0:128]
+            last = outer[8 * n : 8 * n + 8, 128:256]
+        else:
+            top = 8 * n - FIELDS * EH
+            first = ext[top : top + 8, 0:128]
+            last = ext[top : top + 8, W - 128 : W]
         if at:
             first = pltpu.roll(first, at, 1)
         last = pltpu.roll(last, at + width, 1)
@@ -312,14 +390,24 @@
     return jnp.dot(a, b, preferred_element_type=jnp.float32)
 
 
-def columns_kernel(rows, ext, shares, held, win, mom, mid, hi, lo):
+def columns_kernel(rows, outer, far, near, ext, shares, held, win, mom, mid, hi, lo, sums, *scratch):
     if INTERPRET:
         mom[:, 0:H] = held[:, 0:H]
+
+    def put(f, b, parts):
+        for i, part in enumerate(parts):
+            at = f * EH + 8 * i
+            spot = slice(128 * b - 128, 128 * b)
+            sums[at : at + 8, spot] = rows[at : at + 8, 128 * b : 128 * b + 128] + part
+
+    halo_rows(far, near, (1, 2), scratch, put)
     for n in range(6):
         here = slice(80 * n, 80 * n + 80)
-        for b in range(4):
-            cols = slice(128 * b, 128 * b + 128)
-            hi[here, cols], lo[here, cols] = split(rows[here, cols])
+        hi[here, 0:128], lo[here, 0:128] = split(outer[here, 0:128])
+        hi[here, 384:512], lo[here, 384:512] = split(outer[here, 128:256])
+        for b in range(2):
+            cols = slice(128 * b + 128, 128 * b + 256)
+            hi[here, cols], lo[here, cols] = split(sums[here, 128 * b : 128 * b + 128])
     left = band(384, 256, 0)
     right = band(384, 256, 128)
     win[:, 0:256] = dot(hi[:, 0:384], left) + dot(lo[:, 0:384], left)
@@ -373,7 +461,7 @@
     def kernel(
         win, ext, mom, shares, mid, far, near,
         depth, base, v0, v1, v2, sums,
-        hi, lo, rim, wide, sem,
+        hi, lo, rim, wide,
     ):
         lane = lax.broadcasted_iota(jnp.int32, (8, 128), 1)
         row = lax.axis_index("row")
@@ -445,8 +533,7 @@
                 wide[2, here, cols] = power
         for n in range(3):
             wide[n, :, 128:384] = mid[n]
-        written = pltpu.make_async_copy(wide.at[1, pl.ds(0, H), pl.ds(0, W)], depth, sem)
-        written.start()
+        depth[...] = wide[1, 0:H, 0:W]
 
         r = lax.broadcasted_iota(jnp.int32, (EH, EW), 0)
         c = lax.broadcasted_iota(jnp.int32, (EH, EW), 1)
@@ -480,7 +567,6 @@
             total = jnp.sum(jnp.sum(product, axis=0, keepdims=True), axis=1, keepdims=True)
             line = jnp.where(spots == n, total, line)
         sums[...] = jnp.broadcast_to(line, (group, 128))
-        written.wait()
 
     return kernel
 
@@ -501,7 +587,9 @@
     return total
 
 
-def final_kernel(parts, base, v0, v1, v2, heights):
+def final_kernel(parts, base, v0, v1, v2, fitted, heights, depth, result, sems):
+    first = pltpu.make_async_copy(fitted, depth, sems.at[0])
+    first.start()
     line = jnp.sum(parts[...], axis=0, keepdims=True)
     spots = lax.broadcasted_iota(jnp.int32, (1, 128), 1)
     b = [
@@ -537,24 +625,33 @@
             for n, x in enumerate(residual)
         ]
         now = after
-    heights[...] = base[...] + (answer[0] * v0[...] + (answer[1] * v1[...] + answer[2] * v2[...]))
+    result[...] = base[...] + (answer[0] * v0[...] + (answer[1] * v1[...] + answer[2] * v2[...]))
+    second = pltpu.make_async_copy(result, heights, sems.at[1])
+    second.start()
+    first.wait()
+    second.wait()
 
 
 def solution(mesh):
     row_count = mesh.shape["row"]
     col_count = mesh.shape["col"]
-    near_count = 2 * col_count
-    far_count = row_count // 2
 
     def index(r, c):
         return r * col_count + c
 
+    ring = max(col_count // 8, 1)
     near_groups = [
-        [index(2 * y + core, c) for core in range(2) for c in range(col_count)] for y in range(far_count)
+        [index(2 * y + core, x + ring * z) for core in range(2) for z in range(col_count // ring)]
+        for y in range(row_count // 2)
+        for x in range(ring)
     ]
     far_groups = [
-        [index(2 * y + core, c) for y in range(far_count)] for core in range(2) for c in range(col_count)
+        [index(2 * y + core, x + ring * z) for y in range(row_count // 2) for x in range(ring)]
+        for core in range(2)
+        for z in range(col_count // ring)
     ]
+    near_count = len(near_groups[0])
+    far_count = len(far_groups[0])
     both = ("row", "col")
 
     def swap(count, start):
@@ -565,24 +662,19 @@
         sv = scatter_vectors.reshape(FIELDS, H, W)
         inputs = (sv, wavenumber, phase, extinction)
 
-        def edges(lifts, name):
-            return call(
-                edges_kernel(lifts),
-                f32(SEND_ROWS, W),
-                [ANY] * 4,
-                [
-                    pltpu.VMEM((FIELDS, 8, W), jnp.float32),
-                    pltpu.VMEM((FIELDS, 8, W), jnp.float32),
-                    pltpu.VMEM((3, 8, W), jnp.float32),
-                    pltpu.SemaphoreType.DMA((5,)),
-                ],
-                name=name,
-                far=range(4),
-            )(*inputs)
-
+        tile = pltpu.VMEM((FIELDS, 8, W), jnp.float32)
+        edge = call(
+            far_edges_kernel,
+            f32(SEND_ROWS, W),
+            [ANY] * 4,
+            [tile, tile, pltpu.VMEM((3, 8, W), jnp.float32), pltpu.SemaphoreType.DMA((5,))],
+            name="faredges",
+            far=range(4),
+        )(*inputs)
         busy = pl.CostEstimate(flops=6000000, transcendentals=0, bytes_accessed=0)
-        far = lax.ppermute(edges(0, "faredges"), "row", swap(row_count, 1))
-        near = lax.ppermute(edges(1, "nearedges"), "row", swap(row_count, 0))
+        far = lax.ppermute(edge, "row", swap(row_count, 1))
+        edge = call(near_edges_kernel, f32(SEND_ROWS, W), [VM] * 4, name="nearedges", kept=range(4))(*inputs)
+        near = lax.ppermute(edge, "row", swap(row_count, 0))
         mom, shares = call(
             early_kernel,
             (f32(5, EH, W), f32(40, 128)),
@@ -591,27 +683,38 @@
             kept=(1, 2),
             cost=busy,
         )(ground_ratio, phase, extinction)
-        far, near, mom, shares = lax.optimization_barrier((far, near, mom, shares))
-        rows, ext, left, right = call(
-            rows_kernel,
-            (f32(FIELDS * EH, W), f32(3 * EH, W), f32(PACK, 128), f32(PACK, 128)),
+        rows = call(
+            own_rows_kernel,
+            f32(FIELDS * EH, W),
+            [VM],
+            [pltpu.VMEM((4, 88, 128), jnp.float32), pltpu.VMEM((4, 64, 128), jnp.float32)],
+            name="ownrows",
+            kept=(0,),
+            cost=busy,
+        )(sv)
+        far, near, mom, shares, rows = lax.optimization_barrier((far, near, mom, shares, rows))
+        outer, ext, left, right = call(
+            sides_kernel,
+            (f32(FIELDS * EH, 256), f32(3 * EH, W), f32(PACK, 128), f32(PACK, 128)),
             [VM] * 6,
-            [pltpu.VMEM((4, 88, 128), jnp.float32), pltpu.VMEM((4, 64, 128), jnp.float32)],
-            name="rowsums",
+            HALO_SCRATCH,
+            name="sides",
             kept=range(6),
-        )(*inputs, far, near)
-        far = lax.ppermute(left, "col", swap(col_count, 1))
-        near = lax.ppermute(right, "col", swap(col_count, 0))
+        )(rows, wavenumber, phase, extinction, far, near)
+        far_side = lax.ppermute(left, "col", swap(col_count, 1))
+        near_side = lax.ppermute(right, "col", swap(col_count, 0))
         win, mom, mid = call(
             columns_kernel,
             (f32(FIELDS * EH, EW), f32(5, EH, W), f32(3, EH, 256)),
-            [VM] * 4,
-            [pltpu.VMEM((FIELDS * EH, W), jnp.bfloat16)] * 2,
+            [VM] * 7,
+            [pltpu.VMEM((FIELDS * EH, W), jnp.bfloat16)] * 2
+            + [pltpu.VMEM((FIELDS * EH, 256), jnp.float32)]
+            + HALO_SCRATCH,
             name="colsums",
-            kept=range(4),
-            aliases={3: 1},
+            kept=range(7),
+            aliases={6: 1},
             cost=busy,
-        )(rows, ext, shares, mom)
+        )(rows, outer, far, near, ext, shares, mom)
         depth, base, v0, v1, v2, sums = call(
             make_fit_kernel(row_count, col_count, near_count),
             tuple(f32(H, W) for _ in range(5)) + (f32(near_count, 128),),
@@ -620,12 +723,10 @@
             + [
                 pltpu.VMEM((FIELDS * EH, 384), jnp.float32),
                 pltpu.VMEM((3, EH, EW), jnp.float32),
-                pltpu.SemaphoreType.DMA,
             ],
             name="fit",
             kept=range(7),
-            leaves=(0,),
-        )(win, ext, mom, shares, mid, far, near)
+        )(win, ext, mom, shares, mid, far_side, near_side)
         parts = lax.all_to_all(
             sums.reshape(near_count, 1, 128), both, 0, 0, axis_index_groups=near_groups
         ).reshape(near_count, 128)
@@ -633,8 +734,15 @@
         parts = lax.all_to_all(
             parts.reshape(far_count, 1, 128), both, 0, 0, axis_index_groups=far_groups
         ).reshape(far_count, 128)
-        heights = call(final_kernel, f32(H, W), [VM] * 5, name="final", kept=range(5), plain=(0,))(parts, base, v0, v1, v2)
-        return heights, depth
+        return call(
+            final_kernel,
+            (f32(H, W), f32(H, W)),
+            [VM] * 6,
+            [pltpu.VMEM((H, W), jnp.float32), pltpu.SemaphoreType.DMA((2,))],
+            name="final",
+            kept=range(6),
+            leaves=(0, 1),
+        )(parts, base, v0, v1, v2, depth)
 
     placed = (P(None, None, None, "row", "col"), P(), P("row", "col"), P("row", "col"), P("row", "col"))
     return jax.shard_map(

time: 62 us -> 60.4 us (0.974)
  Pallas kernels: 8.71 us -> 7.59 us
  blocking collectives: 38.5 us -> 37.6 us
    all_to_all x1, blocking collectives: 23.4 us -> 19.1 us  [local(): lax.all_to_all(sums.reshape(near_count, 1, 128), both, 0, 0, axis_index_g...]
    all_to_all x1, blocking collectives: 15 us -> 18.6 us  [local(): lax.all_to_all(parts.reshape(far_count, 1, 128), both, 0, 0, axis_index_g...]
    pallas_call x8 -> x9, Pallas kernels: 8.71 us -> 7.59 us  [apply(): return run(*args)]
where the time goes in v5:
time: 60.4 us; the launch traced here: 60.1 us
  blocking collectives  37.6 us (62%)
  starting transfers between devices  13.9 us (23%)
  Pallas kernels  7.59 us (13%)
  between operations  0.81 us (1%)
    all_to_all x1, blocking collectives, local(): lax.all_to_all(sums.reshape(near_count, 1, 128), both, 0, 0, axis_index_g...  19.1 us
    all_to_all x1, blocking collectives, local(): lax.all_to_all(parts.reshape(far_count, 1, 128), both, 0, 0, axis_index_g...  18.6 us
    pallas_call x9, Pallas kernels, apply(): return run(*args)  7.59 us
    ppermute x1, starting transfers between devices, local(): near = lax.ppermute(edge, 'row', swap(row_count, 0))  4.85 us
    ppermute x1, starting transfers between devices, local(): far = lax.ppermute(edge, 'row', swap(row_count, 1))  4.58 us
    ppermute x1, starting transfers between devices, local(): near_side = lax.ppermute(right, 'col', swap(col_count, 0))  3.79 us
  transfers between devices with their start and end apart: 4, of which 1 were waited for; matrix products, arithmetic and copies ran while one was open for 0% of the time, Pallas kernels for 6%

profile of v5, /device:TPU:1, one launch (start us, length us, event | category | flops | bytes accessed | tf_op | source)
XLA Modules:
  0.0 60.1 jit_solution(10249647701784877825)
XLA Ops:
  0.6 0.0 copy-start.2
  0.6 0.0 copy-start.1
  0.7 0.0 copy-start.3
  0.7 0.0 copy-start
  0.7 1.2 %faredges.1 = f32[168,512]{1,0:T(8,128)S(1)} custom-call(f32[12,32,512]{2,1,0:T(8,128)} %bitcast.9, f32[32,512]{1,0:T(8,128)} %vw.5, f32[32,512]{1,0:T(8,128)} %ip.7, f32[32,512]{1,0:T(8,128)} %ie.7), custom_call_target="tpu_custom_call" | custom-call | tf_op jit(solution)/shard_map/faredges/pallas_call | solution.py:67
  1.9 0.0 copy-start.4
  1.9 4.6 %collective-permute-start = (f32[168,512]{1,0:T(8,128)S(1)}, f32[168,512]{1,0:T(8,128)S(1)}, u32[]{:S(2)}, u32[]{:S(2)}) collective-permute-start(f32[168,512]{1,0:T(8,128)S(1)} %faredges.1), channel_id=1, source_target_pairs={{32,64},{96,128},{160,192},{224,256},{288,320},{352,384},{416,448}... | collective-permute-start | bytes 1032200 | tf_op jit(solution)/shard_map/ppermute | solution.py:675
  6.5 0.0 copy-done.2
  6.5 0.0 copy-done.1
  6.5 0.0 copy-done.3
  6.5 0.0 copy-done
  6.5 0.1 nearedges.1
  6.6 4.8 %collective-permute-start.1 = (f32[168,512]{1,0:T(8,128)S(1)}, f32[168,512]{1,0:T(8,128)S(1)}, u32[]{:S(2)}, u32[]{:S(2)}) collective-permute-start(f32[168,512]{1,0:T(8,128)S(1)} %nearedges.1), channel_id=1, source_target_pairs={{0,32},{64,96},{128,160},{192,224},{256,288},{320,352},{384,416},{... | collective-permute-start | bytes 1032200 | tf_op jit(solution)/shard_map/ppermute | solution.py:677
  11.4 0.7 %ownrows.1.sums.rows = f32[480,512]{1,0:T(8,128)S(1)} custom-call(f32[12,32,512]{2,1,0:T(8,128)S(1)} %bitcast.11), custom_call_target="tpu_custom_call" | custom-call | flops 6000000 | tf_op jit(solution)/shard_map/ownrows/pallas_call | solution.py:67
  12.2 0.0 copy-done.4
  12.2 1.0 %early.1 = (f32[5,40,512]{2,1,0:T(8,128)S(1)}, f32[40,128]{1,0:T(8,128)S(1)}) custom-call(f32[3]{0:T(128)S(1)} %copy-done.4, f32[32,512]{1,0:T(8,128)S(1)} %copy-done.1, f32[32,512]{1,0:T(8,128)S(1)} %copy-done.2), custom_call_target="tpu_custom_call" | custom-call | flops 6000000 | tf_op jit(solution)/shard_map/early/pallas_call | solution.py:67
  13.2 0.0 collective-permute-done.far
  13.2 0.0 collective-permute-done.1.near
  13.2 0.5 sides.1
  13.7 0.7 %collective-permute-start.2 = (f32[64,128]{1,0:T(8,128)S(1)}, f32[64,128]{1,0:T(8,128)S(1)}, u32[]{:S(2)}, u32[]{:S(2)}) collective-permute-start(f32[64,128]{1,0:T(8,128)S(1)} %get-tuple-element.34), channel_id=1, source_target_pairs={{1,2},{3,4},{5,6},{7,8},{9,10},{11,12},{13,14},{15,16},{17,18},{19... | collective-permute-start | bytes 98312 | tf_op jit(solution)/shard_map/ppermute | solution.py:704
  14.4 3.8 %collective-permute-start.3 = (f32[64,128]{1,0:T(8,128)S(1)}, f32[64,128]{1,0:T(8,128)S(1)}, u32[]{:S(2)}, u32[]{:S(2)}) collective-permute-start(f32[64,128]{1,0:T(8,128)S(1)} %get-tuple-element.35), channel_id=1, source_target_pairs={{0,1},{2,3},{4,5},{6,7},{8,9},{10,11},{12,13},{14,15},{16,17},{18,... | collective-permute-start | bytes 98312 | tf_op jit(solution)/shard_map/ppermute | solution.py:705
  18.2 1.7 %colsums.1 = (f32[480,640]{1,0:T(8,128)S(1)}, f32[5,40,512]{2,1,0:T(8,128)S(1)}, f32[3,40,256]{2,1,0:T(8,128)S(1)}) custom-call(f32[480,512]{1,0:T(8,128)S(1)} %ownrows.1.sums.rows, f32[480,256]{1,0:T(8,128)S(1)} %get-tuple-element.27.outer, f32[168,512]{1,0:T(8,128)S(1)} %collective-permute-done.far, ...), custom_call_target="tpu_custom_call", output_to_operand_aliasing={{1}: (6, {})} | custom-call | flops 6000000 | tf_op jit(solution)/shard_map/colsums/pallas_call | solution.py:67
  19.9 0.0 collective-permute-done.2.far
  19.9 0.1 collective-permute-done.3.near
  20.1 1.5 %fit.1 = (f32[32,512]{1,0:T(8,128)S(1)}, f32[32,512]{1,0:T(8,128)S(1)}, f32[32,512]{1,0:T(8,128)S(1)}, f32[32,512]{1,0:T(8,128)S(1)}, f32[32,512]{1,0:T(8,128)S(1)}, /*index=5*/f32[16,128]{1,0:T(8,128)S(1)}) custom-call(f32[480,640]{1,0:T(8,128)S(1)} %get-tuple-element.31.win, f32[120,512]{1,0:T(8,128)S(1)} %get-tuple-element.28.ext, ...), custom_call_target="tpu_custom_call" | custom-call | tf_op jit(solution)/shard_map/fit/pallas_call | solution.py:67
  21.6 19.1 %all_to_all.10 = f32[16,1,128]{2,1,0:T(1,128)S(1)} all-to-all(f32[16,1,128]{2,1,0:T(1,128)S(1)} %bitcast.15), channel_id=1, replica_groups={{0,4,8,12,16,20,24,28,32,36,40,44,48,52,56,60},{1,5,9,13,17,21,25,29,33..., dimensions={0} | all-to-all | bytes 16384 | tf_op jit(solution)/shard_map/all_to_all | solution.py:730
  40.7 18.6 %all_to_all.11 = f32[32,1,128]{2,1,0:T(1,128)S(1)} all-to-all(f32[32,1,128]{2,1,0:T(1,128)S(1)} %bitcast.12), channel_id=1, replica_groups={{0,1,2,3,64,65,66,67,128,129,130,131,192,193,194,195,256,257,258,259,32..., dimensions={0} | all-to-all | bytes 32768 | tf_op jit(solution)/shard_map/all_to_all | solution.py:734
  59.3 0.8 %final.1 = (f32[32,512]{1,0:T(8,128)}, f32[32,512]{1,0:T(8,128)}) custom-call(f32[32,128]{1,0:T(8,128)S(1)} %bitcast.13, f32[32,512]{1,0:T(8,128)S(1)} %get-tuple-element.37.base, f32[32,512]{1,0:T(8,128)S(1)} %get-tuple-element.38.v0, f32[32,512]{1,0:T(8,128)S(1)} %get-tuple-element.39.v1, f32[32,512]{1,0:T(8,128)S(1)} %get-tuple-element.40.v2, ...), custom_call_target="tpu_custom_call" | custom-call | tf_op jit(solution)/shard_map/final/pallas_call | solution.py:67
  (1 shorter events, 0.0 us)
Async XLA Ops:
  0.6 5.9 %copy-start.2 = (f32[32,512]{1,0:T(8,128)S(1)}, f32[32,512]{1,0:T(8,128)}, u32[]{:S(2)}) copy-start(f32[32,512]{1,0:T(8,128)} %ie.7) | copy-start | bytes 196612
  0.6 5.9 %copy-start.1 = (f32[32,512]{1,0:T(8,128)S(1)}, f32[32,512]{1,0:T(8,128)}, u32[]{:S(2)}) copy-start(f32[32,512]{1,0:T(8,128)} %ip.7) | copy-start | bytes 196612
  0.7 5.9 %copy-start.3 = (f32[32,512]{1,0:T(8,128)S(1)}, f32[32,512]{1,0:T(8,128)}, u32[]{:S(2)}) copy-start(f32[32,512]{1,0:T(8,128)} %vw.5) | copy-start | bytes 196612
  0.7 5.9 %copy-start = (f32[2,2,3,32,512]{4,3,2,1,0:T(8,128)S(1)}, f32[2,2,3,32,512]{4,3,2,1,0:T(8,128)}, u32[]{:S(2)}) copy-start(f32[2,2,3,32,512]{4,3,2,1,0:T(8,128)} %param.5) | copy-start | bytes 2359300
  1.9 10.3 %copy-start.4 = (f32[3]{0:T(128)S(1)}, f32[3]{0:T(128)}, u32[]{:S(2)}) copy-start(f32[3]{0:T(128)} %ground.1) | copy-start | bytes 40
  1.9 11.3 %collective-permute-start = (f32[168,512]{1,0:T(8,128)S(1)}, f32[168,512]{1,0:T(8,128)S(1)}, u32[]{:S(2)}, u32[]{:S(2)}) collective-permute-start(f32[168,512]{1,0:T(8,128)S(1)} %faredges.1), channel_id=1, source_target_pairs={{32,64},{96,128},{160,192},{224,256},{288,320},{352,384},{416,448}... | collective-permute-start | bytes 1032200 | tf_op jit(solution)/shard_map/ppermute | solution.py:675
  6.6 6.6 %collective-permute-start.1 = (f32[168,512]{1,0:T(8,128)S(1)}, f32[168,512]{1,0:T(8,128)S(1)}, u32[]{:S(2)}, u32[]{:S(2)}) collective-permute-start(f32[168,512]{1,0:T(8,128)S(1)} %nearedges.1), channel_id=1, source_target_pairs={{0,32},{64,96},{128,160},{192,224},{256,288},{320,352},{384,416},{... | collective-permute-start | bytes 1032200 | tf_op jit(solution)/shard_map/ppermute | solution.py:677
  13.7 6.2 %collective-permute-start.2 = (f32[64,128]{1,0:T(8,128)S(1)}, f32[64,128]{1,0:T(8,128)S(1)}, u32[]{:S(2)}, u32[]{:S(2)}) collective-permute-start(f32[64,128]{1,0:T(8,128)S(1)} %get-tuple-element.34), channel_id=1, source_target_pairs={{1,2},{3,4},{5,6},{7,8},{9,10},{11,12},{13,14},{15,16},{17,18},{19... | collective-permute-start | bytes 98312 | tf_op jit(solution)/shard_map/ppermute | solution.py:704
  14.4 5.7 %collective-permute-start.3 = (f32[64,128]{1,0:T(8,128)S(1)}, f32[64,128]{1,0:T(8,128)S(1)}, u32[]{:S(2)}, u32[]{:S(2)}) collective-permute-start(f32[64,128]{1,0:T(8,128)S(1)} %get-tuple-element.35), channel_id=1, source_target_pairs={{0,1},{2,3},{4,5},{6,7},{8,9},{10,11},{12,13},{14,15},{16,17},{18,... | collective-permute-start | bytes 98312 | tf_op jit(solution)/shard_map/ppermute | solution.py:705

commit v6 on v5

--- a/solution.py
+++ b/solution.py
@@ -19,8 +19,9 @@
 FIELDS = 12
 SIDE = RADIUS + 4
 REST = SIDE - 8
-REST_AT = FIELDS * 8
-EXTRA_AT = REST_AT + FIELDS * REST
+SENT = 9
+REST_AT = SENT * 8
+EXTRA_AT = REST_AT + SENT * REST
 SEND_ROWS = EXTRA_AT + 3 * 4
 GROUPS = 128 // SIDE
 PACK = 8 * (-(-FIELDS * 5 // GROUPS) + 1)
@@ -69,13 +70,24 @@
     return apply
 
 
+def turned(re1, im1, re2, im2):
+    square = re1 * re1 + im1 * im1
+    inverse = lax.rsqrt(square)
+    none = square == 0.0
+    cos = jnp.where(none, 1.0, re1 * inverse)
+    sin = jnp.where(none, 0.0, im1 * inverse)
+    return re1 * cos + im1 * sin, re2 * cos + im2 * sin, im2 * cos - re2 * sin
+
+
 def pack_edges(low, out, tiles, rest, extra):
     bottom = low == 1
-    for f in range(FIELDS):
-        out[8 * f : 8 * f + 8] = tiles(f)
-        at = REST_AT + REST * f
-        value = rest(f)
-        out[at : at + REST] = jnp.where(bottom, value[8 - REST : 8], value[0:REST])
+    for k in range(3):
+        for m, value in enumerate(turned(*(tiles(q * 3 + k) for q in range(4)))):
+            at = 8 * (m * 3 + k)
+            out[at : at + 8] = value
+        for m, value in enumerate(turned(*(rest(q * 3 + k) for q in range(4)))):
+            at = REST_AT + REST * (m * 3 + k)
+            out[at : at + REST] = jnp.where(bottom, value[8 - REST : 8], value[0:REST])
     for j in range(3):
         at = EXTRA_AT + 4 * j
         value = extra(j)
@@ -125,6 +137,10 @@
     )
 
 
+def turned_products(one, re2, im2):
+    return one * one, re2 * re2 + im2 * im2, one * re2, one * im2
+
+
 def own_rows_kernel(sv, rows, px, s4):
     sub = lax.broadcasted_iota(jnp.int32, (8, 128), 0)
     for j in range(4):
@@ -178,15 +194,15 @@
     for b in blocks:
         cols = slice(128 * b, 128 * b + 128)
         for k in range(3):
-            tiles = [sides(8 * (q * 3 + k), 8, cols) for q in range(4)]
-            rests = [sides(REST_AT + REST * (q * 3 + k), REST, cols) for q in range(4)]
-            for j, value in enumerate(products(*(x[0] for x in rests))):
+            tiles = [sides(8 * (m * 3 + k), 8, cols) for m in range(3)]
+            rests = [sides(REST_AT + REST * (m * 3 + k), REST, cols) for m in range(3)]
+            for j, value in enumerate(turned_products(*(x[0] for x in rests))):
                 xa[j, 0:REST] = value
-            for j, value in enumerate(products(*(x[0] for x in tiles))):
+            for j, value in enumerate(turned_products(*(x[0] for x in tiles))):
                 xa[j, REST:SIDE] = value
-            for j, value in enumerate(products(*(x[1] for x in tiles))):
+            for j, value in enumerate(turned_products(*(x[1] for x in tiles))):
                 xb[j, 16:24] = value
-            for j, value in enumerate(products(*(x[1] for x in rests))):
+            for j, value in enumerate(turned_products(*(x[1] for x in rests))):
                 xb[j, 24 : 24 + REST] = value
             for j in range(4):
                 four = (xa[j, 0:16] + xa[j, 1:17]) + (xa[j, 2:18] + xa[j, 3:19])

time: 60.4 us -> 59.7 us (0.988)
  starting transfers between devices: 13.9 us -> 13.1 us
    ppermute x1, starting transfers between devices: 3.79 us -> 3.05 us  [local(): near_side = lax.ppermute(right, 'col', swap(col_count, 0))]
    all_to_all x1, blocking collectives: 19.1 us -> 19.8 us  [local(): lax.all_to_all(sums.reshape(near_count, 1, 128), both, 0, 0, axis_index_g...]
  transfers between devices with their start and end apart: 4 -> 4, of which waited for: 1 -> 0; matrix products, arithmetic and copies ran while one was open for 0% -> 0% of each run, Pallas kernels for 6% -> 6%
where the time goes in v6:
time: 59.7 us; the launch traced here: 59.4 us
  blocking collectives  37.9 us (63%)
  starting transfers between devices  13.1 us (22%)
  Pallas kernels  7.55 us (13%)
  between operations  0.82 us (1%)
    all_to_all x1, blocking collectives, local(): lax.all_to_all(sums.reshape(near_count, 1, 128), both, 0, 0, axis_index_g...  19.8 us
    all_to_all x1, blocking collectives, local(): lax.all_to_all(parts.reshape(far_count, 1, 128), both, 0, 0, axis_index_g...  18.1 us
    pallas_call x9, Pallas kernels, apply(): return run(*args)  7.55 us
    ppermute x1, starting transfers between devices, local(): near = lax.ppermute(edge, 'row', swap(row_count, 0))  4.84 us
    ppermute x1, starting transfers between devices, local(): far = lax.ppermute(edge, 'row', swap(row_count, 1))  4.58 us
    ppermute x1, starting transfers between devices, local(): near_side = lax.ppermute(right, 'col', swap(col_count, 0))  3.05 us
  transfers between devices with their start and end apart: 4, of which 0 were waited for; matrix products, arithmetic and copies ran while one was open for 0% of the time, Pallas kernels for 6%

profile of v6, /device:TPU:1, one launch (start us, length us, event | category | flops | bytes accessed | tf_op | source)
XLA Modules:
  0.0 59.4 jit_solution(5914423570586046585)
XLA Ops:
  0.6 0.0 copy-start.2
  0.6 0.0 copy-start.1
  0.7 0.0 copy-start.3
  0.7 0.0 copy-start
  0.7 1.2 %faredges.1 = f32[129,512]{1,0:T(8,128)S(1)} custom-call(f32[12,32,512]{2,1,0:T(8,128)} %bitcast.9, f32[32,512]{1,0:T(8,128)} %vw.5, f32[32,512]{1,0:T(8,128)} %ip.7, f32[32,512]{1,0:T(8,128)} %ie.7), custom_call_target="tpu_custom_call" | custom-call | tf_op jit(solution)/shard_map/faredges/pallas_call | solution.py:68
  1.9 0.0 copy-start.4
  1.9 4.6 %collective-permute-start = (f32[129,512]{1,0:T(8,128)S(1)}, f32[129,512]{1,0:T(8,128)S(1)}, u32[]{:S(2)}, u32[]{:S(2)}) collective-permute-start(f32[129,512]{1,0:T(8,128)S(1)} %faredges.1), channel_id=1, source_target_pairs={{32,64},{96,128},{160,192},{224,256},{288,320},{352,384},{416,448}... | collective-permute-start | bytes 792584 | tf_op jit(solution)/shard_map/ppermute | solution.py:691
  6.5 0.0 copy-done.2
  6.5 0.0 copy-done.1
  6.5 0.0 copy-done.3
  6.6 0.0 copy-done
  6.6 0.1 nearedges.1
  6.7 4.8 %collective-permute-start.1 = (f32[129,512]{1,0:T(8,128)S(1)}, f32[129,512]{1,0:T(8,128)S(1)}, u32[]{:S(2)}, u32[]{:S(2)}) collective-permute-start(f32[129,512]{1,0:T(8,128)S(1)} %nearedges.1), channel_id=1, source_target_pairs={{0,32},{64,96},{128,160},{192,224},{256,288},{320,352},{384,416},{... | collective-permute-start | bytes 792584 | tf_op jit(solution)/shard_map/ppermute | solution.py:693
  11.5 0.7 %ownrows.1.sums.rows = f32[480,512]{1,0:T(8,128)S(1)} custom-call(f32[12,32,512]{2,1,0:T(8,128)S(1)} %bitcast.11), custom_call_target="tpu_custom_call" | custom-call | flops 6000000 | tf_op jit(solution)/shard_map/ownrows/pallas_call | solution.py:68
  12.3 0.0 copy-done.4
  12.3 1.0 %early.1 = (f32[5,40,512]{2,1,0:T(8,128)S(1)}, f32[40,128]{1,0:T(8,128)S(1)}) custom-call(f32[3]{0:T(128)S(1)} %copy-done.4, f32[32,512]{1,0:T(8,128)S(1)} %copy-done.1, f32[32,512]{1,0:T(8,128)S(1)} %copy-done.2), custom_call_target="tpu_custom_call" | custom-call | flops 6000000 | tf_op jit(solution)/shard_map/early/pallas_call | solution.py:68
  13.2 0.0 collective-permute-done.far
  13.3 0.0 collective-permute-done.1.near
  13.3 0.5 sides.1
  13.8 0.7 %collective-permute-start.2 = (f32[64,128]{1,0:T(8,128)S(1)}, f32[64,128]{1,0:T(8,128)S(1)}, u32[]{:S(2)}, u32[]{:S(2)}) collective-permute-start(f32[64,128]{1,0:T(8,128)S(1)} %get-tuple-element.34), channel_id=1, source_target_pairs={{1,2},{3,4},{5,6},{7,8},{9,10},{11,12},{13,14},{15,16},{17,18},{19... | collective-permute-start | bytes 98312 | tf_op jit(solution)/shard_map/ppermute | solution.py:720
  14.4 3.0 %collective-permute-start.3 = (f32[64,128]{1,0:T(8,128)S(1)}, f32[64,128]{1,0:T(8,128)S(1)}, u32[]{:S(2)}, u32[]{:S(2)}) collective-permute-start(f32[64,128]{1,0:T(8,128)S(1)} %get-tuple-element.35), channel_id=1, source_target_pairs={{0,1},{2,3},{4,5},{6,7},{8,9},{10,11},{12,13},{14,15},{16,17},{18,... | collective-permute-start | bytes 98312 | tf_op jit(solution)/shard_map/ppermute | solution.py:721
  17.5 1.6 %colsums.1 = (f32[480,640]{1,0:T(8,128)S(1)}, f32[5,40,512]{2,1,0:T(8,128)S(1)}, f32[3,40,256]{2,1,0:T(8,128)S(1)}) custom-call(f32[480,512]{1,0:T(8,128)S(1)} %ownrows.1.sums.rows, f32[480,256]{1,0:T(8,128)S(1)} %get-tuple-element.27.outer, f32[129,512]{1,0:T(8,128)S(1)} %collective-permute-done.far, ...), custom_call_target="tpu_custom_call", output_to_operand_aliasing={{1}: (6, {})} | custom-call | flops 6000000 | tf_op jit(solution)/shard_map/colsums/pallas_call | solution.py:68
  19.1 0.0 collective-permute-done.2.far
  19.2 0.0 collective-permute-done.3.near
  19.2 1.5 %fit.1 = (f32[32,512]{1,0:T(8,128)S(1)}, f32[32,512]{1,0:T(8,128)S(1)}, f32[32,512]{1,0:T(8,128)S(1)}, f32[32,512]{1,0:T(8,128)S(1)}, f32[32,512]{1,0:T(8,128)S(1)}, /*index=5*/f32[16,128]{1,0:T(8,128)S(1)}) custom-call(f32[480,640]{1,0:T(8,128)S(1)} %get-tuple-element.31.win, f32[120,512]{1,0:T(8,128)S(1)} %get-tuple-element.28.ext, ...), custom_call_target="tpu_custom_call" | custom-call | tf_op jit(solution)/shard_map/fit/pallas_call | solution.py:68
  20.7 19.8 %all_to_all.10 = f32[16,1,128]{2,1,0:T(1,128)S(1)} all-to-all(f32[16,1,128]{2,1,0:T(1,128)S(1)} %bitcast.15), channel_id=1, replica_groups={{0,4,8,12,16,20,24,28,32,36,40,44,48,52,56,60},{1,5,9,13,17,21,25,29,33..., dimensions={0} | all-to-all | bytes 16384 | tf_op jit(solution)/shard_map/all_to_all | solution.py:746
  40.5 18.1 %all_to_all.11 = f32[32,1,128]{2,1,0:T(1,128)S(1)} all-to-all(f32[32,1,128]{2,1,0:T(1,128)S(1)} %bitcast.12), channel_id=1, replica_groups={{0,1,2,3,64,65,66,67,128,129,130,131,192,193,194,195,256,257,258,259,32..., dimensions={0} | all-to-all | bytes 32768 | tf_op jit(solution)/shard_map/all_to_all | solution.py:750
  58.6 0.8 %final.1 = (f32[32,512]{1,0:T(8,128)}, f32[32,512]{1,0:T(8,128)}) custom-call(f32[32,128]{1,0:T(8,128)S(1)} %bitcast.13, f32[32,512]{1,0:T(8,128)S(1)} %get-tuple-element.37.base, f32[32,512]{1,0:T(8,128)S(1)} %get-tuple-element.38.v0, f32[32,512]{1,0:T(8,128)S(1)} %get-tuple-element.39.v1, f32[32,512]{1,0:T(8,128)S(1)} %get-tuple-element.40.v2, ...), custom_call_target="tpu_custom_call" | custom-call | tf_op jit(solution)/shard_map/final/pallas_call | solution.py:68
  (1 shorter events, 0.0 us)
Async XLA Ops:
  0.6 5.9 %copy-start.2 = (f32[32,512]{1,0:T(8,128)S(1)}, f32[32,512]{1,0:T(8,128)}, u32[]{:S(2)}) copy-start(f32[32,512]{1,0:T(8,128)} %ie.7) | copy-start | bytes 196612
  0.6 5.9 %copy-start.1 = (f32[32,512]{1,0:T(8,128)S(1)}, f32[32,512]{1,0:T(8,128)}, u32[]{:S(2)}) copy-start(f32[32,512]{1,0:T(8,128)} %ip.7) | copy-start | bytes 196612
  0.7 5.9 %copy-start.3 = (f32[32,512]{1,0:T(8,128)S(1)}, f32[32,512]{1,0:T(8,128)}, u32[]{:S(2)}) copy-start(f32[32,512]{1,0:T(8,128)} %vw.5) | copy-start | bytes 196612
  0.7 5.9 %copy-start = (f32[2,2,3,32,512]{4,3,2,1,0:T(8,128)S(1)}, f32[2,2,3,32,512]{4,3,2,1,0:T(8,128)}, u32[]{:S(2)}) copy-start(f32[2,2,3,32,512]{4,3,2,1,0:T(8,128)} %param.5) | copy-start | bytes 2359300
  1.9 10.3 %copy-start.4 = (f32[3]{0:T(128)S(1)}, f32[3]{0:T(128)}, u32[]{:S(2)}) copy-start(f32[3]{0:T(128)} %ground.1) | copy-start | bytes 40
  1.9 11.3 %collective-permute-start = (f32[129,512]{1,0:T(8,128)S(1)}, f32[129,512]{1,0:T(8,128)S(1)}, u32[]{:S(2)}, u32[]{:S(2)}) collective-permute-start(f32[129,512]{1,0:T(8,128)S(1)} %faredges.1), channel_id=1, source_target_pairs={{32,64},{96,128},{160,192},{224,256},{288,320},{352,384},{416,448}... | collective-permute-start | bytes 792584 | tf_op jit(solution)/shard_map/ppermute | solution.py:691
  6.7 6.6 %collective-permute-start.1 = (f32[129,512]{1,0:T(8,128)S(1)}, f32[129,512]{1,0:T(8,128)S(1)}, u32[]{:S(2)}, u32[]{:S(2)}) collective-permute-start(f32[129,512]{1,0:T(8,128)S(1)} %nearedges.1), channel_id=1, source_target_pairs={{0,32},{64,96},{128,160},{192,224},{256,288},{320,352},{384,416},{... | collective-permute-start | bytes 792584 | tf_op jit(solution)/shard_map/ppermute | solution.py:693
  13.8 5.4 %collective-permute-start.2 = (f32[64,128]{1,0:T(8,128)S(1)}, f32[64,128]{1,0:T(8,128)S(1)}, u32[]{:S(2)}, u32[]{:S(2)}) collective-permute-start(f32[64,128]{1,0:T(8,128)S(1)} %get-tuple-element.34), channel_id=1, source_target_pairs={{1,2},{3,4},{5,6},{7,8},{9,10},{11,12},{13,14},{15,16},{17,18},{19... | collective-permute-start | bytes 98312 | tf_op jit(solution)/shard_map/ppermute | solution.py:720
  14.4 4.7 %collective-permute-start.3 = (f32[64,128]{1,0:T(8,128)S(1)}, f32[64,128]{1,0:T(8,128)S(1)}, u32[]{:S(2)}, u32[]{:S(2)}) collective-permute-start(f32[64,128]{1,0:T(8,128)S(1)} %get-tuple-element.35), channel_id=1, source_target_pairs={{0,1},{2,3},{4,5},{6,7},{8,9},{10,11},{12,13},{14,15},{16,17},{18,... | collective-permute-start | bytes 98312 | tf_op jit(solution)/shard_map/ppermute | solution.py:721

commit v7 on v6

--- a/solution.py
+++ b/solution.py
@@ -655,16 +655,17 @@
     def index(r, c):
         return r * col_count + c
 
+    def outward(count):
+        return sorted(range(count), key=lambda i: (abs(i - count // 2), i))
+
     ring = max(col_count // 8, 1)
+    cores, ys = outward(2), outward(row_count // 2)
+    xs, zs = outward(ring), outward(col_count // ring)
     near_groups = [
-        [index(2 * y + core, x + ring * z) for core in range(2) for z in range(col_count // ring)]
-        for y in range(row_count // 2)
-        for x in range(ring)
+        [index(2 * y + core, x + ring * z) for core in cores for z in zs] for y in ys for x in xs
     ]
     far_groups = [
-        [index(2 * y + core, x + ring * z) for y in range(row_count // 2) for x in range(ring)]
-        for core in range(2)
-        for z in range(col_count // ring)
+        [index(2 * y + core, x + ring * z) for y in ys for x in xs] for core in cores for z in zs
     ]
     near_count = len(near_groups[0])
     far_count = len(far_groups[0])

time: 59.7 us -> 52.5 us (0.88)
  blocking collectives: 37.9 us -> 30.1 us
    all_to_all x1, blocking collectives: 18.1 us -> 12.6 us  [local(): lax.all_to_all(parts.reshape(far_count, 1, 128), both, 0, 0, axis_index_g...]
    all_to_all x1, blocking collectives: 19.8 us -> 17.4 us  [local(): lax.all_to_all(sums.reshape(near_count, 1, 128), both, 0, 0, axis_index_g...]
  transfers between devices with their start and end apart: 4 -> 4, of which waited for: 0 -> 0; matrix products, arithmetic and copies ran while one was open for 0% -> 0% of each run, Pallas kernels for 6% -> 7%
where the time goes in v7:
time: 52.5 us; the launch traced here: 51.6 us
  blocking collectives  30.1 us (57%)
  starting transfers between devices  13.1 us (25%)
  Pallas kernels  7.55 us (14%)
  between operations  0.82 us (2%)
    all_to_all x1, blocking collectives, local(): lax.all_to_all(sums.reshape(near_count, 1, 128), both, 0, 0, axis_index_g...  17.4 us
    all_to_all x1, blocking collectives, local(): lax.all_to_all(parts.reshape(far_count, 1, 128), both, 0, 0, axis_index_g...  12.6 us
    pallas_call x9, Pallas kernels, apply(): return run(*args)  7.55 us
    ppermute x1, starting transfers between devices, local(): near = lax.ppermute(edge, 'row', swap(row_count, 0))  4.84 us
    ppermute x1, starting transfers between devices, local(): far = lax.ppermute(edge, 'row', swap(row_count, 1))  4.58 us
    ppermute x1, starting transfers between devices, local(): near_side = lax.ppermute(right, 'col', swap(col_count, 0))  3.05 us
  transfers between devices with their start and end apart: 4, of which 0 were waited for; matrix products, arithmetic and copies ran while one was open for 0% of the time, Pallas kernels for 7%

profile of v7, /device:TPU:1, one launch (start us, length us, event | category | flops | bytes accessed | tf_op | source)
XLA Modules:
  0.0 51.6 jit_solution(4717153859309432911)
XLA Ops:
  0.6 0.0 copy-start.2
  0.6 0.0 copy-start.1
  0.7 0.0 copy-start.3
  0.7 0.0 copy-start
  0.7 1.2 %faredges.1 = f32[129,512]{1,0:T(8,128)S(1)} custom-call(f32[12,32,512]{2,1,0:T(8,128)} %bitcast.9, f32[32,512]{1,0:T(8,128)} %vw.5, f32[32,512]{1,0:T(8,128)} %ip.7, f32[32,512]{1,0:T(8,128)} %ie.7), custom_call_target="tpu_custom_call" | custom-call | tf_op jit(solution)/shard_map/faredges/pallas_call | solution.py:68
  1.9 0.0 copy-start.4
  1.9 4.6 %collective-permute-start = (f32[129,512]{1,0:T(8,128)S(1)}, f32[129,512]{1,0:T(8,128)S(1)}, u32[]{:S(2)}, u32[]{:S(2)}) collective-permute-start(f32[129,512]{1,0:T(8,128)S(1)} %faredges.1), channel_id=1, source_target_pairs={{32,64},{96,128},{160,192},{224,256},{288,320},{352,384},{416,448}... | collective-permute-start | bytes 792584 | tf_op jit(solution)/shard_map/ppermute | solution.py:692
  6.5 0.0 copy-done.2
  6.5 0.0 copy-done.1
  6.5 0.0 copy-done.3
  6.6 0.0 copy-done
  6.6 0.1 nearedges.1
  6.7 4.8 %collective-permute-start.1 = (f32[129,512]{1,0:T(8,128)S(1)}, f32[129,512]{1,0:T(8,128)S(1)}, u32[]{:S(2)}, u32[]{:S(2)}) collective-permute-start(f32[129,512]{1,0:T(8,128)S(1)} %nearedges.1), channel_id=1, source_target_pairs={{0,32},{64,96},{128,160},{192,224},{256,288},{320,352},{384,416},{... | collective-permute-start | bytes 792584 | tf_op jit(solution)/shard_map/ppermute | solution.py:694
  11.5 0.7 %ownrows.1.sums.rows = f32[480,512]{1,0:T(8,128)S(1)} custom-call(f32[12,32,512]{2,1,0:T(8,128)S(1)} %bitcast.11), custom_call_target="tpu_custom_call" | custom-call | flops 6000000 | tf_op jit(solution)/shard_map/ownrows/pallas_call | solution.py:68
  12.3 0.0 copy-done.4
  12.3 1.0 %early.1 = (f32[5,40,512]{2,1,0:T(8,128)S(1)}, f32[40,128]{1,0:T(8,128)S(1)}) custom-call(f32[3]{0:T(128)S(1)} %copy-done.4, f32[32,512]{1,0:T(8,128)S(1)} %copy-done.1, f32[32,512]{1,0:T(8,128)S(1)} %copy-done.2), custom_call_target="tpu_custom_call" | custom-call | flops 6000000 | tf_op jit(solution)/shard_map/early/pallas_call | solution.py:68
  13.2 0.0 collective-permute-done.far
  13.3 0.0 collective-permute-done.1.near
  13.3 0.5 sides.1
  13.8 0.7 %collective-permute-start.2 = (f32[64,128]{1,0:T(8,128)S(1)}, f32[64,128]{1,0:T(8,128)S(1)}, u32[]{:S(2)}, u32[]{:S(2)}) collective-permute-start(f32[64,128]{1,0:T(8,128)S(1)} %get-tuple-element.34), channel_id=1, source_target_pairs={{1,2},{3,4},{5,6},{7,8},{9,10},{11,12},{13,14},{15,16},{17,18},{19... | collective-permute-start | bytes 98312 | tf_op jit(solution)/shard_map/ppermute | solution.py:721
  14.4 3.0 %collective-permute-start.3 = (f32[64,128]{1,0:T(8,128)S(1)}, f32[64,128]{1,0:T(8,128)S(1)}, u32[]{:S(2)}, u32[]{:S(2)}) collective-permute-start(f32[64,128]{1,0:T(8,128)S(1)} %get-tuple-element.35), channel_id=1, source_target_pairs={{0,1},{2,3},{4,5},{6,7},{8,9},{10,11},{12,13},{14,15},{16,17},{18,... | collective-permute-start | bytes 98312 | tf_op jit(solution)/shard_map/ppermute | solution.py:722
  17.5 1.6 %colsums.1 = (f32[480,640]{1,0:T(8,128)S(1)}, f32[5,40,512]{2,1,0:T(8,128)S(1)}, f32[3,40,256]{2,1,0:T(8,128)S(1)}) custom-call(f32[480,512]{1,0:T(8,128)S(1)} %ownrows.1.sums.rows, f32[480,256]{1,0:T(8,128)S(1)} %get-tuple-element.27.outer, f32[129,512]{1,0:T(8,128)S(1)} %collective-permute-done.far, ...), custom_call_target="tpu_custom_call", output_to_operand_aliasing={{1}: (6, {})} | custom-call | flops 6000000 | tf_op jit(solution)/shard_map/colsums/pallas_call | solution.py:68
  19.1 0.0 collective-permute-done.2.far
  19.2 0.0 collective-permute-done.3.near
  19.2 1.5 %fit.1 = (f32[32,512]{1,0:T(8,128)S(1)}, f32[32,512]{1,0:T(8,128)S(1)}, f32[32,512]{1,0:T(8,128)S(1)}, f32[32,512]{1,0:T(8,128)S(1)}, f32[32,512]{1,0:T(8,128)S(1)}, /*index=5*/f32[16,128]{1,0:T(8,128)S(1)}) custom-call(f32[480,640]{1,0:T(8,128)S(1)} %get-tuple-element.31.win, f32[120,512]{1,0:T(8,128)S(1)} %get-tuple-element.28.ext, ...), custom_call_target="tpu_custom_call" | custom-call | tf_op jit(solution)/shard_map/fit/pallas_call | solution.py:68
  20.7 17.4 %all_to_all.10 = f32[16,1,128]{2,1,0:T(1,128)S(1)} all-to-all(f32[16,1,128]{2,1,0:T(1,128)S(1)} %bitcast.15), channel_id=1, replica_groups={{306,302,310,298,314,294,318,290,274,270,278,266,282,262,286,258},{305,..., dimensions={0} | all-to-all | bytes 16384 | tf_op jit(solution)/shard_map/all_to_all | solution.py:747
  38.2 12.6 %all_to_all.11 = f32[32,1,128]{2,1,0:T(1,128)S(1)} all-to-all(f32[32,1,128]{2,1,0:T(1,128)S(1)} %bitcast.12), channel_id=1, replica_groups={{306,305,307,304,242,241,243,240,370,369,371,368,178,177,179,176,434,43..., dimensions={0} | all-to-all | bytes 32768 | tf_op jit(solution)/shard_map/all_to_all | solution.py:751
  50.8 0.8 %final.1 = (f32[32,512]{1,0:T(8,128)}, f32[32,512]{1,0:T(8,128)}) custom-call(f32[32,128]{1,0:T(8,128)S(1)} %bitcast.13, f32[32,512]{1,0:T(8,128)S(1)} %get-tuple-element.37.base, f32[32,512]{1,0:T(8,128)S(1)} %get-tuple-element.38.v0, f32[32,512]{1,0:T(8,128)S(1)} %get-tuple-element.39.v1, f32[32,512]{1,0:T(8,128)S(1)} %get-tuple-element.40.v2, ...), custom_call_target="tpu_custom_call" | custom-call | tf_op jit(solution)/shard_map/final/pallas_call | solution.py:68
  (1 shorter events, 0.0 us)
Async XLA Ops:
  0.6 5.9 %copy-start.2 = (f32[32,512]{1,0:T(8,128)S(1)}, f32[32,512]{1,0:T(8,128)}, u32[]{:S(2)}) copy-start(f32[32,512]{1,0:T(8,128)} %ie.7) | copy-start | bytes 196612
  0.6 5.9 %copy-start.1 = (f32[32,512]{1,0:T(8,128)S(1)}, f32[32,512]{1,0:T(8,128)}, u32[]{:S(2)}) copy-start(f32[32,512]{1,0:T(8,128)} %ip.7) | copy-start | bytes 196612
  0.7 5.9 %copy-start.3 = (f32[32,512]{1,0:T(8,128)S(1)}, f32[32,512]{1,0:T(8,128)}, u32[]{:S(2)}) copy-start(f32[32,512]{1,0:T(8,128)} %vw.5) | copy-start | bytes 196612
  0.7 5.9 %copy-start = (f32[2,2,3,32,512]{4,3,2,1,0:T(8,128)S(1)}, f32[2,2,3,32,512]{4,3,2,1,0:T(8,128)}, u32[]{:S(2)}) copy-start(f32[2,2,3,32,512]{4,3,2,1,0:T(8,128)} %param.5) | copy-start | bytes 2359300
  1.9 10.3 %copy-start.4 = (f32[3]{0:T(128)S(1)}, f32[3]{0:T(128)}, u32[]{:S(2)}) copy-start(f32[3]{0:T(128)} %ground.1) | copy-start | bytes 40
  1.9 11.3 %collective-permute-start = (f32[129,512]{1,0:T(8,128)S(1)}, f32[129,512]{1,0:T(8,128)S(1)}, u32[]{:S(2)}, u32[]{:S(2)}) collective-permute-start(f32[129,512]{1,0:T(8,128)S(1)} %faredges.1), channel_id=1, source_target_pairs={{32,64},{96,128},{160,192},{224,256},{288,320},{352,384},{416,448}... | collective-permute-start | bytes 792584 | tf_op jit(solution)/shard_map/ppermute | solution.py:692
  6.7 6.6 %collective-permute-start.1 = (f32[129,512]{1,0:T(8,128)S(1)}, f32[129,512]{1,0:T(8,128)S(1)}, u32[]{:S(2)}, u32[]{:S(2)}) collective-permute-start(f32[129,512]{1,0:T(8,128)S(1)} %nearedges.1), channel_id=1, source_target_pairs={{0,32},{64,96},{128,160},{192,224},{256,288},{320,352},{384,416},{... | collective-permute-start | bytes 792584 | tf_op jit(solution)/shard_map/ppermute | solution.py:694
  13.8 5.4 %collective-permute-start.2 = (f32[64,128]{1,0:T(8,128)S(1)}, f32[64,128]{1,0:T(8,128)S(1)}, u32[]{:S(2)}, u32[]{:S(2)}) collective-permute-start(f32[64,128]{1,0:T(8,128)S(1)} %get-tuple-element.34), channel_id=1, source_target_pairs={{1,2},{3,4},{5,6},{7,8},{9,10},{11,12},{13,14},{15,16},{17,18},{19... | collective-permute-start | bytes 98312 | tf_op jit(solution)/shard_map/ppermute | solution.py:721
  14.4 4.7 %collective-permute-start.3 = (f32[64,128]{1,0:T(8,128)S(1)}, f32[64,128]{1,0:T(8,128)S(1)}, u32[]{:S(2)}, u32[]{:S(2)}) collective-permute-start(f32[64,128]{1,0:T(8,128)S(1)} %get-tuple-element.35), channel_id=1, source_target_pairs={{0,1},{2,3},{4,5},{6,7},{8,9},{10,11},{12,13},{14,15},{16,17},{18,... | collective-permute-start | bytes 98312 | tf_op jit(solution)/shard_map/ppermute | solution.py:722

commit v8 on v7

--- a/solution.py
+++ b/solution.py
@@ -269,8 +269,7 @@
 def sincos(x):
     turns = jnp.floor(x * 0.3183098861837907 + 0.5)
     y = x - turns * 3.140625
-    y = y - turns * 9.67502593994140625e-4
-    y = y - turns * 1.509957990978376432e-7
+    y = y - turns * 9.676535897932385e-4
     odd = turns - 2.0 * jnp.floor(turns * 0.5)
     sign = 1.0 - 2.0 * odd
     z = y * y

time: 52.5 us -> 52.5 us (level)
  no operation moved by 1% of the time
where the time goes in v8:
time: 52.5 us; the launch traced here: 51.6 us
  blocking collectives  30.1 us (57%)
  starting transfers between devices  13.1 us (25%)
  Pallas kernels  7.55 us (14%)
  between operations  0.82 us (2%)
    all_to_all x1, blocking collectives, local(): lax.all_to_all(sums.reshape(near_count, 1, 128), both, 0, 0, axis_index_g...  17.4 us
    all_to_all x1, blocking collectives, local(): lax.all_to_all(parts.reshape(far_count, 1, 128), both, 0, 0, axis_index_g...  12.6 us
    pallas_call x9, Pallas kernels, apply(): return run(*args)  7.55 us
    ppermute x1, starting transfers between devices, local(): near = lax.ppermute(edge, 'row', swap(row_count, 0))  4.84 us
    ppermute x1, starting transfers between devices, local(): far = lax.ppermute(edge, 'row', swap(row_count, 1))  4.58 us
    ppermute x1, starting transfers between devices, local(): near_side = lax.ppermute(right, 'col', swap(col_count, 0))  3.05 us
  transfers between devices with their start and end apart: 4, of which 0 were waited for; matrix products, arithmetic and copies ran while one was open for 0% of the time, Pallas kernels for 7%

profile of v8, /device:TPU:1, one launch (start us, length us, event | category | flops | bytes accessed | tf_op | source)
XLA Modules:
  0.0 51.6 jit_solution(18358598901308042232)
XLA Ops:
  0.6 0.0 copy-start.2
  0.6 0.0 copy-start.1
  0.7 0.0 copy-start.3
  0.7 0.0 copy-start
  0.7 1.2 %faredges.1 = f32[129,512]{1,0:T(8,128)S(1)} custom-call(f32[12,32,512]{2,1,0:T(8,128)} %bitcast.9, f32[32,512]{1,0:T(8,128)} %vw.5, f32[32,512]{1,0:T(8,128)} %ip.7, f32[32,512]{1,0:T(8,128)} %ie.7), custom_call_target="tpu_custom_call" | custom-call | tf_op jit(solution)/shard_map/faredges/pallas_call | solution.py:68
  1.9 0.0 copy-start.4
  1.9 4.6 %collective-permute-start = (f32[129,512]{1,0:T(8,128)S(1)}, f32[129,512]{1,0:T(8,128)S(1)}, u32[]{:S(2)}, u32[]{:S(2)}) collective-permute-start(f32[129,512]{1,0:T(8,128)S(1)} %faredges.1), channel_id=1, source_target_pairs={{32,64},{96,128},{160,192},{224,256},{288,320},{352,384},{416,448}... | collective-permute-start | bytes 792584 | tf_op jit(solution)/shard_map/ppermute | solution.py:691
  6.5 0.0 copy-done.2
  6.5 0.0 copy-done.1
  6.5 0.0 copy-done.3
  6.6 0.0 copy-done
  6.6 0.1 nearedges.1
  6.7 4.8 %collective-permute-start.1 = (f32[129,512]{1,0:T(8,128)S(1)}, f32[129,512]{1,0:T(8,128)S(1)}, u32[]{:S(2)}, u32[]{:S(2)}) collective-permute-start(f32[129,512]{1,0:T(8,128)S(1)} %nearedges.1), channel_id=1, source_target_pairs={{0,32},{64,96},{128,160},{192,224},{256,288},{320,352},{384,416},{... | collective-permute-start | bytes 792584 | tf_op jit(solution)/shard_map/ppermute | solution.py:693
  11.5 0.7 %ownrows.1.sums.rows = f32[480,512]{1,0:T(8,128)S(1)} custom-call(f32[12,32,512]{2,1,0:T(8,128)S(1)} %bitcast.11), custom_call_target="tpu_custom_call" | custom-call | flops 6000000 | tf_op jit(solution)/shard_map/ownrows/pallas_call | solution.py:68
  12.3 0.0 copy-done.4
  12.3 1.0 %early.1 = (f32[5,40,512]{2,1,0:T(8,128)S(1)}, f32[40,128]{1,0:T(8,128)S(1)}) custom-call(f32[3]{0:T(128)S(1)} %copy-done.4, f32[32,512]{1,0:T(8,128)S(1)} %copy-done.1, f32[32,512]{1,0:T(8,128)S(1)} %copy-done.2), custom_call_target="tpu_custom_call" | custom-call | flops 6000000 | tf_op jit(solution)/shard_map/early/pallas_call | solution.py:68
  13.2 0.0 collective-permute-done.far
  13.3 0.0 collective-permute-done.1.near
  13.3 0.5 sides.1
  13.8 0.7 %collective-permute-start.2 = (f32[64,128]{1,0:T(8,128)S(1)}, f32[64,128]{1,0:T(8,128)S(1)}, u32[]{:S(2)}, u32[]{:S(2)}) collective-permute-start(f32[64,128]{1,0:T(8,128)S(1)} %get-tuple-element.34), channel_id=1, source_target_pairs={{1,2},{3,4},{5,6},{7,8},{9,10},{11,12},{13,14},{15,16},{17,18},{19... | collective-permute-start | bytes 98312 | tf_op jit(solution)/shard_map/ppermute | solution.py:720
  14.4 3.1 %collective-permute-start.3 = (f32[64,128]{1,0:T(8,128)S(1)}, f32[64,128]{1,0:T(8,128)S(1)}, u32[]{:S(2)}, u32[]{:S(2)}) collective-permute-start(f32[64,128]{1,0:T(8,128)S(1)} %get-tuple-element.35), channel_id=1, source_target_pairs={{0,1},{2,3},{4,5},{6,7},{8,9},{10,11},{12,13},{14,15},{16,17},{18,... | collective-permute-start | bytes 98312 | tf_op jit(solution)/shard_map/ppermute | solution.py:721
  17.5 1.6 %colsums.1 = (f32[480,640]{1,0:T(8,128)S(1)}, f32[5,40,512]{2,1,0:T(8,128)S(1)}, f32[3,40,256]{2,1,0:T(8,128)S(1)}) custom-call(f32[480,512]{1,0:T(8,128)S(1)} %ownrows.1.sums.rows, f32[480,256]{1,0:T(8,128)S(1)} %get-tuple-element.27.outer, f32[129,512]{1,0:T(8,128)S(1)} %collective-permute-done.far, ...), custom_call_target="tpu_custom_call", output_to_operand_aliasing={{1}: (6, {})} | custom-call | flops 6000000 | tf_op jit(solution)/shard_map/colsums/pallas_call | solution.py:68
  19.1 0.0 collective-permute-done.2.far
  19.2 0.0 collective-permute-done.3.near
  19.2 1.5 %fit.1 = (f32[32,512]{1,0:T(8,128)S(1)}, f32[32,512]{1,0:T(8,128)S(1)}, f32[32,512]{1,0:T(8,128)S(1)}, f32[32,512]{1,0:T(8,128)S(1)}, f32[32,512]{1,0:T(8,128)S(1)}, /*index=5*/f32[16,128]{1,0:T(8,128)S(1)}) custom-call(f32[480,640]{1,0:T(8,128)S(1)} %get-tuple-element.31.win, f32[120,512]{1,0:T(8,128)S(1)} %get-tuple-element.28.ext, ...), custom_call_target="tpu_custom_call" | custom-call | tf_op jit(solution)/shard_map/fit/pallas_call | solution.py:68
  20.7 17.4 %all_to_all.10 = f32[16,1,128]{2,1,0:T(1,128)S(1)} all-to-all(f32[16,1,128]{2,1,0:T(1,128)S(1)} %bitcast.15), channel_id=1, replica_groups={{306,302,310,298,314,294,318,290,274,270,278,266,282,262,286,258},{305,..., dimensions={0} | all-to-all | bytes 16384 | tf_op jit(solution)/shard_map/all_to_all | solution.py:746
  38.2 12.6 %all_to_all.11 = f32[32,1,128]{2,1,0:T(1,128)S(1)} all-to-all(f32[32,1,128]{2,1,0:T(1,128)S(1)} %bitcast.12), channel_id=1, replica_groups={{306,305,307,304,242,241,243,240,370,369,371,368,178,177,179,176,434,43..., dimensions={0} | all-to-all | bytes 32768 | tf_op jit(solution)/shard_map/all_to_all | solution.py:750
  50.8 0.8 %final.1 = (f32[32,512]{1,0:T(8,128)}, f32[32,512]{1,0:T(8,128)}) custom-call(f32[32,128]{1,0:T(8,128)S(1)} %bitcast.13, f32[32,512]{1,0:T(8,128)S(1)} %get-tuple-element.37.base, f32[32,512]{1,0:T(8,128)S(1)} %get-tuple-element.38.v0, f32[32,512]{1,0:T(8,128)S(1)} %get-tuple-element.39.v1, f32[32,512]{1,0:T(8,128)S(1)} %get-tuple-element.40.v2, ...), custom_call_target="tpu_custom_call" | custom-call | tf_op jit(solution)/shard_map/final/pallas_call | solution.py:68
  (1 shorter events, 0.0 us)
Async XLA Ops:
  0.6 5.9 %copy-start.2 = (f32[32,512]{1,0:T(8,128)S(1)}, f32[32,512]{1,0:T(8,128)}, u32[]{:S(2)}) copy-start(f32[32,512]{1,0:T(8,128)} %ie.7) | copy-start | bytes 196612
  0.6 5.9 %copy-start.1 = (f32[32,512]{1,0:T(8,128)S(1)}, f32[32,512]{1,0:T(8,128)}, u32[]{:S(2)}) copy-start(f32[32,512]{1,0:T(8,128)} %ip.7) | copy-start | bytes 196612
  0.7 5.9 %copy-start.3 = (f32[32,512]{1,0:T(8,128)S(1)}, f32[32,512]{1,0:T(8,128)}, u32[]{:S(2)}) copy-start(f32[32,512]{1,0:T(8,128)} %vw.5) | copy-start | bytes 196612
  0.7 5.9 %copy-start = (f32[2,2,3,32,512]{4,3,2,1,0:T(8,128)S(1)}, f32[2,2,3,32,512]{4,3,2,1,0:T(8,128)}, u32[]{:S(2)}) copy-start(f32[2,2,3,32,512]{4,3,2,1,0:T(8,128)} %param.5) | copy-start | bytes 2359300
  1.9 10.3 %copy-start.4 = (f32[3]{0:T(128)S(1)}, f32[3]{0:T(128)}, u32[]{:S(2)}) copy-start(f32[3]{0:T(128)} %ground.1) | copy-start | bytes 40
  1.9 11.3 %collective-permute-start = (f32[129,512]{1,0:T(8,128)S(1)}, f32[129,512]{1,0:T(8,128)S(1)}, u32[]{:S(2)}, u32[]{:S(2)}) collective-permute-start(f32[129,512]{1,0:T(8,128)S(1)} %faredges.1), channel_id=1, source_target_pairs={{32,64},{96,128},{160,192},{224,256},{288,320},{352,384},{416,448}... | collective-permute-start | bytes 792584 | tf_op jit(solution)/shard_map/ppermute | solution.py:691
  6.7 6.6 %collective-permute-start.1 = (f32[129,512]{1,0:T(8,128)S(1)}, f32[129,512]{1,0:T(8,128)S(1)}, u32[]{:S(2)}, u32[]{:S(2)}) collective-permute-start(f32[129,512]{1,0:T(8,128)S(1)} %nearedges.1), channel_id=1, source_target_pairs={{0,32},{64,96},{128,160},{192,224},{256,288},{320,352},{384,416},{... | collective-permute-start | bytes 792584 | tf_op jit(solution)/shard_map/ppermute | solution.py:693
  13.8 5.4 %collective-permute-start.2 = (f32[64,128]{1,0:T(8,128)S(1)}, f32[64,128]{1,0:T(8,128)S(1)}, u32[]{:S(2)}, u32[]{:S(2)}) collective-permute-start(f32[64,128]{1,0:T(8,128)S(1)} %get-tuple-element.34), channel_id=1, source_target_pairs={{1,2},{3,4},{5,6},{7,8},{9,10},{11,12},{13,14},{15,16},{17,18},{19... | collective-permute-start | bytes 98312 | tf_op jit(solution)/shard_map/ppermute | solution.py:720
  14.4 4.7 %collective-permute-start.3 = (f32[64,128]{1,0:T(8,128)S(1)}, f32[64,128]{1,0:T(8,128)S(1)}, u32[]{:S(2)}, u32[]{:S(2)}) collective-permute-start(f32[64,128]{1,0:T(8,128)S(1)} %get-tuple-element.35), channel_id=1, source_target_pairs={{0,1},{2,3},{4,5},{6,7},{8,9},{10,11},{12,13},{14,15},{16,17},{18,... | collective-permute-start | bytes 98312 | tf_op jit(solution)/shard_map/ppermute | solution.py:721
